TPU v7x, 8 devices: a whole 2x2x1 slice. The times are simulated.
8 devices in a mesh: rep: 2 (over y, z), dp: 4 (over x, core).
Axes of the slice: x: 2, y: 2, z: 1, core: 2. Of those that a mesh axis runs over, the one named last changes fastest.
Arguments:
- x: bfloat16 [8, 2048, 1536], P(('rep', 'dp')), parts along dimension 0
- dy: bfloat16 [8, 2048, 1536], P(('rep', 'dp')), parts along dimension 0
- w_gate: bfloat16 [2, 1536, 4224], replicated
- w_up: bfloat16 [2, 1536, 4224], replicated
- w_down: bfloat16 [2, 4224, 1536], replicated
- m_w_gate: float32 [2, 1536, 4224], P(None, 'dp')
- m_w_up: float32 [2, 1536, 4224], P(None, 'dp')
- m_w_down: float32 [2, 4224, 1536], P(None, 'dp')
- v_w_gate: float32 [2, 1536, 4224], P(None, 'dp')
- v_w_up: float32 [2, 1536, 4224], P(None, 'dp')
- v_w_down: float32 [2, 4224, 1536], P(None, 'dp')
Outputs:
- output 1: bfloat16 [4, 1536, 4224], P('rep'), parts along dimension 0
- output 2: bfloat16 [4, 1536, 4224], P('rep'), parts along dimension 0
- output 3: bfloat16 [4, 4224, 1536], P('rep'), parts along dimension 0
- output 4: float32 [4, 1536, 4224], P('rep', 'dp'), parts along dimension 0
- output 5: float32 [4, 1536, 4224], P('rep', 'dp'), parts along dimension 0
- output 6: float32 [4, 4224, 1536], P('rep', 'dp'), parts along dimension 0
- output 7: float32 [4, 1536, 4224], P('rep', 'dp'), parts along dimension 0
- output 8: float32 [4, 1536, 4224], P('rep', 'dp'), parts along dimension 0
- output 9: float32 [4, 4224, 1536], P('rep', 'dp'), parts along dimension 0
There are 2 independent parts. A program takes and returns all parts, laid end to end along the dimension named above; an argument that names none is the same for every part.
All inputs are finite; a program needn't handle non-finite values.
Results may differ from a plain program's by a relative error of at most 0.02.
Values are sent between devices in bfloat16 or wider.
A program may use at most 2 GiB of HBM per device.

v0:
```python
import jax
import jax.numpy as jnp
from jax import lax

NAMES = ("w_gate", "w_up", "w_down")


def matmul(a, w):
    return jnp.dot(a, w, preferred_element_type=jnp.float32).astype(jnp.bfloat16)


def normed(h):
    wide = h.astype(jnp.float32)
    scale = lax.rsqrt(jnp.mean(wide**2, -1, keepdims=True) + 1e-6)
    return (wide * scale).astype(jnp.bfloat16)


def layer(h, w):
    a = normed(h)
    gate = jnp.dot(a, w["w_gate"], preferred_element_type=jnp.float32)
    up = jnp.dot(a, w["w_up"], preferred_element_type=jnp.float32)
    return h + matmul((jax.nn.silu(gate) * up).astype(jnp.bfloat16), w["w_down"])


def adamw(w, m, v, g):
    m = 0.9 * m + 0.1 * g
    v = 0.95 * v + 0.05 * g * g
    step = m * lax.rsqrt(v + 1e-8) + 0.1 * w
    return (w - 0.02 * step).astype(jnp.bfloat16), m, v


def stack(weights, h):
    for number in range(weights["w_gate"].shape[0]):
        h = layer(h, {name: w[number] for name, w in weights.items()})
    return h


def solution(mesh):
    groups = mesh.shape["rep"]

    def step(x, dy, *arrays):
        weights, m, v = (arrays[i : i + 3] for i in (0, 3, 6))
        x, dy = (t.reshape(groups, -1, *t.shape[1:]) for t in (x, dy))

        def of_a_group(x, dy):
            _, back = jax.vjp(lambda w: stack(w, x), dict(zip(NAMES, weights, strict=True)))
            by_weights = back(dy)[0]
            gradients = [by_weights[name].astype(jnp.float32) for name in NAMES]
            new = [adamw(w.astype(jnp.float32), m, v, g) for w, m, v, g in zip(weights, m, v, gradients, strict=True)]
            return tuple(one[which] for which in range(3) for one in new)

        return tuple(t.reshape(-1, *t.shape[2:]) for t in jax.vmap(of_a_group)(x, dy))

    return step
```

profile of v0, /device:TPU:0, one launch (start us, length us, event | category | flops | bytes accessed | tf_op | source)
XLA Modules:
  0.0 1947.9 jit_solution(3486741206391482366)
XLA Ops:
  7.2 0.0 reduce-scatter.27.cloned.1.call-start
  7.2 4.1 fusion.82
  11.3 8.8 copy
  20.1 37.6 %fusion.77 = f32[2048,4224]{1,0:T(8,128)} fusion(bf16[2,1536,4224]{2,1,0:T(8,128)(2,1)} %param, bf16[1,2048,1536]{2,1,0:T(8,128)(2,1)} %param.2, f32[2048]{0:T(1024)S(1)} %add_rsqrt_fusion), kind=kOutput, calls=%fused_computation.103 | convolution fusion | flops 26584547328 | bytes 53878784 | tf_op jit(solution)/vmap(jvp())/dot_general | solution.py:20
  57.7 34.4 %fusion.75 = f32[2048,4224]{1,0:T(8,128)} fusion(bf16[2,1536,4224]{2,1,0:T(8,128)(2,1)} %param.3, bf16[1,2048,1536]{2,1,0:T(8,128)(2,1)S(1)} %bitcast.355, f32[2048]{0:T(1024)S(1)} %add_rsqrt_fusion), kind=kOutput, calls=%fused_computation.101 | convolution fusion | flops 26584547328 | bytes 53878784 | tf_op jit(solution)/vmap(jvp())/dot_general | solution.py:21
  92.1 28.6 %fusion.35 = bf16[2048,4224]{1,0:T(8,128)(2,1)} fusion(f32[2048,4224]{1,0:T(8,128)} %fusion.75, f32[2048,4224]{1,0:T(8,128)} %fusion.77), kind=kLoop, calls=%fused_computation.50 | loop fusion | flops 51904512 | bytes 86507520
  120.7 48.5 %fusion.86 = (f32[2048]{0:T(1024)S(1)}, bf16[1,1,2048,1536]{2,3,1,0:T(8,128)(2,1)}) fusion(bf16[2048,4224]{1,0:T(8,128)(2,1)} %fusion.35, bf16[2,4224,1536]{2,1,0:T(8,128)(2,1)} %param.4, bf16[1,2048,1536]{1,2,0:T(8,128)(2,1)} %copy), kind=kOutput, calls=%fused_computation.112 | convolution fusion | flops 26590836736 | bytes 42868736 | tf_op jit(solution)/vmap(jvp())/dot_general | solution.py:9
  169.2 0.6 copy-done.2
  169.8 37.6 %fusion.64 = f32[2048,4224]{1,0:T(8,128)} fusion(bf16[2,1536,4224]{2,1,0:T(8,128)(2,1)} %param, bf16[1,1,2048,1536]{2,3,1,0:T(8,128)(2,1)} %get-tuple-element.10, f32[2048]{0:T(1024)S(1)} %bitcast.359), kind=kOutput, calls=%fused_computation.90 | convolution fusion | flops 26584547328 | bytes 53878784 | tf_op jit(solution)/vmap(jvp())/dot_general | solution.py:20
  207.4 35.5 %fusion.68 = f32[2048,4224]{1,0:T(8,128)} fusion(bf16[2,1536,4224]{2,1,0:T(8,128)(2,1)} %param.3, bf16[1,1,2048,1536]{2,3,1,0:T(8,128)(2,1)S(1)} %copy-done, f32[2048]{0:T(1024)S(1)} %bitcast.360), kind=kOutput, calls=%fused_computation.94 | convolution fusion | flops 26584547328 | bytes 53878784 | tf_op jit(solution)/vmap(jvp())/dot_general | solution.py:21
  242.9 41.0 %convolution_bitcast_fusion.1 = f32[1,4224,1536]{2,1,0:T(8,128)} fusion(f32[2048,4224]{1,0:T(8,128)} %fusion.68, f32[2048,4224]{1,0:T(8,128)} %fusion.64, bf16[1,2048,1536]{2,1,0:T(8,128)(2,1)} %param.5), kind=kOutput, calls=%fused_computation.41 | convolution fusion | flops 26627014656 | bytes 101449728 | tf_op jit(solution)/vmap(transpose(jvp()))/dot_general | solution.py:9
  283.9 0.0 reduce-scatter.27.cloned.1.call-update
  283.9 0.0 reduce-scatter.29.cloned.1.call-start
  284.0 9.1 copy.1
  293.0 39.8 %convolution_convert_fusion.1 = bf16[2048,4224]{1,0:T(8,128)(2,1)} fusion(bf16[2,4224,1536]{2,1,0:T(8,128)(2,1)} %param.4, bf16[1,2048,1536]{2,1,0:T(8,128)(2,1)} %param.5), kind=kOutput, calls=%fused_computation.49 | convolution fusion | flops 26583760896 | bytes 36569088 | tf_op jit(solution)/vmap(transpose(jvp()))/dot_general | solution.py:9
  332.8 35.8 %fusion.6 = bf16[2048,4224]{1,0:T(8,128)(2,1)} fusion(f32[2048,4224]{1,0:T(8,128)} %fusion.64, f32[2048,4224]{1,0:T(8,128)} %fusion.68, bf16[2048,4224]{1,0:T(8,128)(2,1)} %convolution_convert_fusion.1), kind=kLoop, calls=%fused_computation.11 | loop fusion | flops 103809024 | bytes 103809024
  368.6 38.2 %fusion.101 = bf16[2048,1536]{0,1:T(8,128)(2,1)} fusion(bf16[2,1536,4224]{2,1,0:T(8,128)(2,1)} %param.3, bf16[2048,4224]{1,0:T(8,128)(2,1)} %convolution_convert_fusion.1, f32[2048,4224]{1,0:T(8,128)} %fusion.64), kind=kOutput, calls=%fused_computation.124 | convolution fusion | flops 26630160384 | bytes 71172096 | tf_op jit(solution)/vmap(transpose(jvp()))/dot_general | solution.py:21
  406.8 38.9 %fusion.88 = (f32[2048]{0:T(1024)S(1)}, bf16[2048,1536]{0,1:T(8,128)(2,1)}) fusion(bf16[1,1,2048,1536]{2,3,1,0:T(8,128)(2,1)} %get-tuple-element.10, bf16[2048,1536]{0,1:T(8,128)(2,1)} %fusion.101, bf16[2048,4224]{1,0:T(8,128)(2,1)} %fusion.6, bf16[2,1536,4224]{2,1,0:T(8,128)(2,1)} %param), kind=kOutput, calls=%fused_computation.114 | convolution fusion | flops 26590836736 | bytes 49160192 | tf_op jit(solution)/vmap(transpose(jvp()))/dot_general | solution.py:20
  445.8 8.7 fusion.118
  454.5 2.7 copy-done.1
  457.2 34.2 %convolution_bitcast_fusion = f32[1,4224,1536]{2,1,0:T(8,128)} fusion(bf16[2048,4224]{1,0:T(8,128)(2,1)} %fusion.35, bf16[2048,1536]{0,1:T(8,128)(2,1)S(1)} %fusion.118), kind=kOutput, calls=%fused_computation.40 | convolution fusion | flops 26575110144 | bytes 49545216 | tf_op jit(solution)/vmap(transpose(jvp()))/dot_general | solution.py:9
  491.3 0.0 reduce-scatter.29.cloned.1.call-update
  491.4 0.0 reduce-scatter.19.cloned.1.call-start
  491.4 36.3 %convolution_bitcast_fusion.2 = f32[1,1536,4224]{2,1,0:T(8,128)} fusion(bf16[2048,4224]{1,0:T(8,128)(2,1)} %fusion.6, bf16[1,1,2048,1536]{2,3,1,0:T(8,128)(2,1)} %get-tuple-element.10, f32[2048]{0:T(1024)S(1)} %bitcast.362), kind=kOutput, calls=%fused_computation.44 | convolution fusion | flops 26584547328 | bytes 49553408 | tf_op jit(solution)/vmap(transpose(jvp()))/dot_general | solution.py:20
  527.7 0.0 reduce-scatter.19.cloned.1.call-update
  527.7 0.0 reduce-scatter.21.cloned.1.call-start
  527.8 36.8 %convolution_convert_fusion = bf16[2048,4224]{1,0:T(8,128)(2,1)} fusion(bf16[2048,1536]{0,1:T(8,128)(2,1)} %copy-done.1, bf16[2,4224,1536]{2,1,0:T(8,128)(2,1)} %param.4), kind=kOutput, calls=%fused_computation.48 | convolution fusion | flops 26583760896 | bytes 36569088 | tf_op jit(solution)/vmap(transpose(jvp()))/dot_general | solution.py:9
  564.6 50.7 %fusion.26 = f32[1,1536,4224]{2,1,0:T(8,128)} fusion(f32[2048,4224]{1,0:T(8,128)} %fusion.77, f32[2048,4224]{1,0:T(8,128)} %fusion.75, bf16[2048,4224]{1,0:T(8,128)(2,1)} %convolution_convert_fusion, bf16[1,2048,1536]{1,2,0:T(8,128)(2,1)} %copy, f32[2048]{0:T(1024)S(1)} %copy-done.8), kind=kOutput, calls=%fused_computation.39 | convolution fusion | flops 26679705600 | bytes 118759424 | tf_op jit(solution)/vmap(transpose(jvp()))/dot_general | solution.py:20
  615.3 0.0 reduce-scatter.21.cloned.1.call-update
  615.3 0.0 reduce-scatter.23.cloned.1.call-start
  615.4 0.6 copy-done.6
  616.0 42.3 %fusion.29 = f32[1,1536,4224]{2,1,0:T(8,128)} fusion(bf16[2048,4224]{1,0:T(8,128)(2,1)} %convolution_convert_fusion.1, f32[2048,4224]{1,0:T(8,128)} %fusion.64, bf16[1,1,2048,1536]{2,3,1,0:T(8,128)(2,1)} %get-tuple-element.10, f32[2048]{0:T(1024)S(1)} %bitcast.363), kind=kOutput, calls=%fused_computation.42 | convolution fusion | flops 26636451840 | bytes 84156416 | tf_op jit(solution)/vmap(transpose(jvp()))/dot_general | solution.py:21
  658.3 0.0 reduce-scatter.25.cloned.1.call-start
  658.4 43.8 %fusion.32 = f32[1,1536,4224]{2,1,0:T(8,128)} fusion(bf16[2048,4224]{1,0:T(8,128)(2,1)} %convolution_convert_fusion, f32[2048,4224]{1,0:T(8,128)} %fusion.77, bf16[1,2048,1536]{1,2,0:T(8,128)(2,1)} %copy, f32[2048]{0:T(1024)S(1)} %copy-done.8), kind=kOutput, calls=%fused_computation.43 | convolution fusion | flops 26636451840 | bytes 84156416 | tf_op jit(solution)/vmap(transpose(jvp()))/dot_general | solution.py:21
  702.2 0.0 reduce-scatter.25.cloned.1.call-update
  702.2 0.0 all-gather.14.cloned.1.call-start
  702.2 0.6 copy-done.9
  702.8 0.6 dynamic-slice
  704.1 0.0 reduce-scatter.27.cloned.1.call-done
  704.1 4.5 convert_bitcast_fusion.4
  708.6 0.0 reduce-scatter.29.cloned.1.call-done
  708.6 3.6 convert_bitcast_fusion.3
  712.2 22.2 %fusion.109 = (f32[2,1056,1536]{2,1,0:T(8,128)}, bf16[1,2,1056,1536]{3,2,1,0:T(8,128)(2,1)}, f32[2,1056,1536]{2,1,0:T(8,128)}) fusion(f32[2,1056,1536]{2,1,0:T(8,128)} %param.10, bf16[1,1,1056,1536]{3,2,1,0:T(8,128)(2,1)S(1)} %convert_bitcast_fusion.3, bf16[1,1,1056,1536]{3,2,1,0:T(8,128)(2,1)S(1)} %convert_bitcast_fusion.4, f32[2,1056,1536]{2,1,0:T(8,128)} %param.9, ...), kind=kLoop, calls=%fused_computation.128 | loop fusion | flops 61636608 | bytes 71368704 | tf_op jit(solution)/reshape | solution.py:52
  734.4 0.0 all-gather.14.cloned.1.call-update
  734.4 0.0 all-gather.10.cloned.1.call-start
  734.5 125.1 %reduce-scatter.19.cloned.1.call-done = f32[1,384,4224]{2,1,0:T(8,128)} async-done(((f32[1,1536,4224]{2,1,0:T(8,128)}), f32[1,384,4224]{2,1,0:T(8,128)}) %reduce-scatter.19.cloned.1.call-update) | async-done | bytes 6488080
  859.6 3.2 convert_bitcast_fusion.8
  862.8 181.5 %reduce-scatter.21.cloned.1.call-done = f32[1,384,4224]{2,1,0:T(8,128)} async-done(((f32[1,1536,4224]{2,1,0:T(8,128)}), f32[1,384,4224]{2,1,0:T(8,128)}) %reduce-scatter.21.cloned.1.call-update) | async-done | bytes 6488080
  1044.3 3.2 convert_bitcast_fusion.7
  1047.4 29.5 %fusion.111 = (f32[2,384,4224]{2,1,0:T(8,128)}, bf16[1,2,384,4224]{3,2,1,0:T(8,128)(2,1)}, f32[2,384,4224]{2,1,0:T(8,128)}) fusion(f32[2,384,4224]{2,1,0:T(8,128)} %param.6, bf16[1,1,384,4224]{3,2,1,0:T(8,128)(2,1)S(1)} %convert_bitcast_fusion.7, bf16[1,1,384,4224]{3,2,1,0:T(8,128)(2,1)S(1)} %convert_bitcast_fusion.8, f32[2,384,4224]{2,1,0:T(8,128)} %param.1, ...), kind=kLoop, calls=%fused_computation.130 | loop fusion | flops 61636608 | bytes 71368704 | tf_op jit(solution)/reshape | solution.py:52
  1077.0 0.0 all-gather.10.cloned.1.call-update
  1077.0 0.0 all-gather.12.cloned.1.call-start
  1077.1 151.3 %reduce-scatter.23.cloned.1.call-done = f32[1,384,4224]{2,1,0:T(8,128)} async-done(((f32[1,1536,4224]{2,1,0:T(8,128)}), f32[1,384,4224]{2,1,0:T(8,128)}) %reduce-scatter.23.cloned.1.call-update) | async-done | bytes 6488080
  1228.3 3.2 convert_bitcast_fusion.6
  1231.5 181.5 %reduce-scatter.25.cloned.1.call-done = f32[1,384,4224]{2,1,0:T(8,128)} async-done(((f32[1,1536,4224]{2,1,0:T(8,128)}), f32[1,384,4224]{2,1,0:T(8,128)}) %reduce-scatter.25.cloned.1.call-update) | async-done | bytes 6488080
  1413.0 3.2 convert_bitcast_fusion.5
  1416.1 27.8 %fusion.110 = (f32[2,384,4224]{2,1,0:T(8,128)}, bf16[1,2,384,4224]{3,2,1,0:T(8,128)(2,1)}, f32[2,384,4224]{2,1,0:T(8,128)}) fusion(f32[2,384,4224]{2,1,0:T(8,128)} %param.8, bf16[1,1,384,4224]{3,2,1,0:T(8,128)(2,1)S(1)} %convert_bitcast_fusion.5, bf16[1,1,384,4224]{3,2,1,0:T(8,128)(2,1)S(1)} %convert_bitcast_fusion.6, f32[2,384,4224]{2,1,0:T(8,128)} %param.7, ...), kind=kLoop, calls=%fused_computation.129 | loop fusion | flops 61636608 | bytes 71368704 | tf_op jit(solution)/reshape | solution.py:52
  1443.9 0.0 all-gather.12.cloned.1.call-update
  1443.9 126.1 %all-gather.14.cloned.1.call-done = bf16[1,2,4224,1536]{3,2,1,0:T(8,128)(2,1)} async-done(((bf16[1,2,1056,1536]{3,2,1,0:T(8,128)(2,1)}), bf16[1,2,4224,1536]{3,2,1,0:T(8,128)(2,1)}) %all-gather.14.cloned.1.call-update) | async-done | bytes 25952272 | tf_op jit(solution)/reshape | solution.py:52
  1570.0 157.6 %all-gather.10.cloned.1.call-done = bf16[1,2,1536,4224]{3,2,1,0:T(8,128)(2,1)} async-done(((bf16[1,2,384,4224]{3,2,1,0:T(8,128)(2,1)}), bf16[1,2,1536,4224]{3,2,1,0:T(8,128)(2,1)}) %all-gather.10.cloned.1.call-update) | async-done | bytes 25952272 | tf_op jit(solution)/reshape | solution.py:52
  1727.6 157.6 %all-gather.12.cloned.1.call-done = bf16[1,2,1536,4224]{3,2,1,0:T(8,128)(2,1)} async-done(((bf16[1,2,384,4224]{3,2,1,0:T(8,128)(2,1)}), bf16[1,2,1536,4224]{3,2,1,0:T(8,128)(2,1)}) %all-gather.12.cloned.1.call-update) | async-done | bytes 25952272 | tf_op jit(solution)/reshape | solution.py:52
  1885.3 23.8 %copy.5 = bf16[2,1536,4224]{2,1,0:T(8,128)(2,1)} copy(bf16[2,1536,4224]{2,1,0:T(8,128)(2,1)} %bitcast.352) | data formatting | bytes 51904512
  1909.1 22.6 %copy.6 = bf16[2,1536,4224]{2,1,0:T(8,128)(2,1)} copy(bf16[2,1536,4224]{2,1,0:T(8,128)(2,1)} %bitcast.353) | data formatting | bytes 51904512
  1931.7 9.2 copy.7
  (41 shorter events, 0.1 us)
Async XLA Ops:
  7.2 696.9 %reduce-scatter.27.cloned.1.call-start = ((), (), s32[]{:S(2)}) async-start(), calls=%async_computation.13 | async-start | bytes 32440320
  11.3 46.4 %slice-start.7 = ((s8[6291456]{0:T(1024)(128)(4,1)}), s8[2097152]{0:T(1024)(128)(4,1)S(1)}, s32[]{:S(2)}) async-start(s8[6291456]{0:T(1024)(128)(4,1)} %bitcast.354), calls=%async_computation.22 | async-start | bytes 4194304
  20.1 37.6 %copy-start.7 = (f32[2048]{0:T(1024)}, f32[2048]{0:T(1024)S(1)}, u32[]{:S(2)}) copy-start(f32[2048]{0:T(1024)S(1)} %add_rsqrt_fusion) | copy-start | bytes 24580
  20.1 37.6 %slice-start.8 = ((s8[6291456]{0:T(1024)(128)(4,1)}), s8[4194304]{0:T(1024)(128)(4,1)S(1)}, s32[]{:S(2)}) async-start(s8[6291456]{0:T(1024)(128)(4,1)} %bitcast.354), calls=%async_computation.23 | async-start | bytes 8388608
  169.2 0.6 copy-start.2
  169.2 38.2 %copy-start.4 = (f32[1,1,2048]{2,1,0:T(1,128)}, f32[1,1,2048]{2,1,0:T(1,128)S(1)}, u32[]{:S(2)}) copy-start(f32[1,1,2048]{2,1,0:T(1,128)S(1)} %rsqrt.31) | copy-start | bytes 24580
  169.8 37.6 %copy-start = (bf16[1,1,2048,1536]{2,3,1,0:T(8,128)(2,1)S(1)}, bf16[1,1,2048,1536]{2,3,1,0:T(8,128)(2,1)}, u32[]{:S(2)}) copy-start(bf16[1,1,2048,1536]{2,3,1,0:T(8,128)(2,1)} %get-tuple-element.10) | copy-start | bytes 18874372
  283.9 424.7 %reduce-scatter.29.cloned.1.call-start = ((), (), s32[]{:S(2)}) async-start(), calls=%async_computation.14 | async-start | bytes 32440320
  406.8 38.9 %copy-start.3 = (f32[2048]{0:T(1024)S(1)}, f32[2048]{0:T(1024)}, u32[]{:S(2)}) copy-start(f32[2048]{0:T(1024)} %copy-done.2) | copy-start | bytes 24580
  406.8 38.9 %copy-start.5 = (f32[1,1,2048]{2,1,0:T(1,128)S(1)}, f32[1,1,2048]{2,1,0:T(1,128)}, u32[]{:S(2)}) copy-start(f32[1,1,2048]{2,1,0:T(1,128)} %copy-done.4) | copy-start | bytes 24580
  454.5 2.7 copy-start.1
  491.4 368.3 %reduce-scatter.19.cloned.1.call-start = ((), (), s32[]{:S(2)}) async-start(), calls=%async_computation.9 | async-start | bytes 32440320
  527.7 36.8 %copy-start.8 = (f32[2048]{0:T(1024)S(1)}, f32[2048]{0:T(1024)}, u32[]{:S(2)}) copy-start(f32[2048]{0:T(1024)} %copy-done.7) | copy-start | bytes 24580
  527.7 516.5 %reduce-scatter.21.cloned.1.call-start = ((), (), s32[]{:S(2)}) async-start(), calls=%async_computation.10 | async-start | bytes 32440320
  615.3 0.7 copy-start.6
  615.3 613.0 %reduce-scatter.23.cloned.1.call-start = ((), (), s32[]{:S(2)}) async-start(), calls=%async_computation.11 | async-start | bytes 32440320
  658.3 754.6 %reduce-scatter.25.cloned.1.call-start = ((), (), s32[]{:S(2)}) async-start(), calls=%async_computation.12 | async-start | bytes 32440320
  702.2 0.7 copy-start.9
  702.2 867.8 %all-gather.14.cloned.1.call-start = ((), (), s32[]{:S(2)}) async-start(), calls=%async_computation.8 | async-start | bytes 32440320 | tf_op jit(solution)/reshape | solution.py:52
  734.4 993.2 %all-gather.10.cloned.1.call-start = ((), (), s32[]{:S(2)}) async-start(), calls=%async_computation.6 | async-start | bytes 32440320 | tf_op jit(solution)/reshape | solution.py:52
  1077.0 808.2 %all-gather.12.cloned.1.call-start = ((), (), s32[]{:S(2)}) async-start(), calls=%async_computation.7 | async-start | bytes 32440320 | tf_op jit(solution)/reshape | solution.py:52
  1885.2 46.4 %slice-start = ((s8[25952256]{0:T(1024)(128)(4,1)}), s8[4194304]{0:T(1024)(128)(4,1)S(1)}, s32[]{:S(2)}) async-start(s8[25952256]{0:T(1024)(128)(4,1)} %bitcast.349), calls=%async_computation.15 | async-start | bytes 8388608
  1885.3 46.4 %slice-start.1 = ((s8[25952256]{0:T(1024)(128)(4,1)}), s8[4194304]{0:T(1024)(128)(4,1)S(1)}, s32[]{:S(2)}) async-start(s8[25952256]{0:T(1024)(128)(4,1)} %bitcast.349), calls=%async_computation.16 | async-start | bytes 8388608
  1885.3 46.4 %slice-start.2 = ((s8[25952256]{0:T(1024)(128)(4,1)}), s8[4194304]{0:T(1024)(128)(4,1)S(1)}, s32[]{:S(2)}) async-start(s8[25952256]{0:T(1024)(128)(4,1)} %bitcast.349), calls=%async_computation.17 | async-start | bytes 8388608
  1885.3 46.4 %slice-start.3 = ((s8[25952256]{0:T(1024)(128)(4,1)}), s8[4194304]{0:T(1024)(128)(4,1)S(1)}, s32[]{:S(2)}) async-start(s8[25952256]{0:T(1024)(128)(4,1)} %bitcast.349), calls=%async_computation.18 | async-start | bytes 8388608
  1909.1 22.6 %slice-start.4 = ((s8[25952256]{0:T(1024)(128)(4,1)}), s8[4194304]{0:T(1024)(128)(4,1)S(1)}, s32[]{:S(2)}) async-start(s8[25952256]{0:T(1024)(128)(4,1)} %bitcast.349), calls=%async_computation.19 | async-start | bytes 8388608
  1909.1 22.6 %slice-start.5 = ((s8[25952256]{0:T(1024)(128)(4,1)}), s8[4194304]{0:T(1024)(128)(4,1)S(1)}, s32[]{:S(2)}) async-start(s8[25952256]{0:T(1024)(128)(4,1)} %bitcast.349), calls=%async_computation.20 | async-start | bytes 8388608
  1909.1 22.6 %slice-start.6 = ((s8[25952256]{0:T(1024)(128)(4,1)}), s8[786432]{0:T(1024)(128)(4,1)S(1)}, s32[]{:S(2)}) async-start(s8[25952256]{0:T(1024)(128)(4,1)} %bitcast.349), calls=%async_computation.21 | async-start | bytes 1572864
Sparse Core Ops, SparseCore 0:
  284.0 184.3 reduce-scatter.26
  491.5 183.3 reduce-scatter.28
  678.0 181.5 reduce-scatter.18
  862.7 181.5 reduce-scatter.20
  1046.7 181.5 reduce-scatter.22
  1231.3 181.5 reduce-scatter.24
  1414.5 155.4 all-gather.13
  1572.1 155.4 all-gather.9
  1729.7 155.4 all-gather.11
where the time goes:
time: 1960 us; the launch traced here: 1950 us
  waiting for transfers between devices  1080 us (55%)
  matrix products  595 us (30%)
  other arithmetic  178 us (9%)
  local copies, waits for them, and re-layouts  78.5 us (4%)
    unnamed x15, waiting for transfers between devices  640 us
    reshape x3, waiting for transfers between devices, step(): t.reshape(-1, *t.shape[2:])  441 us
    dot_general x5, matrix products, layer(): gate = jnp.dot(a, w['w_gate'], preferred_element_type=jnp.float32)  201 us
    dot_general x5, matrix products, matmul(): jnp.dot(a, w, preferred_element_type=jnp.float32).astype(jnp.bfloat16)  200 us
    dot_general x5, matrix products, layer(): up = jnp.dot(a, w['w_up'], preferred_element_type=jnp.float32)  194 us
    reshape x3, other arithmetic, step(): t.reshape(-1, *t.shape[2:])  79.6 us
    unnamed x43, local copies, waits for them, and re-layouts  77.9 us
    unnamed x5, other arithmetic  73.1 us
  transfers between devices with their start and end apart: 9, of which 7 were waited for; matrix products, arithmetic and copies ran while one was open for 26% of the time, Pallas kernels for 0%

commit v1 on v0

v1 whole, which is shorter than its diff:
```python
import functools

import jax
import jax.numpy as jnp
from jax import lax
from jax.experimental import pallas as pl
from jax.experimental.pallas import tpu as pltpu
from jax.sharding import PartitionSpec as P


F32, BF16 = jnp.float32, jnp.bfloat16
VMEM_LIMIT = 60 * 1024 * 1024
BN = 256
CROSS = [(i, i ^ 2) for i in range(4)]
INCHIP = [(i, i ^ 1) for i in range(4)]


def params(axes):
    return pltpu.CompilerParams(dimension_semantics=("arbitrary",) * axes, vmem_limit_bytes=VMEM_LIMIT)


def cost(matmuls, elements, moved):
    return pl.CostEstimate(flops=2 * matmuls * elements, bytes_accessed=moved, transcendentals=0)


def dot(a, b, contract):
    return lax.dot_general(a, b, (contract, ((), ())), preferred_element_type=F32)


def normed(h):
    wide = h.astype(F32)
    scale = lax.rsqrt(jnp.mean(wide**2, -1, keepdims=True) + 1e-6)
    return (wide * scale).astype(BF16)


def silu_parts(gate):
    s = jax.nn.sigmoid(gate)
    return gate * s, s + gate * s * (1 - s)


def once(shape, index):
    return pl.BlockSpec(shape, index, pipeline_mode=pl.Buffered(1))


def norm_into(h, a, rows=256):
    def chunk(i, _):
        at = pl.ds(pl.multiple_of(i * rows, rows), rows)
        a[at, :] = normed(h[at, :])

    lax.fori_loop(0, h.shape[0] // rows, chunk, None)


def gates(x, w_gate, w_up, layer, bn=BN):
    t, d = x.shape
    f = w_gate.shape[2]
    n = pl.cdiv(f, bn)

    def body(x, wg, wu, a, gate, up, act):
        @pl.when(pl.program_id(0) == 0)
        def _():
            norm_into(x, a)

        rows = a[...]
        g = dot(rows, wg[...], ((1,), (0,)))
        u = dot(rows, wu[...], ((1,), (0,)))
        gate[...] = g
        up[...] = u
        act[...] = (g * jax.nn.sigmoid(g) * u).astype(BF16)

    return pl.pallas_call(
        body,
        grid=(n,),
        in_specs=[once((t, d), lambda j: (0, 0))] + [pl.BlockSpec((None, d, bn), lambda j: (layer, 0, j))] * 2,
        out_specs=[pl.BlockSpec((t, d), lambda j: (0, 0))]
        + [pl.BlockSpec((None, t, bn), lambda j: (j, 0, 0))] * 2
        + [pl.BlockSpec((t, bn), lambda j: (0, j))],
        out_shape=[jax.ShapeDtypeStruct((t, d), BF16)]
        + [jax.ShapeDtypeStruct((n, t, bn), F32)] * 2
        + [jax.ShapeDtypeStruct((t, f), BF16)],
        compiler_params=params(1),
        cost_estimate=cost(2, t * d * f, 2 * (2 * d * f) + 10 * t * f),
        name="gates",
    )(x, w_gate, w_up)


def down(act, w_down, h, layer, bm=1024, bn=512):
    t, f = act.shape
    d = w_down.shape[2]

    def body(act, w, h, out):
        out[...] = h[...] + dot(act[...], w[...], ((1,), (0,))).astype(BF16)

    return pl.pallas_call(
        body,
        grid=(d // bn, t // bm),
        in_specs=[
            pl.BlockSpec((bm, f), lambda j, i: (i, 0)),
            pl.BlockSpec((None, f, bn), lambda j, i: (layer, 0, j)),
            pl.BlockSpec((bm, bn), lambda j, i: (i, j)),
        ],
        out_specs=pl.BlockSpec((bm, bn), lambda j, i: (i, j)),
        out_shape=jax.ShapeDtypeStruct((t, d), BF16),
        compiler_params=params(2),
        cost_estimate=cost(1, t * d * f, 2 * d * f + 6 * t * f),
        name="down",
    )(act, w_down, h)


def last_layer(h, dy, w_gate, w_up, w_down, layer, bn=BN):
    t, d = h.shape
    f = w_gate.shape[2]

    def body(h, dy, wg, wu, wd, a, act, d_gate, d_up):
        @pl.when(pl.program_id(0) == 0)
        def _():
            norm_into(h, a)

        g = dot(a[...], wg[...], ((1,), (0,)))
        u = dot(a[...], wu[...], ((1,), (0,)))
        da = dot(dy[...], wd[...], ((1,), (1,))).astype(BF16).astype(F32)
        silu, slope = silu_parts(g)
        act[...] = (silu * u).astype(BF16)
        d_gate[...] = (da * u * slope).astype(BF16)
        d_up[...] = (da * silu).astype(BF16)

    return pl.pallas_call(
        body,
        grid=(pl.cdiv(f, bn),),
        in_specs=[once((t, d), lambda j: (0, 0))] * 2
        + [pl.BlockSpec((None, d, bn), lambda j: (layer, 0, j))] * 2
        + [pl.BlockSpec((None, bn, d), lambda j: (layer, j, 0))],
        out_specs=[pl.BlockSpec((t, d), lambda j: (0, 0))] + [pl.BlockSpec((t, bn), lambda j: (0, j))] * 3,
        out_shape=[jax.ShapeDtypeStruct((t, d), BF16)] + [jax.ShapeDtypeStruct((t, f), BF16)] * 3,
        compiler_params=params(1),
        cost_estimate=cost(3, t * d * f, 6 * d * f + 6 * t * f),
        name="last_layer",
    )(h, dy, w_gate, w_up, w_down)


def into_layer(d_gate, d_up, w_gate, w_up, h, dy, layer, bm=256):
    t, f = d_gate.shape
    d = w_gate.shape[1]

    def body(dg, du, wg, wu, h, dy, out):
        by_gate = dot(dg[...], wg[...], ((1,), (1,))).astype(BF16)
        by_up = dot(du[...], wu[...], ((1,), (1,))).astype(BF16)
        by_a = (by_gate.astype(F32) + by_up.astype(F32)).astype(BF16).astype(F32)
        wide = h[...].astype(F32)
        square = jnp.mean(wide**2, -1, keepdims=True) + 1e-6
        scale = lax.rsqrt(square)
        by_square = jnp.sum(by_a * wide, -1, keepdims=True) * (-0.5 * scale / square)
        by_h = (by_a * scale + by_square / d * 2 * wide).astype(BF16)
        out[...] = (dy[...].astype(F32) + by_h.astype(F32)).astype(BF16)

    return pl.pallas_call(
        body,
        grid=(t // bm,),
        in_specs=[pl.BlockSpec((bm, f), lambda i: (i, 0))] * 2
        + [once((None, d, f), lambda i: (layer, 0, 0))] * 2
        + [pl.BlockSpec((bm, d), lambda i: (i, 0))] * 2,
        out_specs=pl.BlockSpec((bm, d), lambda i: (i, 0)),
        out_shape=jax.ShapeDtypeStruct((t, d), BF16),
        compiler_params=params(1),
        cost_estimate=cost(2, t * d * f, 4 * d * f + 4 * t * f),
        name="into_layer",
    )(d_gate, d_up, w_gate, w_up, h, dy)


def to_gates(dh, w_down, gate, up, layer, first, columns, bn=BN):
    t, d = dh.shape

    def body(dh, wd, gate, up, d_gate, d_up):
        da = dot(dh[...], wd[...], ((1,), (1,))).astype(BF16).astype(F32)
        silu, slope = silu_parts(gate[...])
        d_gate[...] = (da * up[...] * slope).astype(BF16)
        d_up[...] = (da * silu).astype(BF16)

    return pl.pallas_call(
        body,
        grid=(pl.cdiv(columns, bn),),
        in_specs=[once((t, d), lambda j: (0, 0)), pl.BlockSpec((None, bn, d), lambda j: (layer, j + first // bn, 0))]
        + [pl.BlockSpec((None, t, bn), lambda j: (j + first // bn, 0, 0))] * 2,
        out_specs=[pl.BlockSpec((t, bn), lambda j: (0, j))] * 2,
        out_shape=[jax.ShapeDtypeStruct((t, columns), BF16)] * 2,
        compiler_params=params(1),
        cost_estimate=cost(1, t * d * columns, 2 * d * columns + 12 * t * columns),
        name="to_gates",
    )(dh, w_down, gate, up)


def weight_gradient(pairs, bm, bn, first=None, rows=None, piece=None):
    k = pairs[0][0].shape[0]
    n = pairs[0][1].shape[1] if piece is None else bn
    skip = 0 if piece is None else piece
    m = pairs[0][0].shape[1] if rows is None else rows
    start = jnp.zeros((1,), jnp.int32) if first is None else (first * (rows // bm)).reshape(1).astype(jnp.int32)
    count = len(pairs)

    def body(start, *refs):
        out = refs[-1]
        total = dot(refs[0][...], refs[1][...], ((0,), (0,)))
        for i in range(1, count):
            total += dot(refs[2 * i][...], refs[2 * i + 1][...], ((0,), (0,)))
        out[...] = total.astype(BF16)

    return pl.pallas_call(
        body,
        grid_spec=pltpu.PrefetchScalarGridSpec(
            num_scalar_prefetch=1,
            grid=(pl.cdiv(n, bn), m // bm),
            in_specs=[
                pl.BlockSpec((k, bm), lambda j, i, s: (0, i + s[0])),
                pl.BlockSpec((k, bn), lambda j, i, s: (0, j + skip)),
            ]
            * count,
            out_specs=pl.BlockSpec((bm, bn), lambda j, i, s: (i, j)),
        ),
        out_shape=jax.ShapeDtypeStruct((m, n), BF16),
        compiler_params=params(2),
        cost_estimate=cost(count, k * m * n, 2 * count * k * (m + n) + 2 * m * n),
        name="weight_gradient",
    )(start, *(t for pair in pairs for t in pair))


def adamw(terms, w, m, v, layer, place, so_far, steps=6):
    _, rows, columns = m.shape
    bm = rows // steps
    arrays, specs, counts = [], [], []
    for run in terms:
        counts.append(len(run))
        for array, entry in run:
            arrays.append(array)
            if entry is None:
                specs.append(pl.BlockSpec((bm, array.shape[-1]), lambda i, s: (i, 0)))
            elif array.ndim == 2:
                specs.append(pl.BlockSpec((bm, array.shape[-1]), lambda i, s, entry=entry: (s[entry] * steps + i, 0)))
            else:
                specs.append(pl.BlockSpec((None, bm, array.shape[-1]), lambda i, s, entry=entry: (s[entry], i, 0)))
    count = len(arrays)

    def body(place, *refs):
        runs, at = [], 0
        for n in counts:
            total = refs[at][...].astype(F32)
            for t in refs[at + 1 : at + n]:
                total += t[...].astype(F32)
            runs.append(total.astype(BF16).astype(F32))
            at += n
        g = jnp.concatenate(runs, 1) if len(runs) > 1 else runs[0]
        w, m, v = (r[...] for r in refs[count : count + 3])
        own, w_out, m_out, v_out = refs[-4:]
        w = w.astype(F32)
        m = 0.9 * m + 0.1 * g
        v = 0.95 * v + 0.05 * g * g
        new = (w - 0.02 * (m * lax.rsqrt(v + 1e-8) + 0.1 * w)).astype(BF16)
        own[...] = new
        w_out[...] = new
        m_out[...] = m
        v_out[...] = v

    plain = pl.BlockSpec((bm, columns), lambda i, s: (i, 0))
    of_w = pl.BlockSpec((None, bm, columns), lambda i, s: (layer, i + s[0] * steps, 0))
    of_m = pl.BlockSpec((None, bm, columns), lambda i, s: (layer, i, 0))
    aliased = [] if so_far is None else list(so_far)
    return pl.pallas_call(
        body,
        grid_spec=pltpu.PrefetchScalarGridSpec(
            num_scalar_prefetch=1,
            grid=(steps,),
            in_specs=specs + [of_w, of_m, of_m] + [pl.BlockSpec(memory_space=pl.ANY)] * len(aliased),
            out_specs=[plain, of_w, of_m, of_m],
        ),
        out_shape=[
            jax.ShapeDtypeStruct((rows, columns), BF16),
            jax.ShapeDtypeStruct(w.shape, BF16),
            jax.ShapeDtypeStruct(m.shape, F32),
            jax.ShapeDtypeStruct(v.shape, F32),
        ],
        input_output_aliases={1 + count + 3 + i: 1 + i for i in range(len(aliased))},
        compiler_params=params(1),
        cost_estimate=pl.CostEstimate(flops=10**9, bytes_accessed=rows * columns * 28, transcendentals=0),
        name="adamw",
    )(place, *arrays, w, m, v, *aliased)


def place(new, blocks, positions, layer, steps=3):
    rows, columns = blocks[0].shape
    bm = rows // steps
    count = len(blocks)

    def body(at, *refs):
        for which in range(count):

            @pl.when(pl.program_id(0) == which)
            def _():
                refs[-1][...] = refs[which][...]

    def of_block(which):
        return pl.BlockSpec((bm, columns), lambda k, i, at: (jnp.where(k == which, i, jnp.where(k < which, 0, steps - 1)), 0))

    return pl.pallas_call(
        body,
        grid_spec=pltpu.PrefetchScalarGridSpec(
            num_scalar_prefetch=1,
            grid=(count, steps),
            in_specs=[of_block(which) for which in range(count)] + [pl.BlockSpec(memory_space=pl.ANY)],
            out_specs=pl.BlockSpec((None, bm, columns), lambda k, i, at: (layer, at[k] * steps + i, 0)),
        ),
        out_shape=jax.ShapeDtypeStruct(new.shape, new.dtype),
        input_output_aliases={count + 1: 0},
        compiler_params=params(2),
        cost_estimate=pl.CostEstimate(flops=10**9, bytes_accessed=4 * count * rows * columns, transcendentals=0),
        name="place",
    )(jnp.stack(positions), *blocks, new)


def step(x, dy, w_gate, w_up, w_down, *moments):
    x, dy = x[0], dy[0]
    index = lax.axis_index("dp").astype(jnp.int32)
    chip, core = index // 2, index % 2

    def across(t):
        return lax.ppermute(t, "dp", CROSS)

    def within(t):
        return lax.ppermute(t, "dp", INCHIP)

    dy_far = across(dy)
    a0, gate0, up0, act0 = gates(x, w_gate, w_up, 0)
    h1 = down(act0, w_down, x, 0)
    h1_far = across(h1)
    a1, act1, d_gate1, d_up1 = last_layer(h1, dy, w_gate, w_up, w_down, 1)
    dh1 = into_layer(d_gate1, d_up1, w_gate, w_up, h1, dy, 1)

    def group_sum(g):
        rows = g.shape[0] // 4
        blocks = g.reshape(2, 2, rows, g.shape[1])
        near = within(lax.dynamic_index_in_dim(blocks, 1 - core, 1, keepdims=False))
        ours = lax.dynamic_index_in_dim(g.reshape(4, rows, g.shape[1]), (1 - chip) * 2 + core, 0, False)
        far = across((ours.astype(F32) + lax.dynamic_index_in_dim(near, 1 - chip, 0, False).astype(F32)).astype(BF16))
        return [(g, 0), (near, 1), (far, None)]

    _, d = x.shape
    f = act0.shape[1]
    terms0 = {name: [] for name in "gud"}
    for number, name in enumerate("abc"):
        g = weight_gradient([(act0, dh1)], 1408, d // 3, piece=number)
        terms0["d"].append(group_sum(g))
    cut = f // 2 // BN * BN
    for first, columns, bn in ((0, cut, 512), (cut, f - cut, 768)):
        d_gate0, d_up0 = to_gates(dh1, w_down, gate0, up0, 0, first, columns)
        g = weight_gradient([(a0, d_gate0)], d, bn)
        terms0["g"].append(group_sum(g))
        g = weight_gradient([(a0, d_up0)], d, bn)
        terms0["u"].append(group_sum(g))

    h1_far, _ = lax.optimization_barrier((h1_far, g))
    a1_far, act1_far, d_gate1_far, d_up1_far = last_layer(h1_far, dy_far, w_gate, w_up, w_down, 1)
    act1, act1_far = lax.optimization_barrier((act1, act1_far))
    lanes = f // 2 // 128 * 128
    columns_of = functools.partial(lax.dynamic_slice_in_dim, start_index=chip * lanes, slice_size=f - lanes, axis=1)
    g_down1 = weight_gradient([(columns_of(act1), dy), (columns_of(act1_far), dy_far)], f - lanes, 512)
    half = d // 2
    g_gate1 = weight_gradient([(a1, d_gate1), (a1_far, d_gate1_far)], half, 512, chip, half)
    g_up1 = weight_gradient([(a1, d_up1), (a1_far, d_up1_far)], half, 512, chip, half)

    def of_the_chip(g, rows, offset=None):
        start = 0 if offset is None else offset
        near = within(lax.dynamic_slice_in_dim(g, start + (1 - core) * rows, rows, 0))
        ours = (g, 2) if offset is None else (lax.dynamic_slice_in_dim(g, start + core * rows, rows, 0), None)
        return [[ours, (near, None)]]

    terms1 = {
        "g": of_the_chip(g_gate1, half // 2),
        "u": of_the_chip(g_up1, half // 2),
        "d": of_the_chip(g_down1, f // 4, chip * (f // 2 - lanes)),
    }

    here = jnp.stack([index, chip, core])
    at_near, at_far, at_newer = chip * 2 + 1 - core, (1 - chip) * 2 + core, (1 - chip) * 2 + 1 - core
    new = []
    for which, name in enumerate("gud"):
        w, m, v = (w_gate, w_up, w_down)[which], moments[which], moments[3 + which]
        own0, *so_far = adamw(terms0[name], w, m, v, 0, here, None)
        own1, w_new, m_new, v_new = adamw(terms1[name], w, m, v, 1, here, so_far)
        for layer, own in ((0, own0), (1, own1)):
            label = name + str(layer)
            near = within(own)
            if label != "d1":
                far = across(own)
                newer = within(far)
                w_new = place(w_new, (near, far, newer), (at_near, at_far, at_newer), layer)
                continue
            rows = own.shape[0] // 2
            far = [across(own[part * rows :][:rows]) for part in (0, 1)]
            newer = [within(t) for t in far]
            w_new = place(w_new, (near,), (at_near,), layer)
            w_new = place(w_new, (far[0], newer[0]), (at_far * 2, at_newer * 2), layer)
            w_new = place(w_new, (far[1],), (at_far * 2 + 1,), layer)
            w_new = place(w_new, (newer[1],), (at_newer * 2 + 1,), layer)
        new.append((w_new, m_new, v_new))
    return tuple(one[which] for which in range(3) for one in new)


def solution(mesh):
    sequences, whole, rows, group = P(("rep", "dp")), P(), P(None, "dp"), P("rep")

    return jax.shard_map(
        step,
        mesh=mesh,
        in_specs=(sequences,) * 2 + (whole,) * 3 + (rows,) * 6,
        out_specs=(group,) * 3 + (P("rep", "dp"),) * 6,
        check_vma=False,
    )
```

time: 1960 us -> 1550 us (0.79)
  Pallas kernels: 0 us -> 848 us
  matrix products: 595 us -> 0 us
  waiting for transfers between devices: 1080 us -> 591 us
  other arithmetic: 178 us -> 20.1 us
  starting transfers between devices: 0.37 us -> 24.5 us
    pallas_call x0 -> x32, Pallas kernels: none -> 848 us  [the longest x10 231 us: weight_gradient(): pl.pallas_call(body, grid_spec=pltpu.PrefetchScalarGridSpec(num_scalar_pr...]
    unnamed x15 -> x0, waiting for transfers between devices: 640 us -> none
    dot_general x15 -> x0, matrix products: 595 us -> none  [the longest x5 201 us: layer(): gate = jnp.dot(a, w['w_gate'], preferred_element_type=jnp.float32)]
    ppermute x0 -> x39, waiting for transfers between devices: none -> 591 us  [the longest x16 591 us: across(): return lax.ppermute(t, 'dp', CROSS)]
    reshape x3 -> x0, waiting for transfers between devices: 441 us -> none  [step(): t.reshape(-1, *t.shape[2:])]
    reshape x3 -> x0, other arithmetic: 79.6 us -> none  [step(): t.reshape(-1, *t.shape[2:])]
    unnamed x5 -> x0, other arithmetic: 73.1 us -> none
    unnamed x43 -> x24, local copies, waits for them, and re-layouts: 77.9 us -> 8.32 us
  transfers between devices with their start and end apart: 9 -> 39, of which waited for: 7 -> 9; matrix products, arithmetic and copies ran while one was open for 26% -> 4% of each run, Pallas kernels for 0% -> 33%
where the time goes in v1:
time: 1550 us; the launch traced here: 1540 us
  Pallas kernels  848 us (55%)
  waiting for transfers between devices  591 us (38%)
  local copies, waits for them, and re-layouts  59.2 us (4%)
  starting transfers between devices  24.5 us (2%)
  other arithmetic  20.1 us (1%)
    ppermute x16, waiting for transfers between devices, across(): return lax.ppermute(t, 'dp', CROSS)  591 us
    pallas_call x10, Pallas kernels, weight_gradient(): pl.pallas_call(body, grid_spec=pltpu.PrefetchScalarGridSpec(num_scalar_pr...  231 us
    pallas_call x2, Pallas kernels, last_layer(): pl.pallas_call(body, grid=(pl.cdiv(f, bn),), in_specs=[once((t, d), lambd...  208 us
    pallas_call x6, Pallas kernels, adamw(): pl.pallas_call(body, grid_spec=pltpu.PrefetchScalarGridSpec(num_scalar_pr...  104 us
    pallas_call x1, Pallas kernels, into_layer(): pl.pallas_call(body, grid=(t // bm,), in_specs=[pl.BlockSpec((bm, f), lam...  73 us
    pallas_call x9, Pallas kernels, place(): pl.pallas_call(body, grid_spec=pltpu.PrefetchScalarGridSpec(num_scalar_pr...  72.4 us
    pallas_call x1, Pallas kernels, gates(): pl.pallas_call(body, grid=(n,), in_specs=[once((t, d), lambda j: (0, 0))]...  66.9 us
    pallas_call x2, Pallas kernels, to_gates(): pl.pallas_call(body, grid=(pl.cdiv(columns, bn),), in_specs=[once((t, d),...  57.1 us
  transfers between devices with their start and end apart: 39, of which 9 were waited for; matrix products, arithmetic and copies ran while one was open for 4% of the time, Pallas kernels for 33%

profile of v1, /device:TPU:0, one launch (start us, length us, event | category | flops | bytes accessed | tf_op | source)
XLA Modules:
  0.0 1544.3 jit_solution(4215965274418794451)
XLA Ops:
  0.7 66.9 %gates.1 = (bf16[2048,1536]{1,0:T(8,128)(2,1)}, f32[17,2048,256]{2,1,0:T(8,128)}, f32[17,2048,256]{2,1,0:T(8,128)}, bf16[2048,4224]{1,0:T(8,128)(2,1)}) custom-call(bf16[2048,1536]{1,0:T(8,128)(2,1)} %bitcast.82, bf16[2,1536,4224]{2,1,0:T(8,128)(2,1)} %refs_2_.3, bf16[2,1536,4224]{2,1,0:T(8,128)(2,1)} %refs_2_.4), custom_call_target="tpu_custom_call" | custom-call | flops 53150220288 | bytes 112459776 | tf_op jit(solution)/shard_map/gates/pallas_call | solution.py:70
  67.6 36.0 %down.1.h = bf16[2048,1536]{1,0:T(8,128)(2,1)} custom-call(bf16[2048,4224]{1,0:T(8,128)(2,1)} %get-tuple-element.52.act.refs_0_, bf16[2,4224,1536]{2,1,0:T(8,128)(2,1)} %refs_2_.5, bf16[2048,1536]{1,0:T(8,128)(2,1)} %bitcast.83), custom_call_target="tpu_custom_call" | custom-call | flops 26575110144 | bytes 64880640 | tf_op jit(solution)/shard_map/down/pallas_call | solution.py:93
  103.6 104.0 %last_layer.2 = (bf16[2048,1536]{1,0:T(8,128)(2,1)}, bf16[2048,4224]{1,0:T(8,128)(2,1)}, bf16[2048,4224]{1,0:T(8,128)(2,1)}, bf16[2048,4224]{1,0:T(8,128)(2,1)}) custom-call(bf16[2048,1536]{1,0:T(8,128)(2,1)} %down.1.h, bf16[2048,1536]{1,0:T(8,128)(2,1)} %bitcast.84, bf16[2,1536,4224]{2,1,0:T(8,128)(2,1)} %refs_2_.3, bf16[2,1536,4224]{2,1,0:T(8,128)(2,1)} %refs_2_.4, ...), custom_call_target="tpu_custom_call" | custom-call | flops 79725330432 | bytes 90832896 | tf_op jit(solution)/shard_map/last_layer/pallas_call | solution.py:126
  207.5 73.0 %into_layer.1.dh.refs_1_ = bf16[2048,1536]{1,0:T(8,128)(2,1)} custom-call(bf16[2048,4224]{1,0:T(8,128)(2,1)} %get-tuple-element.54.dg.refs_1_, bf16[2048,4224]{1,0:T(8,128)(2,1)} %get-tuple-element.56.du.refs_1_, bf16[2,1536,4224]{2,1,0:T(8,128)(2,1)} %refs_2_.3, bf16[2,1536,4224]{2,1,0:T(8,128)(2,1)} %refs_2_.4, bf16[2048,1536]{1,0:T(8,128)(2,1)} %down.1.h, ...), custom_call_target="tpu_custom_call" | custom-call | flops 53150220288 | bytes 60555264 | tf_op jit(solution)/shard_map/into_layer/pallas_call | solution.py:155
  280.5 27.2 %to_gates.3 = (bf16[2048,2048]{1,0:T(8,128)(2,1)}, bf16[2048,2048]{1,0:T(8,128)(2,1)}) custom-call(bf16[2048,1536]{1,0:T(8,128)(2,1)} %into_layer.1.dh.refs_1_, bf16[2,4224,1536]{2,1,0:T(8,128)(2,1)} %refs_2_.5, f32[17,2048,256]{2,1,0:T(8,128)} %get-tuple-element.57.gate, f32[17,2048,256]{2,1,0:T(8,128)} %get-tuple-element.58.up), custom_call_target="tpu_custom_call" | custom-call | flops 12884901888 | bytes 56623104 | tf_op jit(solution)/shard_map/to_gates/pallas_call | solution.py:178
  307.8 18.5 %weight_gradient.12.refs_0_ = bf16[1536,2048]{1,0:T(8,128)(2,1)} custom-call(s32[1]{0:T(128)} %constant.100.clone.1.start, bf16[2048,1536]{1,0:T(8,128)(2,1)} %get-tuple-element.55.refs_0_, bf16[2048,2048]{1,0:T(8,128)(2,1)} %get-tuple-element.63.refs_1_), custom_call_target="tpu_custom_call" | custom-call | flops 12884901888 | bytes 20971520 | tf_op jit(solution)/shard_map/weight_gradient/pallas_call | solution.py:206
  326.3 4.0 dynamic-slice_bitcast_fusion.3
  331.1 18.8 %weight_gradient.15.refs_0_ = bf16[1536,2048]{1,0:T(8,128)(2,1)} custom-call(s32[1]{0:T(128)} %constant.100.clone.1.start, bf16[2048,1536]{1,0:T(8,128)(2,1)} %get-tuple-element.55.refs_0_, bf16[2048,2048]{1,0:T(8,128)(2,1)} %get-tuple-element.72.refs_1_), custom_call_target="tpu_custom_call" | custom-call | flops 12884901888 | bytes 20971520 | tf_op jit(solution)/shard_map/weight_gradient/pallas_call | solution.py:206
  349.9 4.0 dynamic-slice_bitcast_fusion.2
  353.8 14.0 weight_gradient.17.refs_0_
  367.8 3.1 dynamic-slice_bitcast_fusion.6
  371.5 14.0 weight_gradient.18.refs_3_
  385.5 3.1 dynamic-slice_bitcast_fusion.5
  388.5 14.0 weight_gradient.19.refs_6_
  402.5 3.1 dynamic-slice_bitcast_fusion.4
  406.1 29.9 %to_gates.2 = (bf16[2048,2176]{1,0:T(8,128)(2,1)}, bf16[2048,2176]{1,0:T(8,128)(2,1)}) custom-call(bf16[2048,1536]{1,0:T(8,128)(2,1)} %into_layer.1.dh.refs_1_, bf16[2,4224,1536]{2,1,0:T(8,128)(2,1)} %refs_2_.5, f32[17,2048,256]{2,1,0:T(8,128)} %get-tuple-element.57.gate, f32[17,2048,256]{2,1,0:T(8,128)} %get-tuple-element.58.up), custom_call_target="tpu_custom_call" | custom-call | flops 13690208256 | bytes 60162048 | tf_op jit(solution)/shard_map/to_gates/pallas_call | solution.py:178
  436.1 20.6 %weight_gradient.10.refs_3_ = bf16[1536,2176]{1,0:T(8,128)(2,1)} custom-call(s32[1]{0:T(128)} %constant.100.clone.1.start, bf16[2048,1536]{1,0:T(8,128)(2,1)} %get-tuple-element.55.refs_0_, bf16[2048,2176]{1,0:T(8,128)(2,1)} %get-tuple-element.59.refs_1_), custom_call_target="tpu_custom_call" | custom-call | flops 13690208256 | bytes 21889024 | tf_op jit(solution)/shard_map/weight_gradient/pallas_call | solution.py:206
  456.6 20.9 %weight_gradient.13.refs_3_ = bf16[1536,2176]{1,0:T(8,128)(2,1)} custom-call(s32[1]{0:T(128)} %constant.100.clone.1.start, bf16[2048,1536]{1,0:T(8,128)(2,1)} %get-tuple-element.55.refs_0_, bf16[2048,2176]{1,0:T(8,128)(2,1)} %get-tuple-element.64.refs_1_), custom_call_target="tpu_custom_call" | custom-call | flops 13690208256 | bytes 21889024 | tf_op jit(solution)/shard_map/weight_gradient/pallas_call | solution.py:206
  477.5 4.1 dynamic-slice_bitcast_fusion.1
  482.6 2.0 dynamic-slice_bitcast_fusion
  486.0 3.0 collective-permute-start
  488.9 1.9 fusion.4
  490.8 2.0 collective-permute-start.26
  492.8 1.9 fusion.5
  494.7 2.5 fusion.2
  497.2 285.6 %collective-permute-done.26.refs_2_ = bf16[1056,512]{1,0:T(8,128)(2,1)S(1)} collective-permute-done((bf16[1056,512]{1,0:T(8,128)(2,1)S(1)}, bf16[1056,512]{1,0:T(8,128)(2,1)S(1)}, u32[]{:S(2)}, u32[]{:S(2)}) %collective-permute-start.26) | collective-permute-done | bytes 1081376 | tf_op jit(solution)/shard_map/ppermute | solution.py:323
  782.8 1.7 collective-permute-start.4
  784.6 1.9 fusion.6
  788.5 3.5 fusion
  792.0 3.0 fusion.1
  795.1 48.2 %collective-permute-done.28.refs_5_ = bf16[1056,512]{1,0:T(8,128)(2,1)S(1)} collective-permute-done((bf16[1056,512]{1,0:T(8,128)(2,1)S(1)}, bf16[1056,512]{1,0:T(8,128)(2,1)S(1)}, u32[]{:S(2)}, u32[]{:S(2)}) %collective-permute-start.28) | collective-permute-done | bytes 1081376 | tf_op jit(solution)/shard_map/ppermute | solution.py:323
  843.3 1.7 collective-permute-start.6
  845.0 21.4 %collective-permute-done.30.refs_8_ = bf16[1056,512]{1,0:T(8,128)(2,1)S(1)} collective-permute-done((bf16[1056,512]{1,0:T(8,128)(2,1)S(1)}, bf16[1056,512]{1,0:T(8,128)(2,1)S(1)}, u32[]{:S(2)}, u32[]{:S(2)}) %collective-permute-start.30) | collective-permute-done | bytes 1081376 | tf_op jit(solution)/shard_map/ppermute | solution.py:323
  868.2 3.7 fusion.3
  874.1 17.9 %adamw.10 = (bf16[1056,1536]{1,0:T(8,128)(2,1)}, bf16[2,4224,1536]{2,1,0:T(8,128)(2,1)}, f32[2,1056,1536]{2,1,0:T(8,128)}, f32[2,1056,1536]{2,1,0:T(8,128)}) custom-call(s32[3]{0:T(128)} %pad_add_fusion.1.place, bf16[4224,512]{1,0:T(8,128)(2,1)} %weight_gradient.17.refs_0_, bf16[2,1056,512]{2,1,0:T(8,128)(2,1)} %copy-done.3, bf16[1056,512]{1,0:T(8,128)(2,1)} %copy-done.9, ...), custom_call_target="tpu_custom_call" | custom-call | flops 1000000000 | bytes 45416448 | tf_op jit(solution)/shard_map/adamw/pallas_call | solution.py:265
  892.0 10.2 collective-permute-done.6.refs_5_
  903.4 17.7 %adamw.6 = (bf16[384,4224]{1,0:T(8,128)(2,1)}, bf16[2,1536,4224]{2,1,0:T(8,128)(2,1)}, f32[2,384,4224]{2,1,0:T(8,128)}, f32[2,384,4224]{2,1,0:T(8,128)}) custom-call(s32[3]{0:T(128)} %pad_add_fusion.1.place, bf16[1536,2048]{1,0:T(8,128)(2,1)} %weight_gradient.12.refs_0_, bf16[2,384,2048]{2,1,0:T(8,128)(2,1)} %collective-permute-done.3.refs_1_, ...), custom_call_target="tpu_custom_call" | custom-call | flops 1000000000 | bytes 45416448 | tf_op jit(solution)/shard_map/adamw/pallas_call | solution.py:265
  921.1 49.3 %collective-permute-done.15.refs_2_ = bf16[384,2048]{1,0:T(8,128)(2,1)} collective-permute-done((bf16[384,2048]{1,0:T(8,128)(2,1)}, bf16[384,2048]{1,0:T(8,128)(2,1)}, u32[]{:S(2)}, u32[]{:S(2)}) %collective-permute-start.15) | collective-permute-done | bytes 1572896 | tf_op jit(solution)/shard_map/ppermute | solution.py:323
  973.1 17.7 %adamw.8 = (bf16[384,4224]{1,0:T(8,128)(2,1)}, bf16[2,1536,4224]{2,1,0:T(8,128)(2,1)}, f32[2,384,4224]{2,1,0:T(8,128)}, f32[2,384,4224]{2,1,0:T(8,128)}) custom-call(s32[3]{0:T(128)} %pad_add_fusion.1.place, bf16[1536,2048]{1,0:T(8,128)(2,1)} %weight_gradient.15.refs_0_, bf16[2,384,2048]{2,1,0:T(8,128)(2,1)} %collective-permute-done.14.refs_1_, ...), custom_call_target="tpu_custom_call" | custom-call | flops 1000000000 | bytes 45416448 | tf_op jit(solution)/shard_map/adamw/pallas_call | solution.py:265
  991.4 104.0 %last_layer.3 = (bf16[2048,1536]{1,0:T(8,128)(2,1)}, bf16[2048,4224]{1,0:T(8,128)(2,1)}, bf16[2048,4224]{1,0:T(8,128)(2,1)}, bf16[2048,4224]{1,0:T(8,128)(2,1)}) custom-call(bf16[2048,1536]{1,0:T(8,128)(2,1)} %collective-permute-done.h, bf16[2048,1536]{1,0:T(8,128)(2,1)} %collective-permute-done.1.dy.refs_3_, bf16[2,1536,4224]{2,1,0:T(8,128)(2,1)} %refs_2_.3, ...), custom_call_target="tpu_custom_call" | custom-call | flops 79725330432 | bytes 90832896 | tf_op jit(solution)/shard_map/last_layer/pallas_call | solution.py:126
  1095.3 11.9 constant_dynamic-slice_fusion.2
  1107.2 37.4 %weight_gradient.16 = bf16[2176,1536]{1,0:T(8,128)(2,1)} custom-call(s32[1]{0:T(128)} %constant.100.clone.1.start, bf16[2048,2176]{1,0:T(8,128)(2,1)} %get-tuple-element.100.refs_0_, bf16[2048,1536]{1,0:T(8,128)(2,1)} %bitcast.87, bf16[2048,2176]{1,0:T(8,128)(2,1)} %get-tuple-element.99.refs_2_, bf16[2048,1536]{1,0:T(8,128)(2,1)} %collective-permute-done.1.dy.refs_3_), custom_call_target="tpu_custom_call" | custom-call | flops 27380416512 | bytes 37093376 | tf_op jit(solution)/shard_map/weight_gradient/pallas_call | solution.py:206
  1144.6 36.1 %weight_gradient.11.refs_0_ = bf16[768,4224]{1,0:T(8,128)(2,1)} custom-call(s32[1]{0:T(128)} %bitcast.4.start, bf16[2048,1536]{1,0:T(8,128)(2,1)} %get-tuple-element.53.refs_0_, bf16[2048,4224]{1,0:T(8,128)(2,1)} %get-tuple-element.54.dg.refs_1_, bf16[2048,1536]{1,0:T(8,128)(2,1)} %get-tuple-element.61.refs_2_, bf16[2048,4224]{1,0:T(8,128)(2,1)} %get-tuple-element.62.refs_3_), custom_call_target="tpu_custom_call" | custom-call | flops 26575110144 | bytes 47382528 | tf_op jit(solution)/shard_map/weight_gradient/pallas_call | solution.py:206
  1180.7 6.0 constant_dynamic-slice_fusion
  1188.4 36.3 %weight_gradient.14.refs_0_ = bf16[768,4224]{1,0:T(8,128)(2,1)} custom-call(s32[1]{0:T(128)} %bitcast.4.start, bf16[2048,1536]{1,0:T(8,128)(2,1)} %get-tuple-element.53.refs_0_, bf16[2048,4224]{1,0:T(8,128)(2,1)} %get-tuple-element.56.du.refs_1_, bf16[2048,1536]{1,0:T(8,128)(2,1)} %get-tuple-element.61.refs_2_, bf16[2048,4224]{1,0:T(8,128)(2,1)} %get-tuple-element.71.refs_3_), custom_call_target="tpu_custom_call" | custom-call | flops 26575110144 | bytes 47382528 | tf_op jit(solution)/shard_map/weight_gradient/pallas_call | solution.py:206
  1224.7 3.9 constant_dynamic-slice_fusion.5
  1229.7 2.0 constant_dynamic-slice_fusion.4
  1232.2 17.0 %adamw.11 = (bf16[1056,1536]{1,0:T(8,128)(2,1)}, bf16[2,4224,1536]{2,1,0:T(8,128)(2,1)}, f32[2,1056,1536]{2,1,0:T(8,128)}, f32[2,1056,1536]{2,1,0:T(8,128)}) custom-call(s32[3]{0:T(128)} %pad_add_fusion.1.place, bf16[1056,1536]{1,0:T(8,128)(2,1)} %get-tuple-element.96.refs_0_, ...), custom_call_target="tpu_custom_call", output_to_operand_aliasing={{1}: (6, {}), {2}: (7, {}), {3}: (8, {})} | custom-call | flops 1000000000 | bytes 45416448 | tf_op jit(solution)/shard_map/adamw/pallas_call | solution.py:265
  1249.1 3.8 fusion.7
  1253.5 6.5 collective-permute-done.22.refs_1_
  1261.5 16.9 %adamw.7 = (bf16[384,4224]{1,0:T(8,128)(2,1)}, bf16[2,1536,4224]{2,1,0:T(8,128)(2,1)}, f32[2,384,4224]{2,1,0:T(8,128)}, f32[2,384,4224]{2,1,0:T(8,128)}) custom-call(s32[3]{0:T(128)} %pad_add_fusion.1.place, bf16[768,4224]{1,0:T(8,128)(2,1)} %weight_gradient.11.refs_0_, ...), custom_call_target="tpu_custom_call", output_to_operand_aliasing={{1}: (6, {}), {2}: (7, {}), {3}: (8, {})} | custom-call | flops 1000000000 | bytes 45416448 | tf_op jit(solution)/shard_map/adamw/pallas_call | solution.py:265
  1279.2 16.9 %adamw.9 = (bf16[384,4224]{1,0:T(8,128)(2,1)}, bf16[2,1536,4224]{2,1,0:T(8,128)(2,1)}, f32[2,384,4224]{2,1,0:T(8,128)}, f32[2,384,4224]{2,1,0:T(8,128)}) custom-call(s32[3]{0:T(128)} %pad_add_fusion.1.place, bf16[768,4224]{1,0:T(8,128)(2,1)} %weight_gradient.14.refs_0_, ...), custom_call_target="tpu_custom_call", output_to_operand_aliasing={{1}: (6, {}), {2}: (7, {}), {3}: (8, {})} | custom-call | flops 1000000000 | bytes 45416448 | tf_op jit(solution)/shard_map/adamw/pallas_call | solution.py:265
  1297.6 32.1 %collective-permute-done.33.refs_0_ = bf16[528,1536]{1,0:T(8,128)(2,1)} collective-permute-done((bf16[528,1536]{1,0:T(8,128)(2,1)}, bf16[528,1536]{1,0:T(8,128)(2,1)}, u32[]{:S(2)}, u32[]{:S(2)}) %collective-permute-start.33) | collective-permute-done | bytes 1622048 | tf_op jit(solution)/shard_map/ppermute | solution.py:323
  1330.2 69.0 %collective-permute-done.8.refs_1_ = bf16[384,4224]{1,0:T(8,128)(2,1)} collective-permute-done((bf16[384,4224]{1,0:T(8,128)(2,1)}, bf16[384,4224]{1,0:T(8,128)(2,1)}, u32[]{:S(2)}, u32[]{:S(2)}) %collective-permute-start.8) | collective-permute-done | bytes 3244064 | tf_op jit(solution)/shard_map/ppermute | solution.py:323
  1399.1 69.0 %collective-permute-done.19.refs_1_ = bf16[384,4224]{1,0:T(8,128)(2,1)} collective-permute-done((bf16[384,4224]{1,0:T(8,128)(2,1)}, bf16[384,4224]{1,0:T(8,128)(2,1)}, u32[]{:S(2)}, u32[]{:S(2)}) %collective-permute-start.19) | collective-permute-done | bytes 3244064 | tf_op jit(solution)/shard_map/ppermute | solution.py:323
  1470.0 11.0 place.13.refs_1_
  1480.9 11.0 place.9.refs_3_
  1491.9 11.0 place.11.refs_3_
  1502.9 4.5 place.14.refs_2_
  1507.4 6.2 place.15.refs_1_
  1513.6 3.4 place.16.refs_1_
  1517.0 3.4 place.17
  1522.0 11.0 place.10
  1533.0 11.0 place.12
  (92 shorter events, 26.3 us)
Async XLA Ops:
  330.3 158.6 %collective-permute-start.3 = (bf16[2,384,2048]{2,1,0:T(8,128)(2,1)}, bf16[2,384,2048]{2,1,0:T(8,128)(2,1)}, u32[]{:S(2)}, u32[]{:S(2)}) collective-permute-start(bf16[2,384,2048]{2,1,0:T(8,128)(2,1)} %dynamic-slice_bitcast_fusion.3), channel_id=1, source_target_pairs={{0,1},{1,0},{2,3},{3,2},{4,5},{5,4},{6,7},{7,6}} | collective-permute-start | bytes 9437192 | tf_op jit(solution)/shard_map/ppermute | solution.py:326
  353.8 137.0 %collective-permute-start.14 = (bf16[2,384,2048]{2,1,0:T(8,128)(2,1)}, bf16[2,384,2048]{2,1,0:T(8,128)(2,1)}, u32[]{:S(2)}, u32[]{:S(2)}) collective-permute-start(bf16[2,384,2048]{2,1,0:T(8,128)(2,1)} %dynamic-slice_bitcast_fusion.2), channel_id=1, source_target_pairs={{0,1},{1,0},{2,3},{3,2},{4,5},{5,4},{6,7},{7,6}} | collective-permute-start | bytes 9437192 | tf_op jit(solution)/shard_map/ppermute | solution.py:326
  370.9 113.6 %collective-permute-start.25 = (bf16[2,1056,512]{2,1,0:T(8,128)(2,1)}, bf16[2,1056,512]{2,1,0:T(8,128)(2,1)S(1)}, u32[]{:S(2)}, u32[]{:S(2)}) collective-permute-start(bf16[2,1056,512]{2,1,0:T(8,128)(2,1)} %dynamic-slice_bitcast_fusion.6), channel_id=1, source_target_pairs={{0,1},{1,0},{2,3},{3,2},{4,5},{5,4},{6,7},{7,6}} | collective-permute-start | bytes 6488072 | tf_op jit(solution)/shard_map/ppermute | solution.py:326
  388.5 97.4 %collective-permute-start.27 = (bf16[2,1056,512]{2,1,0:T(8,128)(2,1)}, bf16[2,1056,512]{2,1,0:T(8,128)(2,1)}, u32[]{:S(2)}, u32[]{:S(2)}) collective-permute-start(bf16[2,1056,512]{2,1,0:T(8,128)(2,1)} %dynamic-slice_bitcast_fusion.5), channel_id=1, source_target_pairs={{0,1},{1,0},{2,3},{3,2},{4,5},{5,4},{6,7},{7,6}} | collective-permute-start | bytes 6488072 | tf_op jit(solution)/shard_map/ppermute | solution.py:326
  405.6 80.3 %collective-permute-start.29 = (bf16[2,1056,512]{2,1,0:T(8,128)(2,1)}, bf16[2,1056,512]{2,1,0:T(8,128)(2,1)}, u32[]{:S(2)}, u32[]{:S(2)}) collective-permute-start(bf16[2,1056,512]{2,1,0:T(8,128)(2,1)} %dynamic-slice_bitcast_fusion.4), channel_id=1, source_target_pairs={{0,1},{1,0},{2,3},{3,2},{4,5},{5,4},{6,7},{7,6}} | collective-permute-start | bytes 6488072 | tf_op jit(solution)/shard_map/ppermute | solution.py:326
  477.5 5.1 copy-start
  484.6 1.3 copy-start.3
  484.6 301.8 %collective-permute-start.5 = (bf16[2,384,2176]{2,1,0:T(8,128)(2,1)}, bf16[2,384,2176]{2,1,0:T(8,128)(2,1)}, u32[]{:S(2)}, u32[]{:S(2)}) collective-permute-start(bf16[2,384,2176]{2,1,0:T(8,128)(2,1)} %dynamic-slice_bitcast_fusion.1), channel_id=1, source_target_pairs={{0,1},{1,0},{2,3},{3,2},{4,5},{5,4},{6,7},{7,6}} | collective-permute-start | bytes 10027016 | tf_op jit(solution)/shard_map/ppermute | solution.py:326
  485.9 300.9 %collective-permute-start.16 = (bf16[2,384,2176]{2,1,0:T(8,128)(2,1)}, bf16[2,384,2176]{2,1,0:T(8,128)(2,1)S(1)}, u32[]{:S(2)}, u32[]{:S(2)}) collective-permute-start(bf16[2,384,2176]{2,1,0:T(8,128)(2,1)} %dynamic-slice_bitcast_fusion), channel_id=1, source_target_pairs={{0,1},{1,0},{2,3},{3,2},{4,5},{5,4},{6,7},{7,6}} | collective-permute-start | bytes 10027016 | tf_op jit(solution)/shard_map/ppermute | solution.py:326
  486.0 504.8 %collective-permute-start = (bf16[2048,1536]{1,0:T(8,128)(2,1)}, bf16[2048,1536]{1,0:T(8,128)(2,1)}, u32[]{:S(2)}, u32[]{:S(2)}) collective-permute-start(bf16[2048,1536]{1,0:T(8,128)(2,1)} %down.1.h), channel_id=1, source_target_pairs={{0,2},{1,3},{2,0},{3,1},{4,6},{5,7},{6,4},{7,5}} | collective-permute-start | bytes 18874376 | tf_op jit(solution)/shard_map/ppermute | solution.py:323
  488.9 502.4 %collective-permute-start.1 = (bf16[2048,1536]{1,0:T(8,128)(2,1)}, bf16[2048,1536]{1,0:T(8,128)(2,1)}, u32[]{:S(2)}, u32[]{:S(2)}) collective-permute-start(bf16[2048,1536]{1,0:T(8,128)(2,1)} %bitcast.86), channel_id=1, source_target_pairs={{0,2},{1,3},{2,0},{3,1},{4,6},{5,7},{6,4},{7,5}} | collective-permute-start | bytes 18874376 | tf_op jit(solution)/shard_map/ppermute | solution.py:323
  490.8 292.0 %collective-permute-start.26 = (bf16[1056,512]{1,0:T(8,128)(2,1)S(1)}, bf16[1056,512]{1,0:T(8,128)(2,1)S(1)}, u32[]{:S(2)}, u32[]{:S(2)}) collective-permute-start(bf16[1056,512]{1,0:T(8,128)(2,1)S(1)} %fusion.4), channel_id=1, source_target_pairs={{0,2},{1,3},{2,0},{3,1},{4,6},{5,7},{6,4},{7,5}} | collective-permute-start | bytes 3244040 | tf_op jit(solution)/shard_map/ppermute | solution.py:323
  782.8 4.0 copy-start.9
  782.8 89.0 %collective-permute-start.4 = (bf16[384,2048]{1,0:T(8,128)(2,1)S(1)}, bf16[384,2048]{1,0:T(8,128)(2,1)S(1)}, u32[]{:S(2)}, u32[]{:S(2)}) collective-permute-start(bf16[384,2048]{1,0:T(8,128)(2,1)S(1)} %fusion.2), channel_id=1, source_target_pairs={{0,2},{1,3},{2,0},{3,1},{4,6},{5,7},{6,4},{7,5}} | collective-permute-start | bytes 4718600 | tf_op jit(solution)/shard_map/ppermute | solution.py:323
  786.5 56.8 %collective-permute-start.28 = (bf16[1056,512]{1,0:T(8,128)(2,1)S(1)}, bf16[1056,512]{1,0:T(8,128)(2,1)S(1)}, u32[]{:S(2)}, u32[]{:S(2)}) collective-permute-start(bf16[1056,512]{1,0:T(8,128)(2,1)S(1)} %fusion.5), channel_id=1, source_target_pairs={{0,2},{1,3},{2,0},{3,1},{4,6},{5,7},{6,4},{7,5}} | collective-permute-start | bytes 3244040 | tf_op jit(solution)/shard_map/ppermute | solution.py:323
  786.9 8.2 copy-start.2
  786.9 79.6 %collective-permute-start.30 = (bf16[1056,512]{1,0:T(8,128)(2,1)S(1)}, bf16[1056,512]{1,0:T(8,128)(2,1)S(1)}, u32[]{:S(2)}, u32[]{:S(2)}) collective-permute-start(bf16[1056,512]{1,0:T(8,128)(2,1)S(1)} %fusion.6), channel_id=1, source_target_pairs={{0,2},{1,3},{2,0},{3,1},{4,6},{5,7},{6,4},{7,5}} | collective-permute-start | bytes 3244040 | tf_op jit(solution)/shard_map/ppermute | solution.py:323
  843.3 28.6 %copy-start.10 = (bf16[1056,512]{1,0:T(8,128)(2,1)}, bf16[1056,512]{1,0:T(8,128)(2,1)S(1)}, u32[]{:S(2)}) copy-start(bf16[1056,512]{1,0:T(8,128)(2,1)S(1)} %collective-permute-done.28.refs_5_) | copy-start | bytes 3244036
  843.3 59.0 %collective-permute-start.6 = (bf16[384,2176]{1,0:T(8,128)(2,1)}, bf16[384,2176]{1,0:T(8,128)(2,1)S(1)}, u32[]{:S(2)}, u32[]{:S(2)}) collective-permute-start(bf16[384,2176]{1,0:T(8,128)(2,1)} %fusion), channel_id=1, source_target_pairs={{0,2},{1,3},{2,0},{3,1},{4,6},{5,7},{6,4},{7,5}} | collective-permute-start | bytes 5013512 | tf_op jit(solution)/shard_map/ppermute | solution.py:323
  866.4 5.4 copy-start.11
  866.5 105.4 %collective-permute-start.17 = (bf16[384,2176]{1,0:T(8,128)(2,1)}, bf16[384,2176]{1,0:T(8,128)(2,1)S(1)}, u32[]{:S(2)}, u32[]{:S(2)}) collective-permute-start(bf16[384,2176]{1,0:T(8,128)(2,1)} %fusion.1), channel_id=1, source_target_pairs={{0,2},{1,3},{2,0},{3,1},{4,6},{5,7},{6,4},{7,5}} | collective-permute-start | bytes 5013512 | tf_op jit(solution)/shard_map/ppermute | solution.py:323
  871.9 1.2 copy-start.8
  873.1 97.3 %collective-permute-start.15 = (bf16[384,2048]{1,0:T(8,128)(2,1)}, bf16[384,2048]{1,0:T(8,128)(2,1)}, u32[]{:S(2)}, u32[]{:S(2)}) collective-permute-start(bf16[384,2048]{1,0:T(8,128)(2,1)} %fusion.3), channel_id=1, source_target_pairs={{0,2},{1,3},{2,0},{3,1},{4,6},{5,7},{6,4},{7,5}} | collective-permute-start | bytes 4718600 | tf_op jit(solution)/shard_map/ppermute | solution.py:323
  902.3 1.2 copy-start.7
  902.3 284.4 %collective-permute-start.36 = (bf16[1056,1536]{1,0:T(8,128)(2,1)}, bf16[1056,1536]{1,0:T(8,128)(2,1)}, u32[]{:S(2)}, u32[]{:S(2)}) collective-permute-start(bf16[1056,1536]{1,0:T(8,128)(2,1)} %get-tuple-element.87), channel_id=1, source_target_pairs={{0,1},{1,0},{2,3},{3,2},{4,5},{5,4},{6,7},{7,6}} | collective-permute-start | bytes 9732104 | tf_op jit(solution)/shard_map/ppermute | solution.py:326
  970.4 217.8 %collective-permute-start.37 = (bf16[1056,1536]{1,0:T(8,128)(2,1)}, bf16[1056,1536]{1,0:T(8,128)(2,1)}, u32[]{:S(2)}, u32[]{:S(2)}) collective-permute-start(bf16[1056,1536]{1,0:T(8,128)(2,1)} %get-tuple-element.87), channel_id=1, source_target_pairs={{0,2},{1,3},{2,0},{3,1},{4,6},{5,7},{6,4},{7,5}} | collective-permute-start | bytes 9732104 | tf_op jit(solution)/shard_map/ppermute | solution.py:323
  971.8 1.2 copy-start.6
  971.8 256.8 %collective-permute-start.10 = (bf16[384,4224]{1,0:T(8,128)(2,1)}, bf16[384,4224]{1,0:T(8,128)(2,1)}, u32[]{:S(2)}, u32[]{:S(2)}) collective-permute-start(bf16[384,4224]{1,0:T(8,128)(2,1)} %get-tuple-element.69), channel_id=1, source_target_pairs={{0,1},{1,0},{2,3},{3,2},{4,5},{5,4},{6,7},{7,6}} | collective-permute-start | bytes 9732104 | tf_op jit(solution)/shard_map/ppermute | solution.py:326
  990.8 240.9 %collective-permute-start.11 = (bf16[384,4224]{1,0:T(8,128)(2,1)}, bf16[384,4224]{1,0:T(8,128)(2,1)}, u32[]{:S(2)}, u32[]{:S(2)}) collective-permute-start(bf16[384,4224]{1,0:T(8,128)(2,1)} %get-tuple-element.69), channel_id=1, source_target_pairs={{0,2},{1,3},{2,0},{3,1},{4,6},{5,7},{6,4},{7,5}} | collective-permute-start | bytes 9732104 | tf_op jit(solution)/shard_map/ppermute | solution.py:323
  991.4 261.6 %collective-permute-start.21 = (bf16[384,4224]{1,0:T(8,128)(2,1)}, bf16[384,4224]{1,0:T(8,128)(2,1)}, u32[]{:S(2)}, u32[]{:S(2)}) collective-permute-start(bf16[384,4224]{1,0:T(8,128)(2,1)} %get-tuple-element.77), channel_id=1, source_target_pairs={{0,1},{1,0},{2,3},{3,2},{4,5},{5,4},{6,7},{7,6}} | collective-permute-start | bytes 9732104 | tf_op jit(solution)/shard_map/ppermute | solution.py:326
  1186.7 73.3 %collective-permute-start.22 = (bf16[384,4224]{1,0:T(8,128)(2,1)}, bf16[384,4224]{1,0:T(8,128)(2,1)S(1)}, u32[]{:S(2)}, u32[]{:S(2)}) collective-permute-start(bf16[384,4224]{1,0:T(8,128)(2,1)} %get-tuple-element.77), channel_id=1, source_target_pairs={{0,2},{1,3},{2,0},{3,1},{4,6},{5,7},{6,4},{7,5}} | collective-permute-start | bytes 9732104 | tf_op jit(solution)/shard_map/ppermute | solution.py:323
  1188.2 43.8 %collective-permute-start.24 = (bf16[1056,1536]{1,0:T(8,128)(2,1)}, bf16[1056,1536]{1,0:T(8,128)(2,1)}, u32[]{:S(2)}, u32[]{:S(2)}) collective-permute-start(bf16[1056,1536]{1,0:T(8,128)(2,1)} %get-tuple-element.95), channel_id=1, source_target_pairs={{0,1},{1,0},{2,3},{3,2},{4,5},{5,4},{6,7},{7,6}} | collective-permute-start | bytes 9732104 | tf_op jit(solution)/shard_map/ppermute | solution.py:326
  1224.7 5.0 copy-start.1
  1228.6 31.4 %collective-permute-start.2 = (bf16[384,4224]{1,0:T(8,128)(2,1)}, bf16[384,4224]{1,0:T(8,128)(2,1)}, u32[]{:S(2)}, u32[]{:S(2)}) collective-permute-start(bf16[384,4224]{1,0:T(8,128)(2,1)} %constant_dynamic-slice_fusion.5), channel_id=1, source_target_pairs={{0,1},{1,0},{2,3},{3,2},{4,5},{5,4},{6,7},{7,6}} | collective-permute-start | bytes 9732104 | tf_op jit(solution)/shard_map/ppermute | solution.py:326
  1231.6 46.7 %collective-permute-start.13 = (bf16[384,4224]{1,0:T(8,128)(2,1)}, bf16[384,4224]{1,0:T(8,128)(2,1)}, u32[]{:S(2)}, u32[]{:S(2)}) collective-permute-start(bf16[384,4224]{1,0:T(8,128)(2,1)} %constant_dynamic-slice_fusion.4), channel_id=1, source_target_pairs={{0,1},{1,0},{2,3},{3,2},{4,5},{5,4},{6,7},{7,6}} | collective-permute-start | bytes 9732104 | tf_op jit(solution)/shard_map/ppermute | solution.py:326
  1232.0 46.7 %collective-permute-start.38 = (bf16[1056,1536]{1,0:T(8,128)(2,1)}, bf16[1056,1536]{1,0:T(8,128)(2,1)}, u32[]{:S(2)}, u32[]{:S(2)}) collective-permute-start(bf16[1056,1536]{1,0:T(8,128)(2,1)} %collective-permute-done.37.refs_1_), channel_id=1, source_target_pairs={{0,1},{1,0},{2,3},{3,2},{4,5},{5,4},{6,7},{7,6}} | collective-permute-start | bytes 9732104 | tf_op jit(solution)/shard_map/ppermute | solution.py:326
  1253.0 43.1 %collective-permute-start.31 = (bf16[528,1536]{1,0:T(8,128)(2,1)}, bf16[528,1536]{1,0:T(8,128)(2,1)}, u32[]{:S(2)}, u32[]{:S(2)}) collective-permute-start(bf16[528,1536]{1,0:T(8,128)(2,1)} %get-tuple-element.98), channel_id=1, source_target_pairs={{0,2},{1,3},{2,0},{3,1},{4,6},{5,7},{6,4},{7,5}} | collective-permute-start | bytes 4866056 | tf_op jit(solution)/shard_map/ppermute | solution.py:323
  1260.0 18.4 %copy-start.4 = (bf16[384,4224]{1,0:T(8,128)(2,1)}, bf16[384,4224]{1,0:T(8,128)(2,1)S(1)}, u32[]{:S(2)}) copy-start(bf16[384,4224]{1,0:T(8,128)(2,1)S(1)} %collective-permute-done.22.refs_1_) | copy-start | bytes 9732100
  1260.0 69.6 %collective-permute-start.12 = (bf16[384,4224]{1,0:T(8,128)(2,1)}, bf16[384,4224]{1,0:T(8,128)(2,1)}, u32[]{:S(2)}, u32[]{:S(2)}) collective-permute-start(bf16[384,4224]{1,0:T(8,128)(2,1)} %collective-permute-done.11.refs_1_), channel_id=1, source_target_pairs={{0,1},{1,0},{2,3},{3,2},{4,5},{5,4},{6,7},{7,6}} | collective-permute-start | bytes 9732104 | tf_op jit(solution)/shard_map/ppermute | solution.py:326
  1260.0 69.6 %collective-permute-start.33 = (bf16[528,1536]{1,0:T(8,128)(2,1)}, bf16[528,1536]{1,0:T(8,128)(2,1)}, u32[]{:S(2)}, u32[]{:S(2)}) collective-permute-start(bf16[528,1536]{1,0:T(8,128)(2,1)} %get-tuple-element.97), channel_id=1, source_target_pairs={{0,2},{1,3},{2,0},{3,1},{4,6},{5,7},{6,4},{7,5}} | collective-permute-start | bytes 4866056 | tf_op jit(solution)/shard_map/ppermute | solution.py:323
  1278.4 51.7 %collective-permute-start.23 = (bf16[384,4224]{1,0:T(8,128)(2,1)S(1)}, bf16[384,4224]{1,0:T(8,128)(2,1)}, u32[]{:S(2)}, u32[]{:S(2)}) collective-permute-start(bf16[384,4224]{1,0:T(8,128)(2,1)S(1)} %collective-permute-done.22.refs_1_), channel_id=1, source_target_pairs={{0,1},{1,0},{2,3},{3,2},{4,5},{5,4},{6,7},{7,6}} | collective-permute-start | bytes 9732104 | tf_op jit(solution)/shard_map/ppermute | solution.py:326
  1278.6 120.5 %collective-permute-start.8 = (bf16[384,4224]{1,0:T(8,128)(2,1)}, bf16[384,4224]{1,0:T(8,128)(2,1)}, u32[]{:S(2)}, u32[]{:S(2)}) collective-permute-start(bf16[384,4224]{1,0:T(8,128)(2,1)} %get-tuple-element.68), channel_id=1, source_target_pairs={{0,2},{1,3},{2,0},{3,1},{4,6},{5,7},{6,4},{7,5}} | collective-permute-start | bytes 9732104 | tf_op jit(solution)/shard_map/ppermute | solution.py:323
  1296.1 172.1 %collective-permute-start.19 = (bf16[384,4224]{1,0:T(8,128)(2,1)}, bf16[384,4224]{1,0:T(8,128)(2,1)}, u32[]{:S(2)}, u32[]{:S(2)}) collective-permute-start(bf16[384,4224]{1,0:T(8,128)(2,1)} %get-tuple-element.76), channel_id=1, source_target_pairs={{0,2},{1,3},{2,0},{3,1},{4,6},{5,7},{6,4},{7,5}} | collective-permute-start | bytes 9732104 | tf_op jit(solution)/shard_map/ppermute | solution.py:323
  1329.6 139.1 %collective-permute-start.35 = (bf16[1056,1536]{1,0:T(8,128)(2,1)}, bf16[1056,1536]{1,0:T(8,128)(2,1)}, u32[]{:S(2)}, u32[]{:S(2)}) collective-permute-start(bf16[1056,1536]{1,0:T(8,128)(2,1)} %get-tuple-element.86), channel_id=1, source_target_pairs={{0,1},{1,0},{2,3},{3,2},{4,5},{5,4},{6,7},{7,6}} | collective-permute-start | bytes 9732104 | tf_op jit(solution)/shard_map/ppermute | solution.py:326
  1329.6 138.6 %collective-permute-start.34 = (bf16[528,1536]{1,0:T(8,128)(2,1)}, bf16[528,1536]{1,0:T(8,128)(2,1)}, u32[]{:S(2)}, u32[]{:S(2)}) collective-permute-start(bf16[528,1536]{1,0:T(8,128)(2,1)} %collective-permute-done.33.refs_0_), channel_id=1, source_target_pairs={{0,1},{1,0},{2,3},{3,2},{4,5},{5,4},{6,7},{7,6}} | collective-permute-start | bytes 4866056 | tf_op jit(solution)/shard_map/ppermute | solution.py:326
  1330.1 190.2 %collective-permute-start.7 = (bf16[384,4224]{1,0:T(8,128)(2,1)}, bf16[384,4224]{1,0:T(8,128)(2,1)S(1)}, u32[]{:S(2)}, u32[]{:S(2)}) collective-permute-start(bf16[384,4224]{1,0:T(8,128)(2,1)} %get-tuple-element.68), channel_id=1, source_target_pairs={{0,1},{1,0},{2,3},{3,2},{4,5},{5,4},{6,7},{7,6}} | collective-permute-start | bytes 9732104 | tf_op jit(solution)/shard_map/ppermute | solution.py:326
  1399.1 121.2 %collective-permute-start.9 = (bf16[384,4224]{1,0:T(8,128)(2,1)}, bf16[384,4224]{1,0:T(8,128)(2,1)}, u32[]{:S(2)}, u32[]{:S(2)}) collective-permute-start(bf16[384,4224]{1,0:T(8,128)(2,1)} %collective-permute-done.8.refs_1_), channel_id=1, source_target_pairs={{0,1},{1,0},{2,3},{3,2},{4,5},{5,4},{6,7},{7,6}} | collective-permute-start | bytes 9732104 | tf_op jit(solution)/shard_map/ppermute | solution.py:326
  1468.2 64.8 %collective-permute-start.18 = (bf16[384,4224]{1,0:T(8,128)(2,1)}, bf16[384,4224]{1,0:T(8,128)(2,1)}, u32[]{:S(2)}, u32[]{:S(2)}) collective-permute-start(bf16[384,4224]{1,0:T(8,128)(2,1)} %get-tuple-element.76), channel_id=1, source_target_pairs={{0,1},{1,0},{2,3},{3,2},{4,5},{5,4},{6,7},{7,6}} | collective-permute-start | bytes 9732104 | tf_op jit(solution)/shard_map/ppermute | solution.py:326
  1468.2 64.8 %collective-permute-start.20 = (bf16[384,4224]{1,0:T(8,128)(2,1)}, bf16[384,4224]{1,0:T(8,128)(2,1)}, u32[]{:S(2)}, u32[]{:S(2)}) collective-permute-start(bf16[384,4224]{1,0:T(8,128)(2,1)} %collective-permute-done.19.refs_1_), channel_id=1, source_target_pairs={{0,1},{1,0},{2,3},{3,2},{4,5},{5,4},{6,7},{7,6}} | collective-permute-start | bytes 9732104 | tf_op jit(solution)/shard_map/ppermute | solution.py:326
  1468.7 48.3 %collective-permute-start.32 = (bf16[528,1536]{1,0:T(8,128)(2,1)}, bf16[528,1536]{1,0:T(8,128)(2,1)}, u32[]{:S(2)}, u32[]{:S(2)}) collective-permute-start(bf16[528,1536]{1,0:T(8,128)(2,1)} %collective-permute-done.31.refs_0_), channel_id=1, source_target_pairs={{0,1},{1,0},{2,3},{3,2},{4,5},{5,4},{6,7},{7,6}} | collective-permute-start | bytes 4866056 | tf_op jit(solution)/shard_map/ppermute | solution.py:326
  1520.4 1.7 copy-start.5

commit v2 on v1

--- a/solution.py
+++ b/solution.py
@@ -1,5 +1,3 @@
-import functools
-
 import jax
 import jax.numpy as jnp
 from jax import lax
@@ -42,6 +40,10 @@
     return pl.BlockSpec(shape, index, pipeline_mode=pl.Buffered(1))
 
 
+def parts(n, count=4):
+    return [pl.ds(i * (n // count), n // count) for i in range(count)]
+
+
 def norm_into(h, a, rows=256):
     def chunk(i, _):
         at = pl.ds(pl.multiple_of(i * rows, rows), rows)
@@ -60,12 +62,12 @@
         def _():
             norm_into(x, a)
 
-        rows = a[...]
-        g = dot(rows, wg[...], ((1,), (0,)))
-        u = dot(rows, wu[...], ((1,), (0,)))
-        gate[...] = g
-        up[...] = u
-        act[...] = (g * jax.nn.sigmoid(g) * u).astype(BF16)
+        for at in parts(t):
+            g = dot(a[at, :], wg[...], ((1,), (0,)))
+            u = dot(a[at, :], wu[...], ((1,), (0,)))
+            gate[at, :] = g
+            up[at, :] = u
+            act[at, :] = (g * jax.nn.sigmoid(g) * u).astype(BF16)
 
     return pl.pallas_call(
         body,
@@ -106,35 +108,50 @@
     )(act, w_down, h)
 
 
-def last_layer(h, dy, w_gate, w_up, w_down, layer, bn=BN):
+def last_layer(h, dy, w_gate, w_up, w_down, layer, chip, kept, bn=BN):
     t, d = h.shape
     f = w_gate.shape[2]
-
-    def body(h, dy, wg, wu, wd, a, act, d_gate, d_up):
+    skip = f // 2 // bn
+    wanted = pl.cdiv(kept, bn)
+
+    def body(chip, h, dy, wg, wu, wd, a, act, d_gate, d_up):
         @pl.when(pl.program_id(0) == 0)
         def _():
             norm_into(h, a)
 
-        g = dot(a[...], wg[...], ((1,), (0,)))
-        u = dot(a[...], wu[...], ((1,), (0,)))
-        da = dot(dy[...], wd[...], ((1,), (1,))).astype(BF16).astype(F32)
-        silu, slope = silu_parts(g)
-        act[...] = (silu * u).astype(BF16)
-        d_gate[...] = (da * u * slope).astype(BF16)
-        d_up[...] = (da * silu).astype(BF16)
-
-    return pl.pallas_call(
-        body,
-        grid=(pl.cdiv(f, bn),),
-        in_specs=[once((t, d), lambda j: (0, 0))] * 2
-        + [pl.BlockSpec((None, d, bn), lambda j: (layer, 0, j))] * 2
-        + [pl.BlockSpec((None, bn, d), lambda j: (layer, j, 0))],
-        out_specs=[pl.BlockSpec((t, d), lambda j: (0, 0))] + [pl.BlockSpec((t, bn), lambda j: (0, j))] * 3,
-        out_shape=[jax.ShapeDtypeStruct((t, d), BF16)] + [jax.ShapeDtypeStruct((t, f), BF16)] * 3,
+        for at in parts(t):
+            g = dot(a[at, :], wg[...], ((1,), (0,)))
+            u = dot(a[at, :], wu[...], ((1,), (0,)))
+            da = dot(dy[at, :], wd[...], ((1,), (1,))).astype(BF16).astype(F32)
+            silu, slope = silu_parts(g)
+            act[at, :] = (silu * u).astype(BF16)
+            d_gate[at, :] = (da * u * slope).astype(BF16)
+            d_up[at, :] = (da * silu).astype(BF16)
+
+    def act_block(j, s):
+        at = j - s[0] * skip
+        return 0, jnp.where(jnp.logical_and(at >= 0, at < wanted), at, wanted)
+
+    return pl.pallas_call(
+        body,
+        grid_spec=pltpu.PrefetchScalarGridSpec(
+            num_scalar_prefetch=1,
+            grid=(pl.cdiv(f, bn),),
+            in_specs=[once((t, d), lambda j, s: (0, 0))] * 2
+            + [pl.BlockSpec((None, d, bn), lambda j, s: (layer, 0, j))] * 2
+            + [pl.BlockSpec((None, bn, d), lambda j, s: (layer, j, 0))],
+            out_specs=[
+                pl.BlockSpec((t, d), lambda j, s: (0, 0)),
+                pl.BlockSpec((t, bn), act_block),
+            ]
+            + [pl.BlockSpec((t, bn), lambda j, s: (0, j))] * 2,
+        ),
+        out_shape=[jax.ShapeDtypeStruct((t, d), BF16), jax.ShapeDtypeStruct((t, (wanted + 1) * bn), BF16)]
+        + [jax.ShapeDtypeStruct((t, f), BF16)] * 2,
         compiler_params=params(1),
         cost_estimate=cost(3, t * d * f, 6 * d * f + 6 * t * f),
         name="last_layer",
-    )(h, dy, w_gate, w_up, w_down)
+    )(chip.reshape(1), h, dy, w_gate, w_up, w_down)
 
 
 def into_layer(d_gate, d_up, w_gate, w_up, h, dy, layer, bm=256):
@@ -170,17 +187,21 @@
     t, d = dh.shape
 
     def body(dh, wd, gate, up, d_gate, d_up):
-        da = dot(dh[...], wd[...], ((1,), (1,))).astype(BF16).astype(F32)
-        silu, slope = silu_parts(gate[...])
-        d_gate[...] = (da * up[...] * slope).astype(BF16)
-        d_up[...] = (da * silu).astype(BF16)
-
-    return pl.pallas_call(
-        body,
-        grid=(pl.cdiv(columns, bn),),
-        in_specs=[once((t, d), lambda j: (0, 0)), pl.BlockSpec((None, bn, d), lambda j: (layer, j + first // bn, 0))]
-        + [pl.BlockSpec((None, t, bn), lambda j: (j + first // bn, 0, 0))] * 2,
-        out_specs=[pl.BlockSpec((t, bn), lambda j: (0, j))] * 2,
+        for block in range(2):
+            columns_at = pl.ds(block * bn, bn)
+            for at in parts(t):
+                da = dot(dh[at, :], wd[columns_at, :], ((1,), (1,))).astype(BF16).astype(F32)
+                silu, slope = silu_parts(gate[block, at, :])
+                d_gate[at, columns_at] = (da * up[block, at, :] * slope).astype(BF16)
+                d_up[at, columns_at] = (da * silu).astype(BF16)
+
+    skip = first // (2 * bn)
+    return pl.pallas_call(
+        body,
+        grid=(pl.cdiv(columns, 2 * bn),),
+        in_specs=[once((t, d), lambda j: (0, 0)), pl.BlockSpec((None, 2 * bn, d), lambda j: (layer, j + skip, 0))]
+        + [pl.BlockSpec((2, t, bn), lambda j: (j + skip, 0, 0))] * 2,
+        out_specs=[pl.BlockSpec((t, 2 * bn), lambda j: (0, j))] * 2,
         out_shape=[jax.ShapeDtypeStruct((t, columns), BF16)] * 2,
         compiler_params=params(1),
         cost_estimate=cost(1, t * d * columns, 2 * d * columns + 12 * t * columns),
@@ -328,38 +349,42 @@
     dy_far = across(dy)
     a0, gate0, up0, act0 = gates(x, w_gate, w_up, 0)
     h1 = down(act0, w_down, x, 0)
+    f = act0.shape[1]
+    kept = f - f // 2 // BN * BN
     h1_far = across(h1)
-    a1, act1, d_gate1, d_up1 = last_layer(h1, dy, w_gate, w_up, w_down, 1)
+    a1, act1, d_gate1, d_up1 = last_layer(h1, dy, w_gate, w_up, w_down, 1, chip, kept)
     dh1 = into_layer(d_gate1, d_up1, w_gate, w_up, h1, dy, 1)
 
-    def group_sum(g):
+    def group_sum(g, whole=True):
         rows = g.shape[0] // 4
-        blocks = g.reshape(2, 2, rows, g.shape[1])
-        near = within(lax.dynamic_index_in_dim(blocks, 1 - core, 1, keepdims=False))
-        ours = lax.dynamic_index_in_dim(g.reshape(4, rows, g.shape[1]), (1 - chip) * 2 + core, 0, False)
-        far = across((ours.astype(F32) + lax.dynamic_index_in_dim(near, 1 - chip, 0, False).astype(F32)).astype(BF16))
-        return [(g, 0), (near, 1), (far, None)]
+        blocks = g.reshape(4, rows, g.shape[1])
+        far_block = (1 - chip) * 2 + core
+        if whole:
+            near = within(g)
+            theirs = lax.dynamic_index_in_dim(near.reshape(blocks.shape), far_block, 0, False)
+        else:
+            near = within(lax.dynamic_index_in_dim(g.reshape(2, 2, rows, g.shape[1]), 1 - core, 1, keepdims=False))
+            theirs = lax.dynamic_index_in_dim(near, 1 - chip, 0, False)
+        ours = lax.dynamic_index_in_dim(blocks, far_block, 0, False)
+        far = across((ours.astype(F32) + theirs.astype(F32)).astype(BF16))
+        return [(g, 0), (near, 0 if whole else 1), (far, None)]
 
     _, d = x.shape
-    f = act0.shape[1]
     terms0 = {name: [] for name in "gud"}
     for number, name in enumerate("abc"):
         g = weight_gradient([(act0, dh1)], 1408, d // 3, piece=number)
-        terms0["d"].append(group_sum(g))
+        terms0["d"].append(group_sum(g, name != "c"))
     cut = f // 2 // BN * BN
-    for first, columns, bn in ((0, cut, 512), (cut, f - cut, 768)):
+    for name, first, columns, bn in (("a", 0, cut, 512), ("b", cut, f - cut, 768)):
         d_gate0, d_up0 = to_gates(dh1, w_down, gate0, up0, 0, first, columns)
         g = weight_gradient([(a0, d_gate0)], d, bn)
-        terms0["g"].append(group_sum(g))
+        terms0["g"].append(group_sum(g, name != "a"))
         g = weight_gradient([(a0, d_up0)], d, bn)
         terms0["u"].append(group_sum(g))
 
     h1_far, _ = lax.optimization_barrier((h1_far, g))
-    a1_far, act1_far, d_gate1_far, d_up1_far = last_layer(h1_far, dy_far, w_gate, w_up, w_down, 1)
-    act1, act1_far = lax.optimization_barrier((act1, act1_far))
-    lanes = f // 2 // 128 * 128
-    columns_of = functools.partial(lax.dynamic_slice_in_dim, start_index=chip * lanes, slice_size=f - lanes, axis=1)
-    g_down1 = weight_gradient([(columns_of(act1), dy), (columns_of(act1_far), dy_far)], f - lanes, 512)
+    a1_far, act1_far, d_gate1_far, d_up1_far = last_layer(h1_far, dy_far, w_gate, w_up, w_down, 1, chip, kept)
+    g_down1 = weight_gradient([(act1, dy), (act1_far, dy_far)], kept, 512, None, kept)
     half = d // 2
     g_gate1 = weight_gradient([(a1, d_gate1), (a1_far, d_gate1_far)], half, 512, chip, half)
     g_up1 = weight_gradient([(a1, d_up1), (a1_far, d_up1_far)], half, 512, chip, half)
@@ -373,7 +398,7 @@
     terms1 = {
         "g": of_the_chip(g_gate1, half // 2),
         "u": of_the_chip(g_up1, half // 2),
-        "d": of_the_chip(g_down1, f // 4, chip * (f // 2 - lanes)),
+        "d": of_the_chip(g_down1, f // 4, chip * (f // 2 - (f - kept))),
     }
 
     here = jnp.stack([index, chip, core])

time: 1550 us -> 1290 us (0.83)
  waiting for transfers between devices: 591 us -> 373 us
  local copies, waits for them, and re-layouts: 59.2 us -> 21.7 us
    ppermute x16, waiting for transfers between devices: 591 us -> 373 us  [across(): return lax.ppermute(t, 'dp', CROSS)]
    squeeze x7 -> x2, local copies, waits for them, and re-layouts: 23.3 us -> 5.72 us  [group_sum(): lax.dynamic_index_in_dim(g.reshape(2, 2, rows, g.shape[1]), 1 - core, 1,...]
  transfers between devices with their start and end apart: 39 -> 39, of which waited for: 9 -> 8; matrix products, arithmetic and copies ran while one was open for 4% -> 4% of each run, Pallas kernels for 33% -> 56%
where the time goes in v2:
time: 1290 us; the launch traced here: 1280 us
  Pallas kernels  835 us (65%)
  waiting for transfers between devices  373 us (29%)
  other arithmetic  24.2 us (2%)
  starting transfers between devices  22.6 us (2%)
  local copies, waits for them, and re-layouts  21.7 us (2%)
    ppermute x16, waiting for transfers between devices, across(): return lax.ppermute(t, 'dp', CROSS)  373 us
    pallas_call x10, Pallas kernels, weight_gradient(): pl.pallas_call(body, grid_spec=pltpu.PrefetchScalarGridSpec(num_scalar_pr...  231 us
    pallas_call x2, Pallas kernels, last_layer(): pl.pallas_call(body, grid_spec=pltpu.PrefetchScalarGridSpec(num_scalar_pr...  196 us
    pallas_call x6, Pallas kernels, adamw(): pl.pallas_call(body, grid_spec=pltpu.PrefetchScalarGridSpec(num_scalar_pr...  104 us
    pallas_call x1, Pallas kernels, into_layer(): pl.pallas_call(body, grid=(t // bm,), in_specs=[pl.BlockSpec((bm, f), lam...  73 us
    pallas_call x9, Pallas kernels, place(): pl.pallas_call(body, grid_spec=pltpu.PrefetchScalarGridSpec(num_scalar_pr...  72.4 us
    pallas_call x1, Pallas kernels, gates(): pl.pallas_call(body, grid=(n,), in_specs=[once((t, d), lambda j: (0, 0))]...  66.6 us
    pallas_call x2, Pallas kernels, to_gates(): pl.pallas_call(body, grid=(pl.cdiv(columns, 2 * bn),), in_specs=[once((t,...  55.9 us
  transfers between devices with their start and end apart: 39, of which 8 were waited for; matrix products, arithmetic and copies ran while one was open for 4% of the time, Pallas kernels for 56%

profile of v2, /device:TPU:0, one launch (start us, length us, event | category | flops | bytes accessed | tf_op | source)
XLA Modules:
  0.0 1277.5 jit_solution(11430308682193179859)
XLA Ops:
  0.6 66.6 %gates.1 = (bf16[2048,1536]{1,0:T(8,128)(2,1)}, f32[17,2048,256]{2,1,0:T(8,128)}, f32[17,2048,256]{2,1,0:T(8,128)}, bf16[2048,4224]{1,0:T(8,128)(2,1)}) custom-call(bf16[2048,1536]{1,0:T(8,128)(2,1)} %bitcast.57, bf16[2,1536,4224]{2,1,0:T(8,128)(2,1)} %refs_2_.3, bf16[2,1536,4224]{2,1,0:T(8,128)(2,1)} %refs_2_.4), custom_call_target="tpu_custom_call" | custom-call | flops 53150220288 | bytes 112459776 | tf_op jit(solution)/shard_map/gates/pallas_call | solution.py:72
  67.2 35.9 %down.1.h = bf16[2048,1536]{1,0:T(8,128)(2,1)} custom-call(bf16[2048,4224]{1,0:T(8,128)(2,1)} %get-tuple-element.50.act.refs_0_, bf16[2,4224,1536]{2,1,0:T(8,128)(2,1)} %refs_2_.5, bf16[2048,1536]{1,0:T(8,128)(2,1)} %bitcast.58), custom_call_target="tpu_custom_call" | custom-call | flops 26575110144 | bytes 64880640 | tf_op jit(solution)/shard_map/down/pallas_call | solution.py:95
  103.1 3.3 collective-permute-start
  106.4 98.0 %last_layer.2 = (bf16[2048,1536]{1,0:T(8,128)(2,1)}, bf16[2048,2560]{1,0:T(8,128)(2,1)}, bf16[2048,4224]{1,0:T(8,128)(2,1)}, bf16[2048,4224]{1,0:T(8,128)(2,1)}) custom-call(s32[1]{0:T(128)} %bitcast.4.chip.start, bf16[2048,1536]{1,0:T(8,128)(2,1)} %down.1.h, bf16[2048,1536]{1,0:T(8,128)(2,1)} %bitcast.60, bf16[2,1536,4224]{2,1,0:T(8,128)(2,1)} %refs_2_.3, ...), custom_call_target="tpu_custom_call" | custom-call | flops 79725330432 | bytes 90832896 | tf_op jit(solution)/shard_map/last_layer/pallas_call | solution.py:135
  204.4 73.0 %into_layer.1.dh.refs_1_ = bf16[2048,1536]{1,0:T(8,128)(2,1)} custom-call(bf16[2048,4224]{1,0:T(8,128)(2,1)} %get-tuple-element.52.dg.refs_1_, bf16[2048,4224]{1,0:T(8,128)(2,1)} %get-tuple-element.54.du.refs_1_, bf16[2,1536,4224]{2,1,0:T(8,128)(2,1)} %refs_2_.3, bf16[2,1536,4224]{2,1,0:T(8,128)(2,1)} %refs_2_.4, bf16[2048,1536]{1,0:T(8,128)(2,1)} %down.1.h, ...), custom_call_target="tpu_custom_call" | custom-call | flops 53150220288 | bytes 60555264 | tf_op jit(solution)/shard_map/into_layer/pallas_call | solution.py:172
  277.4 14.0 %weight_gradient.17.refs_0_ = bf16[4224,512]{1,0:T(8,128)(2,1)} custom-call(s32[1]{0:T(128)} %constant.84.clone.1.start, bf16[2048,4224]{1,0:T(8,128)(2,1)} %get-tuple-element.50.act.refs_0_, bf16[2048,1536]{1,0:T(8,128)(2,1)} %into_layer.1.dh.refs_1_), custom_call_target="tpu_custom_call" | custom-call | flops 8858370048 | bytes 23724032 | tf_op jit(solution)/shard_map/weight_gradient/pallas_call | solution.py:227
  291.5 14.0 %weight_gradient.18.refs_3_ = bf16[4224,512]{1,0:T(8,128)(2,1)} custom-call(s32[1]{0:T(128)} %constant.84.clone.1.start, bf16[2048,4224]{1,0:T(8,128)(2,1)} %get-tuple-element.50.act.refs_0_, bf16[2048,1536]{1,0:T(8,128)(2,1)} %into_layer.1.dh.refs_1_), custom_call_target="tpu_custom_call" | custom-call | flops 8858370048 | bytes 23724032 | tf_op jit(solution)/shard_map/weight_gradient/pallas_call | solution.py:227
  306.0 14.2 %weight_gradient.19.refs_6_ = bf16[4224,512]{1,0:T(8,128)(2,1)} custom-call(s32[1]{0:T(128)} %constant.84.clone.1.start, bf16[2048,4224]{1,0:T(8,128)(2,1)} %get-tuple-element.50.act.refs_0_, bf16[2048,1536]{1,0:T(8,128)(2,1)} %into_layer.1.dh.refs_1_), custom_call_target="tpu_custom_call" | custom-call | flops 8858370048 | bytes 23724032 | tf_op jit(solution)/shard_map/weight_gradient/pallas_call | solution.py:227
  320.3 1.7 dynamic-slice_bitcast_fusion.1
  322.1 26.2 %to_gates.3 = (bf16[2048,2048]{1,0:T(8,128)(2,1)}, bf16[2048,2048]{1,0:T(8,128)(2,1)}) custom-call(bf16[2048,1536]{1,0:T(8,128)(2,1)} %into_layer.1.dh.refs_1_, bf16[2,4224,1536]{2,1,0:T(8,128)(2,1)} %refs_2_.5, f32[17,2048,256]{2,1,0:T(8,128)} %get-tuple-element.55.gate, f32[17,2048,256]{2,1,0:T(8,128)} %get-tuple-element.56.up), custom_call_target="tpu_custom_call" | custom-call | flops 12884901888 | bytes 56623104 | tf_op jit(solution)/shard_map/to_gates/pallas_call | solution.py:199
  348.3 18.6 %weight_gradient.15.refs_0_ = bf16[1536,2048]{1,0:T(8,128)(2,1)} custom-call(s32[1]{0:T(128)} %constant.84.clone.1.start, bf16[2048,1536]{1,0:T(8,128)(2,1)} %get-tuple-element.53.refs_0_, bf16[2048,2048]{1,0:T(8,128)(2,1)} %get-tuple-element.70.refs_1_), custom_call_target="tpu_custom_call" | custom-call | flops 12884901888 | bytes 20971520 | tf_op jit(solution)/shard_map/weight_gradient/pallas_call | solution.py:227
  367.4 18.6 %weight_gradient.12.refs_0_ = bf16[1536,2048]{1,0:T(8,128)(2,1)} custom-call(s32[1]{0:T(128)} %constant.84.clone.1.start, bf16[2048,1536]{1,0:T(8,128)(2,1)} %get-tuple-element.53.refs_0_, bf16[2048,2048]{1,0:T(8,128)(2,1)} %get-tuple-element.61.refs_1_), custom_call_target="tpu_custom_call" | custom-call | flops 12884901888 | bytes 20971520 | tf_op jit(solution)/shard_map/weight_gradient/pallas_call | solution.py:227
  386.0 4.0 dynamic-slice_bitcast_fusion
  390.0 29.7 %to_gates.2 = (bf16[2048,2176]{1,0:T(8,128)(2,1)}, bf16[2048,2176]{1,0:T(8,128)(2,1)}) custom-call(bf16[2048,1536]{1,0:T(8,128)(2,1)} %into_layer.1.dh.refs_1_, bf16[2,4224,1536]{2,1,0:T(8,128)(2,1)} %refs_2_.5, f32[17,2048,256]{2,1,0:T(8,128)} %get-tuple-element.55.gate, f32[17,2048,256]{2,1,0:T(8,128)} %get-tuple-element.56.up), custom_call_target="tpu_custom_call" | custom-call | flops 13690208256 | bytes 60162048 | tf_op jit(solution)/shard_map/to_gates/pallas_call | solution.py:199
  419.7 2.8 fusion.6
  422.5 2.0 collective-permute-start.30
  424.5 20.6 %weight_gradient.10.refs_3_ = bf16[1536,2176]{1,0:T(8,128)(2,1)} custom-call(s32[1]{0:T(128)} %constant.84.clone.1.start, bf16[2048,1536]{1,0:T(8,128)(2,1)} %get-tuple-element.53.refs_0_, bf16[2048,2176]{1,0:T(8,128)(2,1)} %get-tuple-element.57.refs_1_), custom_call_target="tpu_custom_call" | custom-call | flops 13690208256 | bytes 21889024 | tf_op jit(solution)/shard_map/weight_gradient/pallas_call | solution.py:227
  445.2 0.7 pad_add_fusion.1.place
  445.8 2.8 fusion.4
  448.7 2.9 fusion.5
  451.6 2.0 collective-permute-start.28
  453.6 21.0 %weight_gradient.13.refs_3_ = bf16[1536,2176]{1,0:T(8,128)(2,1)} custom-call(s32[1]{0:T(128)} %constant.84.clone.1.start, bf16[2048,1536]{1,0:T(8,128)(2,1)} %get-tuple-element.53.refs_0_, bf16[2048,2176]{1,0:T(8,128)(2,1)} %get-tuple-element.62.refs_1_), custom_call_target="tpu_custom_call" | custom-call | flops 13690208256 | bytes 21889024 | tf_op jit(solution)/shard_map/weight_gradient/pallas_call | solution.py:227
  474.5 3.2 fusion.2
  477.7 0.9 collective-permute-done.26.refs_2_
  478.6 22.4 %collective-permute-done.28.refs_5_ = bf16[1056,512]{1,0:T(8,128)(2,1)} collective-permute-done((bf16[1056,512]{1,0:T(8,128)(2,1)}, bf16[1056,512]{1,0:T(8,128)(2,1)}, u32[]{:S(2)}, u32[]{:S(2)}) %collective-permute-start.28) | collective-permute-done | bytes 1081376 | tf_op jit(solution)/shard_map/ppermute | solution.py:344
  501.0 17.9 %adamw.10 = (bf16[1056,1536]{1,0:T(8,128)(2,1)}, bf16[2,4224,1536]{2,1,0:T(8,128)(2,1)}, f32[2,1056,1536]{2,1,0:T(8,128)}, f32[2,1056,1536]{2,1,0:T(8,128)}) custom-call(s32[3]{0:T(128)} %pad_add_fusion.1.place, bf16[4224,512]{1,0:T(8,128)(2,1)} %weight_gradient.17.refs_0_, bf16[4224,512]{1,0:T(8,128)(2,1)} %collective-permute-done.25.refs_1_, ...), custom_call_target="tpu_custom_call" | custom-call | flops 1000000000 | bytes 45416448 | tf_op jit(solution)/shard_map/adamw/pallas_call | solution.py:286
  519.3 3.7 fusion.3
  523.0 1.7 collective-permute-start.15
  524.7 98.1 %last_layer.3 = (bf16[2048,1536]{1,0:T(8,128)(2,1)}, bf16[2048,2560]{1,0:T(8,128)(2,1)}, bf16[2048,4224]{1,0:T(8,128)(2,1)}, bf16[2048,4224]{1,0:T(8,128)(2,1)}) custom-call(s32[1]{0:T(128)} %bitcast.4.chip.start, bf16[2048,1536]{1,0:T(8,128)(2,1)} %collective-permute-done.h, bf16[2048,1536]{1,0:T(8,128)(2,1)} %collective-permute-done.1.dy.refs_3_, ...), custom_call_target="tpu_custom_call" | custom-call | flops 79725330432 | bytes 90832896 | tf_op jit(solution)/shard_map/last_layer/pallas_call | solution.py:135
  622.8 37.4 %weight_gradient.16 = bf16[2176,1536]{1,0:T(8,128)(2,1)} custom-call(s32[1]{0:T(128)} %constant.84.clone.1.start, bf16[2048,2560]{1,0:T(8,128)(2,1)} %get-tuple-element.77.refs_0_, bf16[2048,1536]{1,0:T(8,128)(2,1)} %bitcast.62, bf16[2048,2560]{1,0:T(8,128)(2,1)} %get-tuple-element.78.refs_2_, bf16[2048,1536]{1,0:T(8,128)(2,1)} %collective-permute-done.1.dy.refs_3_), custom_call_target="tpu_custom_call" | custom-call | flops 27380416512 | bytes 37093376 | tf_op jit(solution)/shard_map/weight_gradient/pallas_call | solution.py:227
  660.2 6.2 constant_dynamic-slice_fusion
  666.4 36.1 %weight_gradient.11.refs_0_ = bf16[768,4224]{1,0:T(8,128)(2,1)} custom-call(s32[1]{0:T(128)} %bitcast.4.chip.start, bf16[2048,1536]{1,0:T(8,128)(2,1)} %get-tuple-element.51.refs_0_, bf16[2048,4224]{1,0:T(8,128)(2,1)} %get-tuple-element.52.dg.refs_1_, bf16[2048,1536]{1,0:T(8,128)(2,1)} %get-tuple-element.59.refs_2_, bf16[2048,4224]{1,0:T(8,128)(2,1)} %get-tuple-element.60.refs_3_), custom_call_target="tpu_custom_call" | custom-call | flops 26575110144 | bytes 47382528 | tf_op jit(solution)/shard_map/weight_gradient/pallas_call | solution.py:227
  702.5 3.5 fusion
  706.4 36.3 %weight_gradient.14.refs_0_ = bf16[768,4224]{1,0:T(8,128)(2,1)} custom-call(s32[1]{0:T(128)} %bitcast.4.chip.start, bf16[2048,1536]{1,0:T(8,128)(2,1)} %get-tuple-element.51.refs_0_, bf16[2048,4224]{1,0:T(8,128)(2,1)} %get-tuple-element.54.du.refs_1_, bf16[2048,1536]{1,0:T(8,128)(2,1)} %get-tuple-element.59.refs_2_, bf16[2048,4224]{1,0:T(8,128)(2,1)} %get-tuple-element.69.refs_3_), custom_call_target="tpu_custom_call" | custom-call | flops 26575110144 | bytes 47382528 | tf_op jit(solution)/shard_map/weight_gradient/pallas_call | solution.py:227
  742.9 3.5 fusion.1
  746.4 1.6 collective-permute-start.17
  748.0 4.1 constant_dynamic-slice_fusion.3
  752.5 1.9 constant_dynamic-slice_fusion.2
  754.8 17.7 %adamw.6 = (bf16[384,4224]{1,0:T(8,128)(2,1)}, bf16[2,1536,4224]{2,1,0:T(8,128)(2,1)}, f32[2,384,4224]{2,1,0:T(8,128)}, f32[2,384,4224]{2,1,0:T(8,128)}) custom-call(s32[3]{0:T(128)} %pad_add_fusion.1.place, bf16[1536,2048]{1,0:T(8,128)(2,1)} %weight_gradient.12.refs_0_, bf16[2,384,2048]{2,1,0:T(8,128)(2,1)} %copy-done.1, ...), custom_call_target="tpu_custom_call" | custom-call | flops 1000000000 | bytes 45416448 | tf_op jit(solution)/shard_map/adamw/pallas_call | solution.py:286
  772.5 17.0 %adamw.11 = (bf16[1056,1536]{1,0:T(8,128)(2,1)}, bf16[2,4224,1536]{2,1,0:T(8,128)(2,1)}, f32[2,1056,1536]{2,1,0:T(8,128)}, f32[2,1056,1536]{2,1,0:T(8,128)}) custom-call(s32[3]{0:T(128)} %pad_add_fusion.1.place, bf16[1056,1536]{1,0:T(8,128)(2,1)} %get-tuple-element.92.refs_0_, ...), custom_call_target="tpu_custom_call", output_to_operand_aliasing={{1}: (6, {}), {2}: (7, {}), {3}: (8, {})} | custom-call | flops 1000000000 | bytes 45416448 | tf_op jit(solution)/shard_map/adamw/pallas_call | solution.py:286
  789.6 3.8 fusion.7
  793.4 1.7 collective-permute-start.31
  795.1 60.5 %collective-permute-done.37.refs_1_ = bf16[1056,1536]{1,0:T(8,128)(2,1)} collective-permute-done((bf16[1056,1536]{1,0:T(8,128)(2,1)}, bf16[1056,1536]{1,0:T(8,128)(2,1)}, u32[]{:S(2)}, u32[]{:S(2)}) %collective-permute-start.37) | collective-permute-done | bytes 3244064 | tf_op jit(solution)/shard_map/ppermute | solution.py:344
  855.6 1.6 collective-permute-start.11
  857.7 17.7 %adamw.8 = (bf16[384,4224]{1,0:T(8,128)(2,1)}, bf16[2,1536,4224]{2,1,0:T(8,128)(2,1)}, f32[2,384,4224]{2,1,0:T(8,128)}, f32[2,384,4224]{2,1,0:T(8,128)}) custom-call(s32[3]{0:T(128)} %pad_add_fusion.1.place, bf16[1536,2048]{1,0:T(8,128)(2,1)} %weight_gradient.15.refs_0_, bf16[1536,2048]{1,0:T(8,128)(2,1)} %collective-permute-done.14.refs_1_, ...), custom_call_target="tpu_custom_call" | custom-call | flops 1000000000 | bytes 45416448 | tf_op jit(solution)/shard_map/adamw/pallas_call | solution.py:286
  875.4 15.0 %collective-permute-done.31.refs_0_ = bf16[528,1536]{1,0:T(8,128)(2,1)} collective-permute-done((bf16[528,1536]{1,0:T(8,128)(2,1)}, bf16[528,1536]{1,0:T(8,128)(2,1)}, u32[]{:S(2)}, u32[]{:S(2)}) %collective-permute-start.31) | collective-permute-done | bytes 1622048 | tf_op jit(solution)/shard_map/ppermute | solution.py:344
  890.4 1.6 collective-permute-start.22
  892.0 16.9 %adamw.7 = (bf16[384,4224]{1,0:T(8,128)(2,1)}, bf16[2,1536,4224]{2,1,0:T(8,128)(2,1)}, f32[2,384,4224]{2,1,0:T(8,128)}, f32[2,384,4224]{2,1,0:T(8,128)}) custom-call(s32[3]{0:T(128)} %pad_add_fusion.1.place, bf16[768,4224]{1,0:T(8,128)(2,1)} %weight_gradient.11.refs_0_, ...), custom_call_target="tpu_custom_call", output_to_operand_aliasing={{1}: (6, {}), {2}: (7, {}), {3}: (8, {})} | custom-call | flops 1000000000 | bytes 45416448 | tf_op jit(solution)/shard_map/adamw/pallas_call | solution.py:286
  908.9 85.8 %collective-permute-done.33.refs_0_ = bf16[528,1536]{1,0:T(8,128)(2,1)} collective-permute-done((bf16[528,1536]{1,0:T(8,128)(2,1)}, bf16[528,1536]{1,0:T(8,128)(2,1)}, u32[]{:S(2)}, u32[]{:S(2)}) %collective-permute-start.33) | collective-permute-done | bytes 1622048 | tf_op jit(solution)/shard_map/ppermute | solution.py:344
  994.7 1.6 collective-permute-start.8
  996.3 16.9 %adamw.9 = (bf16[384,4224]{1,0:T(8,128)(2,1)}, bf16[2,1536,4224]{2,1,0:T(8,128)(2,1)}, f32[2,384,4224]{2,1,0:T(8,128)}, f32[2,384,4224]{2,1,0:T(8,128)}) custom-call(s32[3]{0:T(128)} %pad_add_fusion.1.place, bf16[768,4224]{1,0:T(8,128)(2,1)} %weight_gradient.14.refs_0_, ...), custom_call_target="tpu_custom_call", output_to_operand_aliasing={{1}: (6, {}), {2}: (7, {}), {3}: (8, {})} | custom-call | flops 1000000000 | bytes 45416448 | tf_op jit(solution)/shard_map/adamw/pallas_call | solution.py:286
  1013.6 50.6 %collective-permute-done.22.refs_1_ = bf16[384,4224]{1,0:T(8,128)(2,1)} collective-permute-done((bf16[384,4224]{1,0:T(8,128)(2,1)}, bf16[384,4224]{1,0:T(8,128)(2,1)}, u32[]{:S(2)}, u32[]{:S(2)}) %collective-permute-start.22) | collective-permute-done | bytes 3244064 | tf_op jit(solution)/shard_map/ppermute | solution.py:344
  1064.7 69.0 %collective-permute-done.8.refs_1_ = bf16[384,4224]{1,0:T(8,128)(2,1)} collective-permute-done((bf16[384,4224]{1,0:T(8,128)(2,1)}, bf16[384,4224]{1,0:T(8,128)(2,1)}, u32[]{:S(2)}, u32[]{:S(2)}) %collective-permute-start.8) | collective-permute-done | bytes 3244064 | tf_op jit(solution)/shard_map/ppermute | solution.py:344
  1133.7 68.9 %collective-permute-done.19.refs_1_ = bf16[384,4224]{1,0:T(8,128)(2,1)} collective-permute-done((bf16[384,4224]{1,0:T(8,128)(2,1)}, bf16[384,4224]{1,0:T(8,128)(2,1)}, u32[]{:S(2)}, u32[]{:S(2)}) %collective-permute-start.19) | collective-permute-done | bytes 3244064 | tf_op jit(solution)/shard_map/ppermute | solution.py:344
  1204.2 0.6 pad_add_fusion.at
  1204.8 11.0 place.13.refs_1_
  1215.8 4.5 place.14.refs_2_
  1220.2 6.2 place.15.refs_1_
  1226.4 3.4 place.16.refs_1_
  1229.8 3.4 place.17
  1233.2 11.0 place.9.refs_3_
  1244.2 11.0 place.11.refs_3_
  1255.2 11.0 place.10
  1266.2 11.0 place.12
  (70 shorter events, 6.1 us)
Async XLA Ops:
  103.1 415.9 %collective-permute-start = (bf16[2048,1536]{1,0:T(8,128)(2,1)}, bf16[2048,1536]{1,0:T(8,128)(2,1)}, u32[]{:S(2)}, u32[]{:S(2)}) collective-permute-start(bf16[2048,1536]{1,0:T(8,128)(2,1)} %down.1.h), channel_id=1, source_target_pairs={{0,2},{1,3},{2,0},{3,1},{4,6},{5,7},{6,4},{7,5}} | collective-permute-start | bytes 18874376 | tf_op jit(solution)/shard_map/ppermute | solution.py:344
  106.4 418.4 %collective-permute-start.1 = (bf16[2048,1536]{1,0:T(8,128)(2,1)}, bf16[2048,1536]{1,0:T(8,128)(2,1)}, u32[]{:S(2)}, u32[]{:S(2)}) collective-permute-start(bf16[2048,1536]{1,0:T(8,128)(2,1)} %bitcast.59), channel_id=1, source_target_pairs={{0,2},{1,3},{2,0},{3,1},{4,6},{5,7},{6,4},{7,5}} | collective-permute-start | bytes 18874376 | tf_op jit(solution)/shard_map/ppermute | solution.py:344
  291.5 98.5 %collective-permute-start.25 = (bf16[4224,512]{1,0:T(8,128)(2,1)}, bf16[4224,512]{1,0:T(8,128)(2,1)}, u32[]{:S(2)}, u32[]{:S(2)}) collective-permute-start(bf16[4224,512]{1,0:T(8,128)(2,1)} %weight_gradient.17.refs_0_), channel_id=1, source_target_pairs={{0,1},{1,0},{2,3},{3,2},{4,5},{5,4},{6,7},{7,6}} | collective-permute-start | bytes 12976136 | tf_op jit(solution)/shard_map/ppermute | solution.py:347
  305.5 117.0 %collective-permute-start.27 = (bf16[4224,512]{1,0:T(8,128)(2,1)}, bf16[4224,512]{1,0:T(8,128)(2,1)}, u32[]{:S(2)}, u32[]{:S(2)}) collective-permute-start(bf16[4224,512]{1,0:T(8,128)(2,1)} %weight_gradient.18.refs_3_), channel_id=1, source_target_pairs={{0,1},{1,0},{2,3},{3,2},{4,5},{5,4},{6,7},{7,6}} | collective-permute-start | bytes 12976136 | tf_op jit(solution)/shard_map/ppermute | solution.py:347
  322.0 44.9 %collective-permute-start.29 = (bf16[2,1056,512]{2,1,0:T(8,128)(2,1)S(1)}, bf16[2,1056,512]{2,1,0:T(8,128)(2,1)}, u32[]{:S(2)}, u32[]{:S(2)}) collective-permute-start(bf16[2,1056,512]{2,1,0:T(8,128)(2,1)S(1)} %dynamic-slice_bitcast_fusion.1), channel_id=1, source_target_pairs={{0,1},{1,0},{2,3},{3,2},{4,5},{5,4},{6,7},{7,6}} | collective-permute-start | bytes 6488072 | tf_op jit(solution)/shard_map/ppermute | solution.py:347
  366.9 152.4 %collective-permute-start.14 = (bf16[1536,2048]{1,0:T(8,128)(2,1)}, bf16[1536,2048]{1,0:T(8,128)(2,1)}, u32[]{:S(2)}, u32[]{:S(2)}) collective-permute-start(bf16[1536,2048]{1,0:T(8,128)(2,1)} %weight_gradient.15.refs_0_), channel_id=1, source_target_pairs={{0,1},{1,0},{2,3},{3,2},{4,5},{5,4},{6,7},{7,6}} | collective-permute-start | bytes 18874376 | tf_op jit(solution)/shard_map/ppermute | solution.py:347
  390.0 61.5 %collective-permute-start.3 = (bf16[2,384,2048]{2,1,0:T(8,128)(2,1)}, bf16[2,384,2048]{2,1,0:T(8,128)(2,1)S(1)}, u32[]{:S(2)}, u32[]{:S(2)}) collective-permute-start(bf16[2,384,2048]{2,1,0:T(8,128)(2,1)} %dynamic-slice_bitcast_fusion), channel_id=1, source_target_pairs={{0,1},{1,0},{2,3},{3,2},{4,5},{5,4},{6,7},{7,6}} | collective-permute-start | bytes 9437192 | tf_op jit(solution)/shard_map/ppermute | solution.py:347
  422.5 29.0 %collective-permute-start.30 = (bf16[1056,512]{1,0:T(8,128)(2,1)}, bf16[1056,512]{1,0:T(8,128)(2,1)}, u32[]{:S(2)}, u32[]{:S(2)}) collective-permute-start(bf16[1056,512]{1,0:T(8,128)(2,1)} %fusion.6), channel_id=1, source_target_pairs={{0,2},{1,3},{2,0},{3,1},{4,6},{5,7},{6,4},{7,5}} | collective-permute-start | bytes 3244040 | tf_op jit(solution)/shard_map/ppermute | solution.py:344
  451.5 23.0 %copy-start.1 = (bf16[2,384,2048]{2,1,0:T(8,128)(2,1)}, bf16[2,384,2048]{2,1,0:T(8,128)(2,1)S(1)}, u32[]{:S(2)}) copy-start(bf16[2,384,2048]{2,1,0:T(8,128)(2,1)S(1)} %collective-permute-done.3.refs_1_) | copy-start | bytes 9437188
  451.5 27.0 %collective-permute-start.26 = (bf16[1056,512]{1,0:T(8,128)(2,1)}, bf16[1056,512]{1,0:T(8,128)(2,1)}, u32[]{:S(2)}, u32[]{:S(2)}) collective-permute-start(bf16[1056,512]{1,0:T(8,128)(2,1)} %fusion.4), channel_id=1, source_target_pairs={{0,2},{1,3},{2,0},{3,1},{4,6},{5,7},{6,4},{7,5}} | collective-permute-start | bytes 3244040 | tf_op jit(solution)/shard_map/ppermute | solution.py:344
  451.6 49.4 %collective-permute-start.28 = (bf16[1056,512]{1,0:T(8,128)(2,1)}, bf16[1056,512]{1,0:T(8,128)(2,1)}, u32[]{:S(2)}, u32[]{:S(2)}) collective-permute-start(bf16[1056,512]{1,0:T(8,128)(2,1)} %fusion.5), channel_id=1, source_target_pairs={{0,2},{1,3},{2,0},{3,1},{4,6},{5,7},{6,4},{7,5}} | collective-permute-start | bytes 3244040 | tf_op jit(solution)/shard_map/ppermute | solution.py:344
  478.6 223.9 %collective-permute-start.5 = (bf16[1536,2176]{1,0:T(8,128)(2,1)}, bf16[1536,2176]{1,0:T(8,128)(2,1)}, u32[]{:S(2)}, u32[]{:S(2)}) collective-permute-start(bf16[1536,2176]{1,0:T(8,128)(2,1)} %weight_gradient.13.refs_3_), channel_id=1, source_target_pairs={{0,1},{1,0},{2,3},{3,2},{4,5},{5,4},{6,7},{7,6}} | collective-permute-start | bytes 20054024 | tf_op jit(solution)/shard_map/ppermute | solution.py:347
  501.0 241.7 %collective-permute-start.16 = (bf16[1536,2176]{1,0:T(8,128)(2,1)}, bf16[1536,2176]{1,0:T(8,128)(2,1)}, u32[]{:S(2)}, u32[]{:S(2)}) collective-permute-start(bf16[1536,2176]{1,0:T(8,128)(2,1)} %weight_gradient.10.refs_3_), channel_id=1, source_target_pairs={{0,1},{1,0},{2,3},{3,2},{4,5},{5,4},{6,7},{7,6}} | collective-permute-start | bytes 20054024 | tf_op jit(solution)/shard_map/ppermute | solution.py:347
  519.0 227.4 %collective-permute-start.4 = (bf16[384,2048]{1,0:T(8,128)(2,1)}, bf16[384,2048]{1,0:T(8,128)(2,1)}, u32[]{:S(2)}, u32[]{:S(2)}) collective-permute-start(bf16[384,2048]{1,0:T(8,128)(2,1)} %fusion.2), channel_id=1, source_target_pairs={{0,2},{1,3},{2,0},{3,1},{4,6},{5,7},{6,4},{7,5}} | collective-permute-start | bytes 4718600 | tf_op jit(solution)/shard_map/ppermute | solution.py:344
  523.0 229.1 %collective-permute-start.15 = (bf16[384,2048]{1,0:T(8,128)(2,1)}, bf16[384,2048]{1,0:T(8,128)(2,1)}, u32[]{:S(2)}, u32[]{:S(2)}) collective-permute-start(bf16[384,2048]{1,0:T(8,128)(2,1)} %fusion.3), channel_id=1, source_target_pairs={{0,2},{1,3},{2,0},{3,1},{4,6},{5,7},{6,4},{7,5}} | collective-permute-start | bytes 4718600 | tf_op jit(solution)/shard_map/ppermute | solution.py:344
  666.4 88.0 %collective-permute-start.24 = (bf16[1056,1536]{1,0:T(8,128)(2,1)}, bf16[1056,1536]{1,0:T(8,128)(2,1)}, u32[]{:S(2)}, u32[]{:S(2)}) collective-permute-start(bf16[1056,1536]{1,0:T(8,128)(2,1)} %get-tuple-element.91), channel_id=1, source_target_pairs={{0,1},{1,0},{2,3},{3,2},{4,5},{5,4},{6,7},{7,6}} | collective-permute-start | bytes 9732104 | tf_op jit(solution)/shard_map/ppermute | solution.py:347
  706.0 46.5 %collective-permute-start.6 = (bf16[384,2176]{1,0:T(8,128)(2,1)}, bf16[384,2176]{1,0:T(8,128)(2,1)}, u32[]{:S(2)}, u32[]{:S(2)}) collective-permute-start(bf16[384,2176]{1,0:T(8,128)(2,1)} %fusion), channel_id=1, source_target_pairs={{0,2},{1,3},{2,0},{3,1},{4,6},{5,7},{6,4},{7,5}} | collective-permute-start | bytes 5013512 | tf_op jit(solution)/shard_map/ppermute | solution.py:344
  742.7 50.7 %collective-permute-start.36 = (bf16[1056,1536]{1,0:T(8,128)(2,1)}, bf16[1056,1536]{1,0:T(8,128)(2,1)S(1)}, u32[]{:S(2)}, u32[]{:S(2)}) collective-permute-start(bf16[1056,1536]{1,0:T(8,128)(2,1)} %get-tuple-element.83), channel_id=1, source_target_pairs={{0,1},{1,0},{2,3},{3,2},{4,5},{5,4},{6,7},{7,6}} | collective-permute-start | bytes 9732104 | tf_op jit(solution)/shard_map/ppermute | solution.py:347
  746.4 6.1 copy-start
  746.4 43.1 %collective-permute-start.17 = (bf16[384,2176]{1,0:T(8,128)(2,1)}, bf16[384,2176]{1,0:T(8,128)(2,1)}, u32[]{:S(2)}, u32[]{:S(2)}) collective-permute-start(bf16[384,2176]{1,0:T(8,128)(2,1)} %fusion.1), channel_id=1, source_target_pairs={{0,2},{1,3},{2,0},{3,1},{4,6},{5,7},{6,4},{7,5}} | collective-permute-start | bytes 5013512 | tf_op jit(solution)/shard_map/ppermute | solution.py:344
  752.1 103.5 %collective-permute-start.37 = (bf16[1056,1536]{1,0:T(8,128)(2,1)}, bf16[1056,1536]{1,0:T(8,128)(2,1)}, u32[]{:S(2)}, u32[]{:S(2)}) collective-permute-start(bf16[1056,1536]{1,0:T(8,128)(2,1)} %get-tuple-element.83), channel_id=1, source_target_pairs={{0,2},{1,3},{2,0},{3,1},{4,6},{5,7},{6,4},{7,5}} | collective-permute-start | bytes 9732104 | tf_op jit(solution)/shard_map/ppermute | solution.py:344
  752.5 104.8 %collective-permute-start.2 = (bf16[384,4224]{1,0:T(8,128)(2,1)}, bf16[384,4224]{1,0:T(8,128)(2,1)}, u32[]{:S(2)}, u32[]{:S(2)}) collective-permute-start(bf16[384,4224]{1,0:T(8,128)(2,1)} %constant_dynamic-slice_fusion.3), channel_id=1, source_target_pairs={{0,1},{1,0},{2,3},{3,2},{4,5},{5,4},{6,7},{7,6}} | collective-permute-start | bytes 9732104 | tf_op jit(solution)/shard_map/ppermute | solution.py:347
  754.3 121.0 %collective-permute-start.13 = (bf16[384,4224]{1,0:T(8,128)(2,1)}, bf16[384,4224]{1,0:T(8,128)(2,1)}, u32[]{:S(2)}, u32[]{:S(2)}) collective-permute-start(bf16[384,4224]{1,0:T(8,128)(2,1)} %constant_dynamic-slice_fusion.2), channel_id=1, source_target_pairs={{0,1},{1,0},{2,3},{3,2},{4,5},{5,4},{6,7},{7,6}} | collective-permute-start | bytes 9732104 | tf_op jit(solution)/shard_map/ppermute | solution.py:347
  789.5 205.1 %collective-permute-start.10 = (bf16[384,4224]{1,0:T(8,128)(2,1)}, bf16[384,4224]{1,0:T(8,128)(2,1)}, u32[]{:S(2)}, u32[]{:S(2)}) collective-permute-start(bf16[384,4224]{1,0:T(8,128)(2,1)} %get-tuple-element.67), channel_id=1, source_target_pairs={{0,1},{1,0},{2,3},{3,2},{4,5},{5,4},{6,7},{7,6}} | collective-permute-start | bytes 9732104 | tf_op jit(solution)/shard_map/ppermute | solution.py:347
  793.4 82.0 %copy-start.2 = (bf16[1056,1536]{1,0:T(8,128)(2,1)}, bf16[1056,1536]{1,0:T(8,128)(2,1)S(1)}, u32[]{:S(2)}) copy-start(bf16[1056,1536]{1,0:T(8,128)(2,1)S(1)} %collective-permute-done.36.refs_0_) | copy-start | bytes 9732100
  793.4 97.0 %collective-permute-start.31 = (bf16[528,1536]{1,0:T(8,128)(2,1)}, bf16[528,1536]{1,0:T(8,128)(2,1)}, u32[]{:S(2)}, u32[]{:S(2)}) collective-permute-start(bf16[528,1536]{1,0:T(8,128)(2,1)} %get-tuple-element.94), channel_id=1, source_target_pairs={{0,2},{1,3},{2,0},{3,1},{4,6},{5,7},{6,4},{7,5}} | collective-permute-start | bytes 4866056 | tf_op jit(solution)/shard_map/ppermute | solution.py:344
  855.6 157.5 %collective-permute-start.11 = (bf16[384,4224]{1,0:T(8,128)(2,1)}, bf16[384,4224]{1,0:T(8,128)(2,1)}, u32[]{:S(2)}, u32[]{:S(2)}) collective-permute-start(bf16[384,4224]{1,0:T(8,128)(2,1)} %get-tuple-element.67), channel_id=1, source_target_pairs={{0,2},{1,3},{2,0},{3,1},{4,6},{5,7},{6,4},{7,5}} | collective-permute-start | bytes 9732104 | tf_op jit(solution)/shard_map/ppermute | solution.py:344
  857.2 137.4 %collective-permute-start.33 = (bf16[528,1536]{1,0:T(8,128)(2,1)}, bf16[528,1536]{1,0:T(8,128)(2,1)}, u32[]{:S(2)}, u32[]{:S(2)}) collective-permute-start(bf16[528,1536]{1,0:T(8,128)(2,1)} %get-tuple-element.93), channel_id=1, source_target_pairs={{0,2},{1,3},{2,0},{3,1},{4,6},{5,7},{6,4},{7,5}} | collective-permute-start | bytes 4866056 | tf_op jit(solution)/shard_map/ppermute | solution.py:344
  875.4 138.3 %collective-permute-start.21 = (bf16[384,4224]{1,0:T(8,128)(2,1)}, bf16[384,4224]{1,0:T(8,128)(2,1)S(1)}, u32[]{:S(2)}, u32[]{:S(2)}) collective-permute-start(bf16[384,4224]{1,0:T(8,128)(2,1)} %get-tuple-element.75), channel_id=1, source_target_pairs={{0,1},{1,0},{2,3},{3,2},{4,5},{5,4},{6,7},{7,6}} | collective-permute-start | bytes 9732104 | tf_op jit(solution)/shard_map/ppermute | solution.py:347
  890.4 173.8 %collective-permute-start.22 = (bf16[384,4224]{1,0:T(8,128)(2,1)}, bf16[384,4224]{1,0:T(8,128)(2,1)}, u32[]{:S(2)}, u32[]{:S(2)}) collective-permute-start(bf16[384,4224]{1,0:T(8,128)(2,1)} %get-tuple-element.75), channel_id=1, source_target_pairs={{0,2},{1,3},{2,0},{3,1},{4,6},{5,7},{6,4},{7,5}} | collective-permute-start | bytes 9732104 | tf_op jit(solution)/shard_map/ppermute | solution.py:344
  994.7 69.5 %collective-permute-start.38 = (bf16[1056,1536]{1,0:T(8,128)(2,1)}, bf16[1056,1536]{1,0:T(8,128)(2,1)}, u32[]{:S(2)}, u32[]{:S(2)}) collective-permute-start(bf16[1056,1536]{1,0:T(8,128)(2,1)} %collective-permute-done.37.refs_1_), channel_id=1, source_target_pairs={{0,1},{1,0},{2,3},{3,2},{4,5},{5,4},{6,7},{7,6}} | collective-permute-start | bytes 9732104 | tf_op jit(solution)/shard_map/ppermute | solution.py:347
  994.7 139.0 %collective-permute-start.8 = (bf16[384,4224]{1,0:T(8,128)(2,1)}, bf16[384,4224]{1,0:T(8,128)(2,1)}, u32[]{:S(2)}, u32[]{:S(2)}) collective-permute-start(bf16[384,4224]{1,0:T(8,128)(2,1)} %get-tuple-element.66), channel_id=1, source_target_pairs={{0,2},{1,3},{2,0},{3,1},{4,6},{5,7},{6,4},{7,5}} | collective-permute-start | bytes 9732104 | tf_op jit(solution)/shard_map/ppermute | solution.py:344
  1013.2 189.4 %collective-permute-start.19 = (bf16[384,4224]{1,0:T(8,128)(2,1)}, bf16[384,4224]{1,0:T(8,128)(2,1)}, u32[]{:S(2)}, u32[]{:S(2)}) collective-permute-start(bf16[384,4224]{1,0:T(8,128)(2,1)} %get-tuple-element.74), channel_id=1, source_target_pairs={{0,2},{1,3},{2,0},{3,1},{4,6},{5,7},{6,4},{7,5}} | collective-permute-start | bytes 9732104 | tf_op jit(solution)/shard_map/ppermute | solution.py:344
  1013.6 202.2 %copy-start.3 = (bf16[384,4224]{1,0:T(8,128)(2,1)}, bf16[384,4224]{1,0:T(8,128)(2,1)S(1)}, u32[]{:S(2)}) copy-start(bf16[384,4224]{1,0:T(8,128)(2,1)S(1)} %collective-permute-done.21.refs_0_) | copy-start | bytes 9732100
  1013.6 189.5 %collective-permute-start.35 = (bf16[1056,1536]{1,0:T(8,128)(2,1)}, bf16[1056,1536]{1,0:T(8,128)(2,1)}, u32[]{:S(2)}, u32[]{:S(2)}) collective-permute-start(bf16[1056,1536]{1,0:T(8,128)(2,1)} %get-tuple-element.82), channel_id=1, source_target_pairs={{0,1},{1,0},{2,3},{3,2},{4,5},{5,4},{6,7},{7,6}} | collective-permute-start | bytes 9732104 | tf_op jit(solution)/shard_map/ppermute | solution.py:347
  1064.2 139.4 %collective-permute-start.12 = (bf16[384,4224]{1,0:T(8,128)(2,1)}, bf16[384,4224]{1,0:T(8,128)(2,1)}, u32[]{:S(2)}, u32[]{:S(2)}) collective-permute-start(bf16[384,4224]{1,0:T(8,128)(2,1)} %collective-permute-done.11.refs_1_), channel_id=1, source_target_pairs={{0,1},{1,0},{2,3},{3,2},{4,5},{5,4},{6,7},{7,6}} | collective-permute-start | bytes 9732104 | tf_op jit(solution)/shard_map/ppermute | solution.py:347
  1064.2 138.4 %collective-permute-start.32 = (bf16[528,1536]{1,0:T(8,128)(2,1)}, bf16[528,1536]{1,0:T(8,128)(2,1)}, u32[]{:S(2)}, u32[]{:S(2)}) collective-permute-start(bf16[528,1536]{1,0:T(8,128)(2,1)} %collective-permute-done.31.refs_0_), channel_id=1, source_target_pairs={{0,1},{1,0},{2,3},{3,2},{4,5},{5,4},{6,7},{7,6}} | collective-permute-start | bytes 4866056 | tf_op jit(solution)/shard_map/ppermute | solution.py:347
  1133.7 69.4 %collective-permute-start.34 = (bf16[528,1536]{1,0:T(8,128)(2,1)}, bf16[528,1536]{1,0:T(8,128)(2,1)}, u32[]{:S(2)}, u32[]{:S(2)}) collective-permute-start(bf16[528,1536]{1,0:T(8,128)(2,1)} %collective-permute-done.33.refs_0_), channel_id=1, source_target_pairs={{0,1},{1,0},{2,3},{3,2},{4,5},{5,4},{6,7},{7,6}} | collective-permute-start | bytes 4866056 | tf_op jit(solution)/shard_map/ppermute | solution.py:347
  1202.6 41.7 %collective-permute-start.23 = (bf16[384,4224]{1,0:T(8,128)(2,1)}, bf16[384,4224]{1,0:T(8,128)(2,1)}, u32[]{:S(2)}, u32[]{:S(2)}) collective-permute-start(bf16[384,4224]{1,0:T(8,128)(2,1)} %collective-permute-done.22.refs_1_), channel_id=1, source_target_pairs={{0,1},{1,0},{2,3},{3,2},{4,5},{5,4},{6,7},{7,6}} | collective-permute-start | bytes 9732104 | tf_op jit(solution)/shard_map/ppermute | solution.py:347
  1202.6 52.7 %collective-permute-start.7 = (bf16[384,4224]{1,0:T(8,128)(2,1)}, bf16[384,4224]{1,0:T(8,128)(2,1)}, u32[]{:S(2)}, u32[]{:S(2)}) collective-permute-start(bf16[384,4224]{1,0:T(8,128)(2,1)} %get-tuple-element.66), channel_id=1, source_target_pairs={{0,1},{1,0},{2,3},{3,2},{4,5},{5,4},{6,7},{7,6}} | collective-permute-start | bytes 9732104 | tf_op jit(solution)/shard_map/ppermute | solution.py:347
  1203.1 52.2 %collective-permute-start.9 = (bf16[384,4224]{1,0:T(8,128)(2,1)}, bf16[384,4224]{1,0:T(8,128)(2,1)}, u32[]{:S(2)}, u32[]{:S(2)}) collective-permute-start(bf16[384,4224]{1,0:T(8,128)(2,1)} %collective-permute-done.8.refs_1_), channel_id=1, source_target_pairs={{0,1},{1,0},{2,3},{3,2},{4,5},{5,4},{6,7},{7,6}} | collective-permute-start | bytes 9732104 | tf_op jit(solution)/shard_map/ppermute | solution.py:347
  1203.1 63.1 %collective-permute-start.18 = (bf16[384,4224]{1,0:T(8,128)(2,1)}, bf16[384,4224]{1,0:T(8,128)(2,1)}, u32[]{:S(2)}, u32[]{:S(2)}) collective-permute-start(bf16[384,4224]{1,0:T(8,128)(2,1)} %get-tuple-element.74), channel_id=1, source_target_pairs={{0,1},{1,0},{2,3},{3,2},{4,5},{5,4},{6,7},{7,6}} | collective-permute-start | bytes 9732104 | tf_op jit(solution)/shard_map/ppermute | solution.py:347
  1203.6 62.6 %collective-permute-start.20 = (bf16[384,4224]{1,0:T(8,128)(2,1)}, bf16[384,4224]{1,0:T(8,128)(2,1)}, u32[]{:S(2)}, u32[]{:S(2)}) collective-permute-start(bf16[384,4224]{1,0:T(8,128)(2,1)} %collective-permute-done.19.refs_1_), channel_id=1, source_target_pairs={{0,1},{1,0},{2,3},{3,2},{4,5},{5,4},{6,7},{7,6}} | collective-permute-start | bytes 9732104 | tf_op jit(solution)/shard_map/ppermute | solution.py:347

commit v3 on v2

--- a/solution.py
+++ b/solution.py
@@ -158,26 +158,54 @@
     t, f = d_gate.shape
     d = w_gate.shape[1]
 
-    def body(dg, du, wg, wu, h, dy, out):
-        by_gate = dot(dg[...], wg[...], ((1,), (1,))).astype(BF16)
-        by_up = dot(du[...], wu[...], ((1,), (1,))).astype(BF16)
-        by_a = (by_gate.astype(F32) + by_up.astype(F32)).astype(BF16).astype(F32)
-        wide = h[...].astype(F32)
-        square = jnp.mean(wide**2, -1, keepdims=True) + 1e-6
-        scale = lax.rsqrt(square)
-        by_square = jnp.sum(by_a * wide, -1, keepdims=True) * (-0.5 * scale / square)
-        by_h = (by_a * scale + by_square / d * 2 * wide).astype(BF16)
-        out[...] = (dy[...].astype(F32) + by_h.astype(F32)).astype(BF16)
-
-    return pl.pallas_call(
-        body,
-        grid=(t // bm,),
-        in_specs=[pl.BlockSpec((bm, f), lambda i: (i, 0))] * 2
-        + [once((None, d, f), lambda i: (layer, 0, 0))] * 2
-        + [pl.BlockSpec((bm, d), lambda i: (i, 0))] * 2,
-        out_specs=pl.BlockSpec((bm, d), lambda i: (i, 0)),
+    steps = t // bm
+
+    def body(dg, du, wg, wu, h, dy, out, w_up, by_gate, done):
+        step = pl.program_id(1)
+        at = pl.ds(pl.multiple_of(step * bm, bm), bm)
+        fetch = pltpu.make_async_copy(wu.at[layer], w_up, done)
+
+        @pl.when(pl.program_id(0) == 0)
+        def _():
+            @pl.when(step == 0)
+            def _():
+                fetch.start()
+
+            by_gate[at, :] = dot(dg[...], wg[...], ((1,), (1,))).astype(BF16)
+
+        @pl.when(pl.program_id(0) == 1)
+        def _():
+            @pl.when(step == 0)
+            def _():
+                fetch.wait()
+
+            by_up = dot(du[...], w_up[...], ((1,), (1,))).astype(BF16)
+            by_a = (by_gate[at, :].astype(F32) + by_up.astype(F32)).astype(BF16).astype(F32)
+            wide = h[...].astype(F32)
+            square = jnp.mean(wide**2, -1, keepdims=True) + 1e-6
+            scale = lax.rsqrt(square)
+            by_square = jnp.sum(by_a * wide, -1, keepdims=True) * (-0.5 * scale / square)
+            by_h = (by_a * scale + by_square / d * 2 * wide).astype(BF16)
+            out[...] = (dy[...].astype(F32) + by_h.astype(F32)).astype(BF16)
+
+    def second(p, i):
+        return i * p, 0
+
+    return pl.pallas_call(
+        body,
+        grid=(2, steps),
+        in_specs=[
+            pl.BlockSpec((bm, f), lambda p, i: (i + (steps - 1 - i) * p, 0)),
+            pl.BlockSpec((bm, f), second),
+            once((None, d, f), lambda p, i: (layer, 0, 0)),
+            pl.BlockSpec(memory_space=pl.ANY),
+            pl.BlockSpec((bm, d), second),
+            pl.BlockSpec((bm, d), second),
+        ],
+        out_specs=pl.BlockSpec((bm, d), second),
         out_shape=jax.ShapeDtypeStruct((t, d), BF16),
-        compiler_params=params(1),
+        scratch_shapes=[pltpu.VMEM((d, f), BF16), pltpu.VMEM((t, d), BF16), pltpu.SemaphoreType.DMA],
+        compiler_params=params(2),
         cost_estimate=cost(2, t * d * f, 4 * d * f + 4 * t * f),
         name="into_layer",
     )(d_gate, d_up, w_gate, w_up, h, dy)
@@ -187,21 +215,19 @@
     t, d = dh.shape
 
     def body(dh, wd, gate, up, d_gate, d_up):
-        for block in range(2):
-            columns_at = pl.ds(block * bn, bn)
-            for at in parts(t):
-                da = dot(dh[at, :], wd[columns_at, :], ((1,), (1,))).astype(BF16).astype(F32)
-                silu, slope = silu_parts(gate[block, at, :])
-                d_gate[at, columns_at] = (da * up[block, at, :] * slope).astype(BF16)
-                d_up[at, columns_at] = (da * silu).astype(BF16)
-
-    skip = first // (2 * bn)
-    return pl.pallas_call(
-        body,
-        grid=(pl.cdiv(columns, 2 * bn),),
-        in_specs=[once((t, d), lambda j: (0, 0)), pl.BlockSpec((None, 2 * bn, d), lambda j: (layer, j + skip, 0))]
-        + [pl.BlockSpec((2, t, bn), lambda j: (j + skip, 0, 0))] * 2,
-        out_specs=[pl.BlockSpec((t, 2 * bn), lambda j: (0, j))] * 2,
+        for at in parts(t):
+            da = dot(dh[at, :], wd[...], ((1,), (1,))).astype(BF16).astype(F32)
+            silu, slope = silu_parts(gate[at, :])
+            d_gate[at, :] = (da * up[at, :] * slope).astype(BF16)
+            d_up[at, :] = (da * silu).astype(BF16)
+
+    skip = first // bn
+    return pl.pallas_call(
+        body,
+        grid=(pl.cdiv(columns, bn),),
+        in_specs=[once((t, d), lambda j: (0, 0)), pl.BlockSpec((None, bn, d), lambda j: (layer, j + skip, 0))]
+        + [pl.BlockSpec((None, t, bn), lambda j: (j + skip, 0, 0))] * 2,
+        out_specs=[pl.BlockSpec((t, bn), lambda j: (0, j))] * 2,
         out_shape=[jax.ShapeDtypeStruct((t, columns), BF16)] * 2,
         compiler_params=params(1),
         cost_estimate=cost(1, t * d * columns, 2 * d * columns + 12 * t * columns),
@@ -374,8 +400,8 @@
     for number, name in enumerate("abc"):
         g = weight_gradient([(act0, dh1)], 1408, d // 3, piece=number)
         terms0["d"].append(group_sum(g, name != "c"))
-    cut = f // 2 // BN * BN
-    for name, first, columns, bn in (("a", 0, cut, 512), ("b", cut, f - cut, 768)):
+    cut = 6 * BN
+    for name, first, columns, bn in (("a", 0, cut, 512), ("b", cut, f - cut, BN)):
         d_gate0, d_up0 = to_gates(dh1, w_down, gate0, up0, 0, first, columns)
         g = weight_gradient([(a0, d_gate0)], d, bn)
         terms0["g"].append(group_sum(g, name != "a"))

time: 1290 us -> 1380 us (1.070)
  waiting for transfers between devices: 373 us -> 467 us
    ppermute x16, waiting for transfers between devices: 373 us -> 463 us  [across(): return lax.ppermute(t, 'dp', CROSS)]
  transfers between devices with their start and end apart: 39 -> 39, of which waited for: 8 -> 13; matrix products, arithmetic and copies ran while one was open for 4% -> 4% of each run, Pallas kernels for 56% -> 53%
where the time goes in v3:
time: 1380 us; the launch traced here: 1370 us
  Pallas kernels  835 us (61%)
  waiting for transfers between devices  467 us (34%)
  local copies, waits for them, and re-layouts  25.4 us (2%)
  other arithmetic  22.9 us (2%)
  starting transfers between devices  18.1 us (1%)
    ppermute x16, waiting for transfers between devices, across(): return lax.ppermute(t, 'dp', CROSS)  463 us
    pallas_call x10, Pallas kernels, weight_gradient(): pl.pallas_call(body, grid_spec=pltpu.PrefetchScalarGridSpec(num_scalar_pr...  231 us
    pallas_call x2, Pallas kernels, last_layer(): pl.pallas_call(body, grid_spec=pltpu.PrefetchScalarGridSpec(num_scalar_pr...  196 us
    pallas_call x6, Pallas kernels, adamw(): pl.pallas_call(body, grid_spec=pltpu.PrefetchScalarGridSpec(num_scalar_pr...  104 us
    pallas_call x9, Pallas kernels, place(): pl.pallas_call(body, grid_spec=pltpu.PrefetchScalarGridSpec(num_scalar_pr...  72.4 us
    pallas_call x1, Pallas kernels, into_layer(): pl.pallas_call(body, grid=(2, steps), in_specs=[pl.BlockSpec((bm, f), lam...  70.8 us
    pallas_call x1, Pallas kernels, gates(): pl.pallas_call(body, grid=(n,), in_specs=[once((t, d), lambda j: (0, 0))]...  66.6 us
    pallas_call x2, Pallas kernels, to_gates(): pl.pallas_call(body, grid=(pl.cdiv(columns, bn),), in_specs=[once((t, d),...  57.8 us
  transfers between devices with their start and end apart: 39, of which 13 were waited for; matrix products, arithmetic and copies ran while one was open for 4% of the time, Pallas kernels for 53%

profile of v3, /device:TPU:0, one launch (start us, length us, event | category | flops | bytes accessed | tf_op | source)
XLA Modules:
  0.0 1369.4 jit_solution(9579278803708783224)
XLA Ops:
  0.6 66.6 %gates.1 = (bf16[2048,1536]{1,0:T(8,128)(2,1)}, f32[17,2048,256]{2,1,0:T(8,128)}, f32[17,2048,256]{2,1,0:T(8,128)}, bf16[2048,4224]{1,0:T(8,128)(2,1)}) custom-call(bf16[2048,1536]{1,0:T(8,128)(2,1)} %bitcast.57, bf16[2,1536,4224]{2,1,0:T(8,128)(2,1)} %refs_2_.3, bf16[2,1536,4224]{2,1,0:T(8,128)(2,1)} %refs_2_.4), custom_call_target="tpu_custom_call" | custom-call | flops 53150220288 | bytes 112459776 | tf_op jit(solution)/shard_map/gates/pallas_call | solution.py:72
  67.2 35.9 %down.1.h = bf16[2048,1536]{1,0:T(8,128)(2,1)} custom-call(bf16[2048,4224]{1,0:T(8,128)(2,1)} %get-tuple-element.50.act.refs_0_, bf16[2,4224,1536]{2,1,0:T(8,128)(2,1)} %refs_2_.5, bf16[2048,1536]{1,0:T(8,128)(2,1)} %bitcast.58), custom_call_target="tpu_custom_call" | custom-call | flops 26575110144 | bytes 64880640 | tf_op jit(solution)/shard_map/down/pallas_call | solution.py:95
  103.1 3.3 collective-permute-start
  106.4 98.0 %last_layer.2 = (bf16[2048,1536]{1,0:T(8,128)(2,1)}, bf16[2048,2560]{1,0:T(8,128)(2,1)}, bf16[2048,4224]{1,0:T(8,128)(2,1)}, bf16[2048,4224]{1,0:T(8,128)(2,1)}) custom-call(s32[1]{0:T(128)} %bitcast.4.chip.start, bf16[2048,1536]{1,0:T(8,128)(2,1)} %down.1.h, bf16[2048,1536]{1,0:T(8,128)(2,1)} %bitcast.59, bf16[2,1536,4224]{2,1,0:T(8,128)(2,1)} %refs_2_.3, ...), custom_call_target="tpu_custom_call" | custom-call | flops 79725330432 | bytes 90832896 | tf_op jit(solution)/shard_map/last_layer/pallas_call | solution.py:135
  204.4 70.8 %into_layer.1.dh.refs_1_ = bf16[2048,1536]{1,0:T(8,128)(2,1)} custom-call(bf16[2048,4224]{1,0:T(8,128)(2,1)} %get-tuple-element.52.dg.refs_1_, bf16[2048,4224]{1,0:T(8,128)(2,1)} %get-tuple-element.54.du.refs_1_, bf16[2,1536,4224]{2,1,0:T(8,128)(2,1)} %refs_2_.3, bf16[2,1536,4224]{2,1,0:T(8,128)(2,1)} %refs_2_.4, bf16[2048,1536]{1,0:T(8,128)(2,1)} %down.1.h, ...), custom_call_target="tpu_custom_call" | custom-call | flops 53150220288 | bytes 60555264 | tf_op jit(solution)/shard_map/into_layer/pallas_call | solution.py:194
  275.2 14.1 %weight_gradient.17.refs_0_ = bf16[4224,512]{1,0:T(8,128)(2,1)} custom-call(s32[1]{0:T(128)} %constant.84.clone.1.start, bf16[2048,4224]{1,0:T(8,128)(2,1)} %get-tuple-element.50.act.refs_0_, bf16[2048,1536]{1,0:T(8,128)(2,1)} %into_layer.1.dh.refs_1_), custom_call_target="tpu_custom_call" | custom-call | flops 8858370048 | bytes 23724032 | tf_op jit(solution)/shard_map/weight_gradient/pallas_call | solution.py:253
  289.3 14.2 %weight_gradient.19.refs_6_ = bf16[4224,512]{1,0:T(8,128)(2,1)} custom-call(s32[1]{0:T(128)} %constant.84.clone.1.start, bf16[2048,4224]{1,0:T(8,128)(2,1)} %get-tuple-element.50.act.refs_0_, bf16[2048,1536]{1,0:T(8,128)(2,1)} %into_layer.1.dh.refs_1_), custom_call_target="tpu_custom_call" | custom-call | flops 8858370048 | bytes 23724032 | tf_op jit(solution)/shard_map/weight_gradient/pallas_call | solution.py:253
  303.4 3.3 dynamic-slice_bitcast_fusion.1
  307.2 21.9 %to_gates.3 = (bf16[2048,1536]{1,0:T(8,128)(2,1)}, bf16[2048,1536]{1,0:T(8,128)(2,1)}) custom-call(bf16[2048,1536]{1,0:T(8,128)(2,1)} %into_layer.1.dh.refs_1_, bf16[2,4224,1536]{2,1,0:T(8,128)(2,1)} %refs_2_.5, f32[17,2048,256]{2,1,0:T(8,128)} %get-tuple-element.55.gate, f32[17,2048,256]{2,1,0:T(8,128)} %get-tuple-element.56.up), custom_call_target="tpu_custom_call" | custom-call | flops 9663676416 | bytes 42467328 | tf_op jit(solution)/shard_map/to_gates/pallas_call | solution.py:225
  329.0 15.1 %weight_gradient.15.refs_0_ = bf16[1536,1536]{1,0:T(8,128)(2,1)} custom-call(s32[1]{0:T(128)} %constant.84.clone.1.start, bf16[2048,1536]{1,0:T(8,128)(2,1)} %get-tuple-element.53.refs_0_, bf16[2048,1536]{1,0:T(8,128)(2,1)} %get-tuple-element.70.refs_1_), custom_call_target="tpu_custom_call" | custom-call | flops 9663676416 | bytes 17301504 | tf_op jit(solution)/shard_map/weight_gradient/pallas_call | solution.py:253
  344.1 14.0 %weight_gradient.18.refs_3_ = bf16[4224,512]{1,0:T(8,128)(2,1)} custom-call(s32[1]{0:T(128)} %constant.84.clone.1.start, bf16[2048,4224]{1,0:T(8,128)(2,1)} %get-tuple-element.50.act.refs_0_, bf16[2048,1536]{1,0:T(8,128)(2,1)} %into_layer.1.dh.refs_1_), custom_call_target="tpu_custom_call" | custom-call | flops 8858370048 | bytes 23724032 | tf_op jit(solution)/shard_map/weight_gradient/pallas_call | solution.py:253
  358.7 15.1 %weight_gradient.12.refs_0_ = bf16[1536,1536]{1,0:T(8,128)(2,1)} custom-call(s32[1]{0:T(128)} %constant.84.clone.1.start, bf16[2048,1536]{1,0:T(8,128)(2,1)} %get-tuple-element.53.refs_0_, bf16[2048,1536]{1,0:T(8,128)(2,1)} %get-tuple-element.61.refs_1_), custom_call_target="tpu_custom_call" | custom-call | flops 9663676416 | bytes 17301504 | tf_op jit(solution)/shard_map/weight_gradient/pallas_call | solution.py:253
  373.7 3.2 dynamic-slice_bitcast_fusion
  377.0 35.9 %to_gates.2 = (bf16[2048,2688]{1,0:T(8,128)(2,1)}, bf16[2048,2688]{1,0:T(8,128)(2,1)}) custom-call(bf16[2048,1536]{1,0:T(8,128)(2,1)} %into_layer.1.dh.refs_1_, bf16[2,4224,1536]{2,1,0:T(8,128)(2,1)} %refs_2_.5, f32[17,2048,256]{2,1,0:T(8,128)} %get-tuple-element.55.gate, f32[17,2048,256]{2,1,0:T(8,128)} %get-tuple-element.56.up), custom_call_target="tpu_custom_call" | custom-call | flops 16911433728 | bytes 74317824 | tf_op jit(solution)/shard_map/to_gates/pallas_call | solution.py:225
  412.9 24.7 %weight_gradient.10.refs_3_ = bf16[1536,2688]{1,0:T(8,128)(2,1)} custom-call(s32[1]{0:T(128)} %constant.84.clone.1.start, bf16[2048,1536]{1,0:T(8,128)(2,1)} %get-tuple-element.53.refs_0_, bf16[2048,2688]{1,0:T(8,128)(2,1)} %get-tuple-element.57.refs_1_), custom_call_target="tpu_custom_call" | custom-call | flops 16911433728 | bytes 25559040 | tf_op jit(solution)/shard_map/weight_gradient/pallas_call | solution.py:253
  437.7 1.9 fusion.6
  439.5 2.8 fusion.4
  442.4 1.2 collective-permute-start.30
  443.6 2.9 fusion.5
  447.3 1.2 collective-permute-start.28
  448.5 24.5 %weight_gradient.13.refs_3_ = bf16[1536,2688]{1,0:T(8,128)(2,1)} custom-call(s32[1]{0:T(128)} %constant.84.clone.1.start, bf16[2048,1536]{1,0:T(8,128)(2,1)} %get-tuple-element.53.refs_0_, bf16[2048,2688]{1,0:T(8,128)(2,1)} %get-tuple-element.62.refs_1_), custom_call_target="tpu_custom_call" | custom-call | flops 16911433728 | bytes 25559040 | tf_op jit(solution)/shard_map/weight_gradient/pallas_call | solution.py:253
  473.6 2.6 fusion.2
  476.2 2.9 fusion.3
  479.1 59.7 %collective-permute-done.30.refs_8_ = bf16[1056,512]{1,0:T(8,128)(2,1)} collective-permute-done((bf16[1056,512]{1,0:T(8,128)(2,1)S(1)}, bf16[1056,512]{1,0:T(8,128)(2,1)}, u32[]{:S(2)}, u32[]{:S(2)}) %collective-permute-start.30) | collective-permute-done | bytes 1081376 | tf_op jit(solution)/shard_map/ppermute | solution.py:370
  538.8 23.2 %collective-permute-done.26.refs_2_ = bf16[1056,512]{1,0:T(8,128)(2,1)} collective-permute-done((bf16[1056,512]{1,0:T(8,128)(2,1)}, bf16[1056,512]{1,0:T(8,128)(2,1)}, u32[]{:S(2)}, u32[]{:S(2)}) %collective-permute-start.26) | collective-permute-done | bytes 1081376 | tf_op jit(solution)/shard_map/ppermute | solution.py:370
  562.0 22.2 %collective-permute-done.28.refs_5_ = bf16[1056,512]{1,0:T(8,128)(2,1)} collective-permute-done((bf16[1056,512]{1,0:T(8,128)(2,1)}, bf16[1056,512]{1,0:T(8,128)(2,1)}, u32[]{:S(2)}, u32[]{:S(2)}) %collective-permute-start.28) | collective-permute-done | bytes 1081376 | tf_op jit(solution)/shard_map/ppermute | solution.py:370
  584.5 17.9 %adamw.10 = (bf16[1056,1536]{1,0:T(8,128)(2,1)}, bf16[2,4224,1536]{2,1,0:T(8,128)(2,1)}, f32[2,1056,1536]{2,1,0:T(8,128)}, f32[2,1056,1536]{2,1,0:T(8,128)}) custom-call(s32[3]{0:T(128)} %pad_add_fusion.1.place, bf16[4224,512]{1,0:T(8,128)(2,1)} %weight_gradient.17.refs_0_, bf16[4224,512]{1,0:T(8,128)(2,1)} %collective-permute-done.25.refs_1_, ...), custom_call_target="tpu_custom_call" | custom-call | flops 1000000000 | bytes 45416448 | tf_op jit(solution)/shard_map/adamw/pallas_call | solution.py:312
  602.5 1.8 collective-permute-start.15
  604.2 98.1 %last_layer.3 = (bf16[2048,1536]{1,0:T(8,128)(2,1)}, bf16[2048,2560]{1,0:T(8,128)(2,1)}, bf16[2048,4224]{1,0:T(8,128)(2,1)}, bf16[2048,4224]{1,0:T(8,128)(2,1)}) custom-call(s32[1]{0:T(128)} %bitcast.4.chip.start, bf16[2048,1536]{1,0:T(8,128)(2,1)} %collective-permute-done.h, bf16[2048,1536]{1,0:T(8,128)(2,1)} %collective-permute-done.1.dy.refs_3_, ...), custom_call_target="tpu_custom_call" | custom-call | flops 79725330432 | bytes 90832896 | tf_op jit(solution)/shard_map/last_layer/pallas_call | solution.py:135
  702.3 36.3 %weight_gradient.11.refs_0_ = bf16[768,4224]{1,0:T(8,128)(2,1)} custom-call(s32[1]{0:T(128)} %bitcast.4.chip.start, bf16[2048,1536]{1,0:T(8,128)(2,1)} %get-tuple-element.51.refs_0_, bf16[2048,4224]{1,0:T(8,128)(2,1)} %get-tuple-element.52.dg.refs_1_, bf16[2048,1536]{1,0:T(8,128)(2,1)} %get-tuple-element.59.refs_2_, bf16[2048,4224]{1,0:T(8,128)(2,1)} %get-tuple-element.60.refs_3_), custom_call_target="tpu_custom_call" | custom-call | flops 26575110144 | bytes 47382528 | tf_op jit(solution)/shard_map/weight_gradient/pallas_call | solution.py:253
  738.6 37.2 %weight_gradient.16 = bf16[2176,1536]{1,0:T(8,128)(2,1)} custom-call(s32[1]{0:T(128)} %constant.84.clone.1.start, bf16[2048,2560]{1,0:T(8,128)(2,1)} %get-tuple-element.77.refs_0_, bf16[2048,1536]{1,0:T(8,128)(2,1)} %bitcast.62, bf16[2048,2560]{1,0:T(8,128)(2,1)} %get-tuple-element.78.refs_2_, bf16[2048,1536]{1,0:T(8,128)(2,1)} %collective-permute-done.1.dy.refs_3_), custom_call_target="tpu_custom_call" | custom-call | flops 27380416512 | bytes 37093376 | tf_op jit(solution)/shard_map/weight_gradient/pallas_call | solution.py:253
  775.8 3.8 constant_dynamic-slice_fusion.3
  779.6 6.2 constant_dynamic-slice_fusion
  786.8 36.3 %weight_gradient.14.refs_0_ = bf16[768,4224]{1,0:T(8,128)(2,1)} custom-call(s32[1]{0:T(128)} %bitcast.4.chip.start, bf16[2048,1536]{1,0:T(8,128)(2,1)} %get-tuple-element.51.refs_0_, bf16[2048,4224]{1,0:T(8,128)(2,1)} %get-tuple-element.54.du.refs_1_, bf16[2048,1536]{1,0:T(8,128)(2,1)} %get-tuple-element.59.refs_2_, bf16[2048,4224]{1,0:T(8,128)(2,1)} %get-tuple-element.69.refs_3_), custom_call_target="tpu_custom_call" | custom-call | flops 26575110144 | bytes 47382528 | tf_op jit(solution)/shard_map/weight_gradient/pallas_call | solution.py:253
  823.1 3.8 constant_dynamic-slice_fusion.2
  827.1 4.0 fusion
  831.1 4.0 fusion.1
  835.1 1.6 collective-permute-start.6
  836.7 17.0 %adamw.11 = (bf16[1056,1536]{1,0:T(8,128)(2,1)}, bf16[2,4224,1536]{2,1,0:T(8,128)(2,1)}, f32[2,1056,1536]{2,1,0:T(8,128)}, f32[2,1056,1536]{2,1,0:T(8,128)}) custom-call(s32[3]{0:T(128)} %pad_add_fusion.1.place, bf16[1056,1536]{1,0:T(8,128)(2,1)} %get-tuple-element.92.refs_0_, ...), custom_call_target="tpu_custom_call", output_to_operand_aliasing={{1}: (6, {}), {2}: (7, {}), {3}: (8, {})} | custom-call | flops 1000000000 | bytes 45416448 | tf_op jit(solution)/shard_map/adamw/pallas_call | solution.py:312
  854.1 5.0 collective-permute-done.37.refs_1_
  859.1 5.0 fusion.7
  864.6 38.9 %collective-permute-done.6.refs_5_ = bf16[384,2688]{1,0:T(8,128)(2,1)} collective-permute-done((bf16[384,2688]{1,0:T(8,128)(2,1)}, bf16[384,2688]{1,0:T(8,128)(2,1)}, u32[]{:S(2)}, u32[]{:S(2)}) %collective-permute-start.6) | collective-permute-done | bytes 2064416 | tf_op jit(solution)/shard_map/ppermute | solution.py:370
  903.9 17.7 %adamw.6 = (bf16[384,4224]{1,0:T(8,128)(2,1)}, bf16[2,1536,4224]{2,1,0:T(8,128)(2,1)}, f32[2,384,4224]{2,1,0:T(8,128)}, f32[2,384,4224]{2,1,0:T(8,128)}) custom-call(s32[3]{0:T(128)} %pad_add_fusion.1.place, bf16[1536,1536]{1,0:T(8,128)(2,1)} %weight_gradient.12.refs_0_, bf16[2,384,1536]{2,1,0:T(8,128)(2,1)} %copy-done, ...), custom_call_target="tpu_custom_call" | custom-call | flops 1000000000 | bytes 45416448 | tf_op jit(solution)/shard_map/adamw/pallas_call | solution.py:312
  921.6 16.9 %adamw.7 = (bf16[384,4224]{1,0:T(8,128)(2,1)}, bf16[2,1536,4224]{2,1,0:T(8,128)(2,1)}, f32[2,384,4224]{2,1,0:T(8,128)}, f32[2,384,4224]{2,1,0:T(8,128)}) custom-call(s32[3]{0:T(128)} %pad_add_fusion.1.place, bf16[768,4224]{1,0:T(8,128)(2,1)} %weight_gradient.11.refs_0_, ...), custom_call_target="tpu_custom_call", output_to_operand_aliasing={{1}: (6, {}), {2}: (7, {}), {3}: (8, {})} | custom-call | flops 1000000000 | bytes 45416448 | tf_op jit(solution)/shard_map/adamw/pallas_call | solution.py:312
  938.5 9.2 collective-permute-done.17.refs_5_
  947.7 34.8 %collective-permute-done.31.refs_0_ = bf16[528,1536]{1,0:T(8,128)(2,1)} collective-permute-done((bf16[528,1536]{1,0:T(8,128)(2,1)}, bf16[528,1536]{1,0:T(8,128)(2,1)}, u32[]{:S(2)}, u32[]{:S(2)}) %collective-permute-start.31) | collective-permute-done | bytes 1622048 | tf_op jit(solution)/shard_map/ppermute | solution.py:370
  982.9 34.3 %collective-permute-done.33.refs_0_ = bf16[528,1536]{1,0:T(8,128)(2,1)} collective-permute-done((bf16[528,1536]{1,0:T(8,128)(2,1)}, bf16[528,1536]{1,0:T(8,128)(2,1)}, u32[]{:S(2)}, u32[]{:S(2)}) %collective-permute-start.33) | collective-permute-done | bytes 1622048 | tf_op jit(solution)/shard_map/ppermute | solution.py:370
  1017.7 3.3 collective-permute-done.32.refs_0_
  1021.5 17.7 %adamw.8 = (bf16[384,4224]{1,0:T(8,128)(2,1)}, bf16[2,1536,4224]{2,1,0:T(8,128)(2,1)}, f32[2,384,4224]{2,1,0:T(8,128)}, f32[2,384,4224]{2,1,0:T(8,128)}) custom-call(s32[3]{0:T(128)} %pad_add_fusion.1.place, bf16[1536,1536]{1,0:T(8,128)(2,1)} %weight_gradient.15.refs_0_, bf16[1536,1536]{1,0:T(8,128)(2,1)} %collective-permute-done.14.refs_1_, ...), custom_call_target="tpu_custom_call" | custom-call | flops 1000000000 | bytes 45416448 | tf_op jit(solution)/shard_map/adamw/pallas_call | solution.py:312
  1039.2 1.6 collective-permute-start.22
  1040.9 16.9 %adamw.9 = (bf16[384,4224]{1,0:T(8,128)(2,1)}, bf16[2,1536,4224]{2,1,0:T(8,128)(2,1)}, f32[2,384,4224]{2,1,0:T(8,128)}, f32[2,384,4224]{2,1,0:T(8,128)}) custom-call(s32[3]{0:T(128)} %pad_add_fusion.1.place, bf16[768,4224]{1,0:T(8,128)(2,1)} %weight_gradient.14.refs_0_, ...), custom_call_target="tpu_custom_call", output_to_operand_aliasing={{1}: (6, {}), {2}: (7, {}), {3}: (8, {})} | custom-call | flops 1000000000 | bytes 45416448 | tf_op jit(solution)/shard_map/adamw/pallas_call | solution.py:312
  1058.2 28.5 %collective-permute-done.11.refs_1_ = bf16[384,4224]{1,0:T(8,128)(2,1)} collective-permute-done((bf16[384,4224]{1,0:T(8,128)(2,1)}, bf16[384,4224]{1,0:T(8,128)(2,1)}, u32[]{:S(2)}, u32[]{:S(2)}) %collective-permute-start.11) | collective-permute-done | bytes 3244064 | tf_op jit(solution)/shard_map/ppermute | solution.py:370
  1086.8 69.4 %collective-permute-done.8.refs_1_ = bf16[384,4224]{1,0:T(8,128)(2,1)S(1)} collective-permute-done((bf16[384,4224]{1,0:T(8,128)(2,1)}, bf16[384,4224]{1,0:T(8,128)(2,1)S(1)}, u32[]{:S(2)}, u32[]{:S(2)}) %collective-permute-start.8) | collective-permute-done | bytes 3244064 | tf_op jit(solution)/shard_map/ppermute | solution.py:370
  1156.7 69.1 %collective-permute-done.22.refs_1_ = bf16[384,4224]{1,0:T(8,128)(2,1)} collective-permute-done((bf16[384,4224]{1,0:T(8,128)(2,1)}, bf16[384,4224]{1,0:T(8,128)(2,1)}, u32[]{:S(2)}, u32[]{:S(2)}) %collective-permute-start.22) | collective-permute-done | bytes 3244064 | tf_op jit(solution)/shard_map/ppermute | solution.py:370
  1225.8 69.0 %collective-permute-done.19.refs_1_ = bf16[384,4224]{1,0:T(8,128)(2,1)} collective-permute-done((bf16[384,4224]{1,0:T(8,128)(2,1)}, bf16[384,4224]{1,0:T(8,128)(2,1)}, u32[]{:S(2)}, u32[]{:S(2)}) %collective-permute-start.19) | collective-permute-done | bytes 3244064 | tf_op jit(solution)/shard_map/ppermute | solution.py:370
  1296.5 11.0 place.13.refs_1_
  1307.5 4.5 place.14.refs_2_
  1311.9 6.2 place.15.refs_1_
  1318.1 3.4 place.16.refs_1_
  1321.5 3.4 place.17
  1324.9 11.0 place.9.refs_3_
  1335.9 11.0 place.10
  1346.9 11.0 place.11.refs_3_
  1357.9 11.0 place.12
  (70 shorter events, 9.3 us)
Async XLA Ops:
  103.1 499.4 %collective-permute-start = (bf16[2048,1536]{1,0:T(8,128)(2,1)}, bf16[2048,1536]{1,0:T(8,128)(2,1)}, u32[]{:S(2)}, u32[]{:S(2)}) collective-permute-start(bf16[2048,1536]{1,0:T(8,128)(2,1)} %down.1.h), channel_id=1, source_target_pairs={{0,2},{1,3},{2,0},{3,1},{4,6},{5,7},{6,4},{7,5}} | collective-permute-start | bytes 18874376 | tf_op jit(solution)/shard_map/ppermute | solution.py:370
  289.3 123.6 %collective-permute-start.25 = (bf16[4224,512]{1,0:T(8,128)(2,1)}, bf16[4224,512]{1,0:T(8,128)(2,1)}, u32[]{:S(2)}, u32[]{:S(2)}) collective-permute-start(bf16[4224,512]{1,0:T(8,128)(2,1)} %weight_gradient.17.refs_0_), channel_id=1, source_target_pairs={{0,1},{1,0},{2,3},{3,2},{4,5},{5,4},{6,7},{7,6}} | collective-permute-start | bytes 12976136 | tf_op jit(solution)/shard_map/ppermute | solution.py:373
  306.7 70.3 %collective-permute-start.29 = (bf16[2,1056,512]{2,1,0:T(8,128)(2,1)}, bf16[2,1056,512]{2,1,0:T(8,128)(2,1)S(1)}, u32[]{:S(2)}, u32[]{:S(2)}) collective-permute-start(bf16[2,1056,512]{2,1,0:T(8,128)(2,1)} %dynamic-slice_bitcast_fusion.1), channel_id=1, source_target_pairs={{0,1},{1,0},{2,3},{3,2},{4,5},{5,4},{6,7},{7,6}} | collective-permute-start | bytes 6488072 | tf_op jit(solution)/shard_map/ppermute | solution.py:373
  344.1 103.1 %collective-permute-start.14 = (bf16[1536,1536]{1,0:T(8,128)(2,1)}, bf16[1536,1536]{1,0:T(8,128)(2,1)}, u32[]{:S(2)}, u32[]{:S(2)}) collective-permute-start(bf16[1536,1536]{1,0:T(8,128)(2,1)} %weight_gradient.15.refs_0_), channel_id=1, source_target_pairs={{0,1},{1,0},{2,3},{3,2},{4,5},{5,4},{6,7},{7,6}} | collective-permute-start | bytes 14155784 | tf_op jit(solution)/shard_map/ppermute | solution.py:373
  358.2 84.2 %collective-permute-start.27 = (bf16[4224,512]{1,0:T(8,128)(2,1)}, bf16[4224,512]{1,0:T(8,128)(2,1)}, u32[]{:S(2)}, u32[]{:S(2)}) collective-permute-start(bf16[4224,512]{1,0:T(8,128)(2,1)} %weight_gradient.18.refs_3_), channel_id=1, source_target_pairs={{0,1},{1,0},{2,3},{3,2},{4,5},{5,4},{6,7},{7,6}} | collective-permute-start | bytes 12976136 | tf_op jit(solution)/shard_map/ppermute | solution.py:373
  377.0 35.9 %copy-start.1 = (bf16[2,1056,512]{2,1,0:T(8,128)(2,1)}, bf16[2,1056,512]{2,1,0:T(8,128)(2,1)S(1)}, u32[]{:S(2)}) copy-start(bf16[2,1056,512]{2,1,0:T(8,128)(2,1)S(1)} %collective-permute-done.29.refs_7_) | copy-start | bytes 6488068
  377.0 227.3 %collective-permute-start.1 = (bf16[2048,1536]{1,0:T(8,128)(2,1)}, bf16[2048,1536]{1,0:T(8,128)(2,1)}, u32[]{:S(2)}, u32[]{:S(2)}) collective-permute-start(bf16[2048,1536]{1,0:T(8,128)(2,1)} %bitcast.61), channel_id=1, source_target_pairs={{0,2},{1,3},{2,0},{3,1},{4,6},{5,7},{6,4},{7,5}} | collective-permute-start | bytes 18874376 | tf_op jit(solution)/shard_map/ppermute | solution.py:370
  412.9 33.6 %collective-permute-start.3 = (bf16[2,384,1536]{2,1,0:T(8,128)(2,1)}, bf16[2,384,1536]{2,1,0:T(8,128)(2,1)S(1)}, u32[]{:S(2)}, u32[]{:S(2)}) collective-permute-start(bf16[2,384,1536]{2,1,0:T(8,128)(2,1)} %dynamic-slice_bitcast_fusion), channel_id=1, source_target_pairs={{0,1},{1,0},{2,3},{3,2},{4,5},{5,4},{6,7},{7,6}} | collective-permute-start | bytes 7077896 | tf_op jit(solution)/shard_map/ppermute | solution.py:373
  442.4 96.5 %collective-permute-start.30 = (bf16[1056,512]{1,0:T(8,128)(2,1)S(1)}, bf16[1056,512]{1,0:T(8,128)(2,1)}, u32[]{:S(2)}, u32[]{:S(2)}) collective-permute-start(bf16[1056,512]{1,0:T(8,128)(2,1)S(1)} %fusion.6), channel_id=1, source_target_pairs={{0,2},{1,3},{2,0},{3,1},{4,6},{5,7},{6,4},{7,5}} | collective-permute-start | bytes 3244040 | tf_op jit(solution)/shard_map/ppermute | solution.py:370
  446.4 27.2 %copy-start = (bf16[2,384,1536]{2,1,0:T(8,128)(2,1)}, bf16[2,384,1536]{2,1,0:T(8,128)(2,1)S(1)}, u32[]{:S(2)}) copy-start(bf16[2,384,1536]{2,1,0:T(8,128)(2,1)S(1)} %collective-permute-done.3.refs_1_) | copy-start | bytes 7077892
  446.4 115.6 %collective-permute-start.26 = (bf16[1056,512]{1,0:T(8,128)(2,1)}, bf16[1056,512]{1,0:T(8,128)(2,1)}, u32[]{:S(2)}, u32[]{:S(2)}) collective-permute-start(bf16[1056,512]{1,0:T(8,128)(2,1)} %fusion.4), channel_id=1, source_target_pairs={{0,2},{1,3},{2,0},{3,1},{4,6},{5,7},{6,4},{7,5}} | collective-permute-start | bytes 3244040 | tf_op jit(solution)/shard_map/ppermute | solution.py:370
  447.3 137.0 %collective-permute-start.28 = (bf16[1056,512]{1,0:T(8,128)(2,1)}, bf16[1056,512]{1,0:T(8,128)(2,1)}, u32[]{:S(2)}, u32[]{:S(2)}) collective-permute-start(bf16[1056,512]{1,0:T(8,128)(2,1)} %fusion.5), channel_id=1, source_target_pairs={{0,2},{1,3},{2,0},{3,1},{4,6},{5,7},{6,4},{7,5}} | collective-permute-start | bytes 3244040 | tf_op jit(solution)/shard_map/ppermute | solution.py:370
  538.8 247.6 %collective-permute-start.5 = (bf16[1536,2688]{1,0:T(8,128)(2,1)}, bf16[1536,2688]{1,0:T(8,128)(2,1)}, u32[]{:S(2)}, u32[]{:S(2)}) collective-permute-start(bf16[1536,2688]{1,0:T(8,128)(2,1)} %weight_gradient.13.refs_3_), channel_id=1, source_target_pairs={{0,1},{1,0},{2,3},{3,2},{4,5},{5,4},{6,7},{7,6}} | collective-permute-start | bytes 24772616 | tf_op jit(solution)/shard_map/ppermute | solution.py:373
  562.0 264.9 %collective-permute-start.16 = (bf16[1536,2688]{1,0:T(8,128)(2,1)}, bf16[1536,2688]{1,0:T(8,128)(2,1)}, u32[]{:S(2)}, u32[]{:S(2)}) collective-permute-start(bf16[1536,2688]{1,0:T(8,128)(2,1)} %weight_gradient.10.refs_3_), channel_id=1, source_target_pairs={{0,1},{1,0},{2,3},{3,2},{4,5},{5,4},{6,7},{7,6}} | collective-permute-start | bytes 24772616 | tf_op jit(solution)/shard_map/ppermute | solution.py:373
  584.2 201.6 %collective-permute-start.4 = (bf16[384,1536]{1,0:T(8,128)(2,1)}, bf16[384,1536]{1,0:T(8,128)(2,1)}, u32[]{:S(2)}, u32[]{:S(2)}) collective-permute-start(bf16[384,1536]{1,0:T(8,128)(2,1)} %fusion.2), channel_id=1, source_target_pairs={{0,2},{1,3},{2,0},{3,1},{4,6},{5,7},{6,4},{7,5}} | collective-permute-start | bytes 3538952 | tf_op jit(solution)/shard_map/ppermute | solution.py:370
  602.5 183.8 %collective-permute-start.15 = (bf16[384,1536]{1,0:T(8,128)(2,1)}, bf16[384,1536]{1,0:T(8,128)(2,1)}, u32[]{:S(2)}, u32[]{:S(2)}) collective-permute-start(bf16[384,1536]{1,0:T(8,128)(2,1)} %fusion.3), channel_id=1, source_target_pairs={{0,2},{1,3},{2,0},{3,1},{4,6},{5,7},{6,4},{7,5}} | collective-permute-start | bytes 3538952 | tf_op jit(solution)/shard_map/ppermute | solution.py:370
  604.2 249.5 %collective-permute-start.36 = (bf16[1056,1536]{1,0:T(8,128)(2,1)}, bf16[1056,1536]{1,0:T(8,128)(2,1)}, u32[]{:S(2)}, u32[]{:S(2)}) collective-permute-start(bf16[1056,1536]{1,0:T(8,128)(2,1)} %get-tuple-element.83), channel_id=1, source_target_pairs={{0,1},{1,0},{2,3},{3,2},{4,5},{5,4},{6,7},{7,6}} | collective-permute-start | bytes 9732104 | tf_op jit(solution)/shard_map/ppermute | solution.py:373
  785.8 73.3 %collective-permute-start.37 = (bf16[1056,1536]{1,0:T(8,128)(2,1)}, bf16[1056,1536]{1,0:T(8,128)(2,1)S(1)}, u32[]{:S(2)}, u32[]{:S(2)}) collective-permute-start(bf16[1056,1536]{1,0:T(8,128)(2,1)} %get-tuple-element.83), channel_id=1, source_target_pairs={{0,2},{1,3},{2,0},{3,1},{4,6},{5,7},{6,4},{7,5}} | collective-permute-start | bytes 9732104 | tf_op jit(solution)/shard_map/ppermute | solution.py:370
  786.2 77.9 %collective-permute-start.2 = (bf16[384,4224]{1,0:T(8,128)(2,1)}, bf16[384,4224]{1,0:T(8,128)(2,1)}, u32[]{:S(2)}, u32[]{:S(2)}) collective-permute-start(bf16[384,4224]{1,0:T(8,128)(2,1)} %constant_dynamic-slice_fusion.3), channel_id=1, source_target_pairs={{0,1},{1,0},{2,3},{3,2},{4,5},{5,4},{6,7},{7,6}} | collective-permute-start | bytes 9732104 | tf_op jit(solution)/shard_map/ppermute | solution.py:373
  786.4 48.7 %collective-permute-start.24 = (bf16[1056,1536]{1,0:T(8,128)(2,1)}, bf16[1056,1536]{1,0:T(8,128)(2,1)}, u32[]{:S(2)}, u32[]{:S(2)}) collective-permute-start(bf16[1056,1536]{1,0:T(8,128)(2,1)} %get-tuple-element.91), channel_id=1, source_target_pairs={{0,1},{1,0},{2,3},{3,2},{4,5},{5,4},{6,7},{7,6}} | collective-permute-start | bytes 9732104 | tf_op jit(solution)/shard_map/ppermute | solution.py:373
  826.9 94.7 %collective-permute-start.13 = (bf16[384,4224]{1,0:T(8,128)(2,1)}, bf16[384,4224]{1,0:T(8,128)(2,1)}, u32[]{:S(2)}, u32[]{:S(2)}) collective-permute-start(bf16[384,4224]{1,0:T(8,128)(2,1)} %constant_dynamic-slice_fusion.2), channel_id=1, source_target_pairs={{0,1},{1,0},{2,3},{3,2},{4,5},{5,4},{6,7},{7,6}} | collective-permute-start | bytes 9732104 | tf_op jit(solution)/shard_map/ppermute | solution.py:373
  835.1 68.4 %collective-permute-start.6 = (bf16[384,2688]{1,0:T(8,128)(2,1)}, bf16[384,2688]{1,0:T(8,128)(2,1)}, u32[]{:S(2)}, u32[]{:S(2)}) collective-permute-start(bf16[384,2688]{1,0:T(8,128)(2,1)} %fusion), channel_id=1, source_target_pairs={{0,2},{1,3},{2,0},{3,1},{4,6},{5,7},{6,4},{7,5}} | collective-permute-start | bytes 6193160 | tf_op jit(solution)/shard_map/ppermute | solution.py:370
  853.7 94.0 %collective-permute-start.17 = (bf16[384,2688]{1,0:T(8,128)(2,1)}, bf16[384,2688]{1,0:T(8,128)(2,1)}, u32[]{:S(2)}, u32[]{:S(2)}) collective-permute-start(bf16[384,2688]{1,0:T(8,128)(2,1)} %fusion.1), channel_id=1, source_target_pairs={{0,2},{1,3},{2,0},{3,1},{4,6},{5,7},{6,4},{7,5}} | collective-permute-start | bytes 6193160 | tf_op jit(solution)/shard_map/ppermute | solution.py:370
  859.1 5.0 copy-start.2
  859.1 158.1 %collective-permute-start.38 = (bf16[1056,1536]{1,0:T(8,128)(2,1)S(1)}, bf16[1056,1536]{1,0:T(8,128)(2,1)}, u32[]{:S(2)}, u32[]{:S(2)}) collective-permute-start(bf16[1056,1536]{1,0:T(8,128)(2,1)S(1)} %collective-permute-done.37.refs_1_), channel_id=1, source_target_pairs={{0,1},{1,0},{2,3},{3,2},{4,5},{5,4},{6,7},{7,6}} | collective-permute-start | bytes 9732104 | tf_op jit(solution)/shard_map/ppermute | solution.py:373
  864.2 118.3 %collective-permute-start.31 = (bf16[528,1536]{1,0:T(8,128)(2,1)}, bf16[528,1536]{1,0:T(8,128)(2,1)}, u32[]{:S(2)}, u32[]{:S(2)}) collective-permute-start(bf16[528,1536]{1,0:T(8,128)(2,1)} %get-tuple-element.94), channel_id=1, source_target_pairs={{0,2},{1,3},{2,0},{3,1},{4,6},{5,7},{6,4},{7,5}} | collective-permute-start | bytes 4866056 | tf_op jit(solution)/shard_map/ppermute | solution.py:370
  903.5 113.8 %collective-permute-start.33 = (bf16[528,1536]{1,0:T(8,128)(2,1)}, bf16[528,1536]{1,0:T(8,128)(2,1)}, u32[]{:S(2)}, u32[]{:S(2)}) collective-permute-start(bf16[528,1536]{1,0:T(8,128)(2,1)} %get-tuple-element.93), channel_id=1, source_target_pairs={{0,2},{1,3},{2,0},{3,1},{4,6},{5,7},{6,4},{7,5}} | collective-permute-start | bytes 4866056 | tf_op jit(solution)/shard_map/ppermute | solution.py:370
  921.6 117.6 %collective-permute-start.35 = (bf16[1056,1536]{1,0:T(8,128)(2,1)}, bf16[1056,1536]{1,0:T(8,128)(2,1)}, u32[]{:S(2)}, u32[]{:S(2)}) collective-permute-start(bf16[1056,1536]{1,0:T(8,128)(2,1)} %get-tuple-element.82), channel_id=1, source_target_pairs={{0,1},{1,0},{2,3},{3,2},{4,5},{5,4},{6,7},{7,6}} | collective-permute-start | bytes 9732104 | tf_op jit(solution)/shard_map/ppermute | solution.py:373
  947.7 110.1 %collective-permute-start.7 = (bf16[384,4224]{1,0:T(8,128)(2,1)}, bf16[384,4224]{1,0:T(8,128)(2,1)}, u32[]{:S(2)}, u32[]{:S(2)}) collective-permute-start(bf16[384,4224]{1,0:T(8,128)(2,1)} %get-tuple-element.66), channel_id=1, source_target_pairs={{0,1},{1,0},{2,3},{3,2},{4,5},{5,4},{6,7},{7,6}} | collective-permute-start | bytes 9732104 | tf_op jit(solution)/shard_map/ppermute | solution.py:373
  982.5 104.3 %collective-permute-start.11 = (bf16[384,4224]{1,0:T(8,128)(2,1)}, bf16[384,4224]{1,0:T(8,128)(2,1)}, u32[]{:S(2)}, u32[]{:S(2)}) collective-permute-start(bf16[384,4224]{1,0:T(8,128)(2,1)} %get-tuple-element.67), channel_id=1, source_target_pairs={{0,2},{1,3},{2,0},{3,1},{4,6},{5,7},{6,4},{7,5}} | collective-permute-start | bytes 9732104 | tf_op jit(solution)/shard_map/ppermute | solution.py:370
  1017.2 3.8 collective-permute-start.32
  1017.2 22.0 %collective-permute-start.34 = (bf16[528,1536]{1,0:T(8,128)(2,1)}, bf16[528,1536]{1,0:T(8,128)(2,1)}, u32[]{:S(2)}, u32[]{:S(2)}) collective-permute-start(bf16[528,1536]{1,0:T(8,128)(2,1)} %collective-permute-done.33.refs_0_), channel_id=1, source_target_pairs={{0,1},{1,0},{2,3},{3,2},{4,5},{5,4},{6,7},{7,6}} | collective-permute-start | bytes 4866056 | tf_op jit(solution)/shard_map/ppermute | solution.py:373
  1021.1 135.1 %collective-permute-start.8 = (bf16[384,4224]{1,0:T(8,128)(2,1)}, bf16[384,4224]{1,0:T(8,128)(2,1)S(1)}, u32[]{:S(2)}, u32[]{:S(2)}) collective-permute-start(bf16[384,4224]{1,0:T(8,128)(2,1)} %get-tuple-element.66), channel_id=1, source_target_pairs={{0,2},{1,3},{2,0},{3,1},{4,6},{5,7},{6,4},{7,5}} | collective-permute-start | bytes 9732104 | tf_op jit(solution)/shard_map/ppermute | solution.py:370
  1039.2 117.0 %collective-permute-start.10 = (bf16[384,4224]{1,0:T(8,128)(2,1)}, bf16[384,4224]{1,0:T(8,128)(2,1)}, u32[]{:S(2)}, u32[]{:S(2)}) collective-permute-start(bf16[384,4224]{1,0:T(8,128)(2,1)} %get-tuple-element.67), channel_id=1, source_target_pairs={{0,1},{1,0},{2,3},{3,2},{4,5},{5,4},{6,7},{7,6}} | collective-permute-start | bytes 9732104 | tf_op jit(solution)/shard_map/ppermute | solution.py:373
  1039.2 186.5 %collective-permute-start.22 = (bf16[384,4224]{1,0:T(8,128)(2,1)}, bf16[384,4224]{1,0:T(8,128)(2,1)}, u32[]{:S(2)}, u32[]{:S(2)}) collective-permute-start(bf16[384,4224]{1,0:T(8,128)(2,1)} %get-tuple-element.75), channel_id=1, source_target_pairs={{0,2},{1,3},{2,0},{3,1},{4,6},{5,7},{6,4},{7,5}} | collective-permute-start | bytes 9732104 | tf_op jit(solution)/shard_map/ppermute | solution.py:370
  1057.8 237.0 %collective-permute-start.19 = (bf16[384,4224]{1,0:T(8,128)(2,1)}, bf16[384,4224]{1,0:T(8,128)(2,1)}, u32[]{:S(2)}, u32[]{:S(2)}) collective-permute-start(bf16[384,4224]{1,0:T(8,128)(2,1)} %get-tuple-element.74), channel_id=1, source_target_pairs={{0,2},{1,3},{2,0},{3,1},{4,6},{5,7},{6,4},{7,5}} | collective-permute-start | bytes 9732104 | tf_op jit(solution)/shard_map/ppermute | solution.py:370
  1086.7 208.1 %collective-permute-start.12 = (bf16[384,4224]{1,0:T(8,128)(2,1)}, bf16[384,4224]{1,0:T(8,128)(2,1)}, u32[]{:S(2)}, u32[]{:S(2)}) collective-permute-start(bf16[384,4224]{1,0:T(8,128)(2,1)} %collective-permute-done.11.refs_1_), channel_id=1, source_target_pairs={{0,1},{1,0},{2,3},{3,2},{4,5},{5,4},{6,7},{7,6}} | collective-permute-start | bytes 9732104 | tf_op jit(solution)/shard_map/ppermute | solution.py:373
  1156.2 151.3 %copy-start.3 = (bf16[384,4224]{1,0:T(8,128)(2,1)}, bf16[384,4224]{1,0:T(8,128)(2,1)S(1)}, u32[]{:S(2)}) copy-start(bf16[384,4224]{1,0:T(8,128)(2,1)S(1)} %collective-permute-done.8.refs_1_) | copy-start | bytes 9732100
  1156.2 179.8 %collective-permute-start.9 = (bf16[384,4224]{1,0:T(8,128)(2,1)S(1)}, bf16[384,4224]{1,0:T(8,128)(2,1)}, u32[]{:S(2)}, u32[]{:S(2)}) collective-permute-start(bf16[384,4224]{1,0:T(8,128)(2,1)S(1)} %collective-permute-done.8.refs_1_), channel_id=1, source_target_pairs={{0,1},{1,0},{2,3},{3,2},{4,5},{5,4},{6,7},{7,6}} | collective-permute-start | bytes 9732104 | tf_op jit(solution)/shard_map/ppermute | solution.py:373
  1156.2 190.8 %collective-permute-start.21 = (bf16[384,4224]{1,0:T(8,128)(2,1)}, bf16[384,4224]{1,0:T(8,128)(2,1)}, u32[]{:S(2)}, u32[]{:S(2)}) collective-permute-start(bf16[384,4224]{1,0:T(8,128)(2,1)} %get-tuple-element.75), channel_id=1, source_target_pairs={{0,1},{1,0},{2,3},{3,2},{4,5},{5,4},{6,7},{7,6}} | collective-permute-start | bytes 9732104 | tf_op jit(solution)/shard_map/ppermute | solution.py:373
  1225.8 121.1 %collective-permute-start.23 = (bf16[384,4224]{1,0:T(8,128)(2,1)}, bf16[384,4224]{1,0:T(8,128)(2,1)}, u32[]{:S(2)}, u32[]{:S(2)}) collective-permute-start(bf16[384,4224]{1,0:T(8,128)(2,1)} %collective-permute-done.22.refs_1_), channel_id=1, source_target_pairs={{0,1},{1,0},{2,3},{3,2},{4,5},{5,4},{6,7},{7,6}} | collective-permute-start | bytes 9732104 | tf_op jit(solution)/shard_map/ppermute | solution.py:373
  1294.8 63.1 %collective-permute-start.18 = (bf16[384,4224]{1,0:T(8,128)(2,1)}, bf16[384,4224]{1,0:T(8,128)(2,1)}, u32[]{:S(2)}, u32[]{:S(2)}) collective-permute-start(bf16[384,4224]{1,0:T(8,128)(2,1)} %get-tuple-element.74), channel_id=1, source_target_pairs={{0,1},{1,0},{2,3},{3,2},{4,5},{5,4},{6,7},{7,6}} | collective-permute-start | bytes 9732104 | tf_op jit(solution)/shard_map/ppermute | solution.py:373
  1294.8 63.1 %collective-permute-start.20 = (bf16[384,4224]{1,0:T(8,128)(2,1)}, bf16[384,4224]{1,0:T(8,128)(2,1)}, u32[]{:S(2)}, u32[]{:S(2)}) collective-permute-start(bf16[384,4224]{1,0:T(8,128)(2,1)} %collective-permute-done.19.refs_1_), channel_id=1, source_target_pairs={{0,1},{1,0},{2,3},{3,2},{4,5},{5,4},{6,7},{7,6}} | collective-permute-start | bytes 9732104 | tf_op jit(solution)/shard_map/ppermute | solution.py:373
